TPU v7x, 32 devices: a whole 2x2x4 slice. The times are simulated.
32 devices in a mesh: section: 2 (over x), dp: 4 (over z), tensor: 4 (over y, core).
Axes of the slice: x: 2, y: 2, z: 4, core: 2. Of those that a mesh axis runs over, the one named last changes fastest.
Arguments:
- stream: bfloat16 [2, 4, 1024, 1536], P(None, 'dp', 'tensor'), may hold values from -6 to 6
- cotangent: bfloat16 [2, 4, 1024, 1536], P(None, 'dp', 'tensor'), may hold values from -6 to 6
- norm_gain: float32 [2, 1536], P('section'), may hold values from 0.25 to 1.75
- in_zx: bfloat16 [2, 1536, 2, 3072], P('section', 'dp', None, 'tensor'), may hold values from -0.15625 to 0.15625
- in_dt: bfloat16 [2, 1536, 48], P('section', 'dp', 'tensor'), may hold values from -0.15625 to 0.15625
- in_bc: bfloat16 [2, 1536, 256], P('section', 'dp'), may hold values from -0.15625 to 0.15625
- out_proj: bfloat16 [2, 3072, 1536], P('section', 'tensor', 'dp'), may hold values from -0.109375 to 0.109375
- conv_x: float32 [2, 4, 3072], P('section', None, 'tensor'), may hold values from -2 to 2
- conv_x_bias: float32 [2, 3072], P('section', 'tensor'), may hold values from -2 to 2
- conv_bc: float32 [2, 4, 256], P('section'), may hold values from -2 to 2
- conv_bc_bias: float32 [2, 256], P('section'), may hold values from -2 to 2
- dt_bias: float32 [2, 48], P('section', 'tensor'), may hold values from -6 to -2
- a_log: float32 [2, 48], P('section', 'tensor'), may hold values from 0 to 2.8
- d_skip: float32 [2, 48], P('section', 'tensor'), may hold values from 0.5 to 1.5
- gate_gain: float32 [2, 3072], P('section', 'tensor'), may hold values from 0.25 to 1.75
Outputs:
- section_out: bfloat16 [2, 2, 4, 1024, 1536], P('section', None, 'dp', 'tensor')
- input_grad: bfloat16 [2, 2, 4, 1024, 1536], P('section', None, 'dp', 'tensor')
- grad_norm_gain: float32 [2, 1536], P('section')
- grad_in_zx: float32 [2, 1536, 2, 3072], P('section', 'dp', None, 'tensor')
- grad_in_dt: float32 [2, 1536, 48], P('section', 'dp', 'tensor')
- grad_in_bc: float32 [2, 1536, 256], P('section', 'dp')
- grad_out_proj: float32 [2, 3072, 1536], P('section', 'tensor', 'dp')
- grad_conv_x: float32 [2, 4, 3072], P('section', None, 'tensor')
- grad_conv_x_bias: float32 [2, 3072], P('section', 'tensor')
- grad_conv_bc: float32 [2, 4, 256], P('section')
- grad_conv_bc_bias: float32 [2, 256], P('section')
- grad_dt_bias: float32 [2, 48], P('section', 'tensor')
- grad_a_log: float32 [2, 48], P('section', 'tensor')
- grad_d_skip: float32 [2, 48], P('section', 'tensor')
- grad_gate_gain: float32 [2, 3072], P('section', 'tensor')
All inputs are finite; a program needn't handle non-finite values.
Results may differ from a plain program's by a relative error of at most 0.014.
Values may be sent and summed in bfloat16 or wider, within the bound.
A program may use at most 320 MiB of HBM per device.

v0:
```python
import jax
import jax.numpy as jnp
from jax import lax
from jax.sharding import PartitionSpec as P

N = 128
CONV = 4
GROUP = 256


EPSILON = 1e-05
PRECISE = lax.Precision.HIGHEST


def from_behind(value, axis, steps):
    count = lax.axis_size(axis)
    leading, last = (max(0, -steps), min(count, count - steps))
    return lax.ppermute(value, axis, [(source, source + steps) for source in range(leading, last)])


def causal_conv(signal, kernel, offset):
    length = signal.shape[0]
    padded = jnp.pad(signal, ((CONV - 1, 0), (0, 0)))
    summed = jnp.broadcast_to(offset[None, :], signal.shape)
    for tap_index in range(CONV):
        summed = summed + kernel[tap_index][None, :] * padded[tap_index : tap_index + length]
    return summed


def state_scan(values, dt_values, rates, b_rows, c_rows):
    length, heads_here, head_size = values.shape
    blocks = length // GROUP
    log_decay = jnp.cumsum((dt_values * rates[None, :]).reshape(blocks, GROUP, heads_here), axis=1)
    x_blocks = values.reshape(blocks, GROUP, heads_here, head_size)
    dt_blocks = dt_values.reshape(blocks, GROUP, heads_here)
    b_blocks = b_rows.reshape(blocks, GROUP, -1)
    c_blocks = c_rows.reshape(blocks, GROUP, -1)
    inner_scores = jnp.einsum("ktn,ksn->kts", c_blocks, b_blocks, precision=PRECISE)
    causal = jnp.arange(GROUP)[:, None] >= jnp.arange(GROUP)[None, :]
    decay_gaps = log_decay[:, :, None, :] - log_decay[:, None, :, :]
    mixing = (
        jnp.exp(jnp.where(causal[None, :, :, None], decay_gaps, -1e30))
        * inner_scores[:, :, :, None]
        * dt_blocks[:, None, :, :]
    )
    within = jnp.einsum("ktsh,kshp->kthp", mixing, x_blocks, precision=PRECISE)
    final_decay = log_decay[:, -1, :]
    to_end = jnp.exp(final_decay[:, None, :] - log_decay) * dt_blocks
    block_states = jnp.einsum("ksh,kshp,ksn->khpn", to_end, x_blocks, b_blocks, precision=PRECISE)

    def advance(running, inputs_now):
        decay_now, fresh_state = inputs_now
        return (decay_now[:, None, None] * running + fresh_state, running)

    _, entering = lax.scan(
        advance,
        jnp.zeros(block_states.shape[1:], jnp.float32),
        (jnp.exp(final_decay), block_states),
    )
    carried = (
        jnp.einsum("ktn,khpn->kthp", c_blocks, entering, precision=PRECISE)
        * jnp.exp(log_decay)[:, :, :, None]
    )
    return (within + carried).reshape(length, heads_here, head_size)


def mixer(
    gate_pre,
    x_pre,
    bc_pre,
    dt_pre,
    conv_x,
    conv_x_bias,
    conv_bc,
    conv_bc_bias,
    dt_bias,
    a_log,
    d_skip,
):
    x_conv = jax.nn.silu(causal_conv(x_pre, conv_x, conv_x_bias))
    bc_conv = jax.nn.silu(causal_conv(bc_pre, conv_bc, conv_bc_bias))
    dt_values = jax.nn.softplus(dt_pre + dt_bias[None, :])
    heads_here = dt_values.shape[1]
    per_head = x_conv.reshape(x_conv.shape[0], heads_here, -1)
    scanned = state_scan(per_head, dt_values, -jnp.exp(a_log), bc_conv[:, :N], bc_conv[:, N:])
    scanned = scanned + d_skip[None, :, None] * per_head
    return scanned.reshape(x_conv.shape) * jax.nn.silu(gate_pre)


def contract_rows(left, right):
    return lax.dot_general(
        left, right, (((0,), (0,)), ((), ())), preferred_element_type=jnp.float32
    )


def contract_cols(left, right):
    return lax.dot_general(
        left, right, (((1,), (1,)), ((), ())), preferred_element_type=jnp.float32
    )


def add_tuples(left_tuple, right_tuple):
    if left_tuple is None:
        return right_tuple
    return tuple(
        (left_value + right_value for left_value, right_value in zip(left_tuple, right_tuple))
    )


def local(
    stream,
    cotangent,
    norm_gain,
    in_zx,
    in_dt,
    in_bc,
    out_proj,
    conv_x,
    conv_x_bias,
    conv_bc,
    conv_bc_bias,
    dt_bias,
    a_log,
    d_skip,
    gate_gain,
):
    is_first = lax.axis_index("section") == 0
    micro = stream.shape[0]
    local_rows = stream.shape[2]
    model_width = stream.shape[3]
    tensor_count = lax.axis_size("tensor")
    row_start = lax.axis_index("tensor") * local_rows
    gain_vec = norm_gain[0]
    gate_vec = gate_gain[0]
    small_params = (
        conv_x[0],
        conv_x_bias[0],
        conv_bc[0],
        conv_bc_bias[0],
        dt_bias[0],
        a_log[0],
        d_skip[0],
    )
    full_zx, full_dt, full_bc, full_out = (
        lax.all_gather(in_zx[0], "dp", axis=0, tiled=True),
        lax.all_gather(in_dt[0], "dp", axis=0, tiled=True),
        lax.all_gather(in_bc[0], "dp", axis=0, tiled=True),
        lax.all_gather(out_proj[0], "dp", axis=1, tiled=True),
    )
    inner_width = full_zx.shape[2]
    heads_here = full_dt.shape[1]
    head_cols = 2 * inner_width + heads_here
    total_inner = inner_width * tensor_count
    head_proj = jnp.concatenate([full_zx.reshape(model_width, 2 * inner_width), full_dt], axis=1)
    all_proj = jnp.concatenate([head_proj, full_bc], axis=1)

    def front(layer_in, want_grad):
        inv_rms = lax.rsqrt(jnp.mean(layer_in * layer_in, axis=1, keepdims=True) + EPSILON)
        normed = (layer_in * inv_rms * gain_vec[None, :]).astype(jnp.bfloat16)
        normed_all = lax.all_gather(normed, "tensor", axis=0, tiled=True)
        projected = jnp.dot(normed_all, all_proj, preferred_element_type=jnp.float32)
        gate_pre = projected[:, :inner_width]
        x_pre = projected[:, inner_width : 2 * inner_width]
        dt_pre = projected[:, 2 * inner_width : head_cols]
        bc_pre = projected[:, head_cols:]
        if want_grad:
            gated, mixer_back = jax.vjp(mixer, gate_pre, x_pre, bc_pre, dt_pre, *small_params)
        else:
            gated = mixer(gate_pre, x_pre, bc_pre, dt_pre, *small_params)
            mixer_back = None
        squares = lax.psum(jnp.sum(gated * gated, axis=1), "tensor")
        gate_scale = lax.rsqrt(squares / total_inner + EPSILON)
        gate_normed = (gated * gate_scale[:, None] * gate_vec[None, :]).astype(jnp.bfloat16)
        return (inv_rms, normed_all, gated, mixer_back, gate_scale, gate_normed)

    received = jnp.zeros((local_rows, model_width), jnp.bfloat16)
    returned = jnp.zeros((local_rows, model_width), jnp.bfloat16)
    forward_outs = []
    backward_outs = []
    large_sum = None
    minor_sum = None
    for tick_index in range(micro + 2):
        if tick_index <= micro:
            own_input = stream[min(tick_index, micro - 1), 0].astype(jnp.float32)
            layer_in = jnp.where(is_first, own_input, received.astype(jnp.float32))
            forward_gate_normed = front(layer_in, False)[5]
            layer_out = (
                layer_in
                + lax.psum_scatter(
                    jnp.dot(forward_gate_normed, full_out, preferred_element_type=jnp.float32),
                    "tensor",
                    scatter_dimension=0,
                    tiled=True,
                )
            ).astype(jnp.bfloat16)
            forward_outs.append(layer_out)
            passed = from_behind(layer_out, "section", 1)
        else:
            layer_in = jnp.zeros((local_rows, model_width), jnp.float32)
        if tick_index >= 1:
            early = min(max(tick_index - 2, 0), micro - 1)
            late = min(tick_index - 1, micro - 1)
            back_in = jnp.where(is_first, stream[early, 0].astype(jnp.float32), layer_in)
            seed_grad = jnp.where(
                is_first, returned.astype(jnp.float32), cotangent[late, 0].astype(jnp.float32)
            )
            (
                backward_inv_rms,
                backward_normed_all,
                backward_gated,
                backward_mixer_back,
                backward_gate_scale,
                backward_gate_normed,
            ) = front(back_in, True)
            incoming = lax.all_gather(seed_grad.astype(jnp.bfloat16), "tensor", axis=0, tiled=True)
            hidden_grad = contract_cols(incoming, full_out)
            hidden_grad, out_weight_grad = (
                hidden_grad,
                contract_rows(backward_gate_normed, incoming),
            )
            gained = hidden_grad * gate_vec[None, :]
            gate_dots = lax.psum(jnp.sum(gained * backward_gated, axis=1), "tensor")
            gated_grad = (
                backward_gate_scale[:, None] * gained
                - backward_gated
                * (
                    backward_gate_scale
                    * backward_gate_scale
                    * backward_gate_scale
                    * gate_dots
                    / total_inner
                )[:, None]
            )
            gate_gain_grad = jnp.sum(
                hidden_grad * backward_gated * backward_gate_scale[:, None], axis=0
            )
            mixed_grads = backward_mixer_back(gated_grad)
            bc_grad, conv_bc_grad, conv_bc_bias_grad = lax.psum(
                (mixed_grads[2], mixed_grads[6], mixed_grads[7]), "tensor"
            )
            head_grad = jnp.concatenate(
                [mixed_grads[0], mixed_grads[1], mixed_grads[3]], axis=1
            ).astype(jnp.bfloat16)
            bc_low = bc_grad.astype(jnp.bfloat16)
            normed_grad = lax.psum_scatter(
                contract_cols(head_grad, head_proj), "tensor", scatter_dimension=0, tiled=True
            )
            normed_grad = normed_grad + contract_cols(
                lax.dynamic_slice_in_dim(bc_low, row_start, local_rows, 0), full_bc
            )
            head_weight_grad = contract_rows(backward_normed_all, head_grad)
            bc_weight_grad = contract_rows(backward_normed_all, bc_low)
            scaled_grad = normed_grad * gain_vec[None, :]
            norm_dots = jnp.sum(scaled_grad * back_in, axis=1, keepdims=True)
            in_grad = (
                seed_grad
                + backward_inv_rms * scaled_grad
                - back_in
                * (backward_inv_rms * backward_inv_rms * backward_inv_rms)
                * norm_dots
                / model_width
            )
            norm_gain_grad = jnp.sum(normed_grad * back_in * backward_inv_rms, axis=0)
            zx_grad = head_weight_grad[:, : 2 * inner_width].reshape(model_width, 2, inner_width)
            dt_weight_grad = head_weight_grad[:, 2 * inner_width :]
            large_grads = (zx_grad, dt_weight_grad, bc_weight_grad, out_weight_grad)
            minor_grads = (
                mixed_grads[4],
                mixed_grads[5],
                conv_bc_grad,
                conv_bc_bias_grad,
                mixed_grads[8],
                mixed_grads[9],
                mixed_grads[10],
                gate_gain_grad,
                norm_gain_grad,
            )
            in_grad, large_grads, minor_grads = (in_grad, large_grads, minor_grads)
            validity = jnp.where(
                is_first, 1.0 if tick_index >= 2 else 0.0, 1.0 if tick_index <= micro else 0.0
            )
            large_grads = tuple((member * validity for member in large_grads))
            minor_grads = tuple((member * validity for member in minor_grads))
            minor_sum = add_tuples(minor_sum, minor_grads)
            zx_part, dt_part, bc_part, out_part = large_grads
            shard_now = (
                lax.psum_scatter(
                    zx_part.astype(jnp.bfloat16), "dp", scatter_dimension=0, tiled=True
                ).astype(jnp.float32),
                lax.psum_scatter(
                    dt_part.astype(jnp.bfloat16), "dp", scatter_dimension=0, tiled=True
                ).astype(jnp.float32),
                lax.psum_scatter(
                    bc_part.astype(jnp.bfloat16), "dp", scatter_dimension=0, tiled=True
                ).astype(jnp.float32),
                lax.psum_scatter(
                    out_part.astype(jnp.bfloat16), "dp", scatter_dimension=1, tiled=True
                ).astype(jnp.float32),
            )
            large_sum = add_tuples(large_sum, shard_now)
            in_low = in_grad.astype(jnp.bfloat16)
            backward_outs.append(in_low)
            returned = from_behind(in_low, "section", -1)
        if tick_index <= micro:
            received = passed
    (
        conv_x_sum,
        conv_x_bias_sum,
        conv_bc_sum,
        conv_bc_bias_sum,
        dt_bias_sum,
        a_log_sum,
        d_skip_sum,
        gate_gain_sum,
        norm_gain_sum,
    ) = minor_sum
    head_totals = lax.psum(
        (
            conv_x_sum,
            conv_x_bias_sum,
            conv_bc_sum,
            conv_bc_bias_sum,
            dt_bias_sum,
            a_log_sum,
            d_skip_sum,
            gate_gain_sum,
        ),
        "dp",
    )
    norm_total = lax.psum(norm_gain_sum, ("dp", "tensor"))
    section_rows = [
        jnp.where(is_first, forward_outs[micro_index], forward_outs[micro_index + 1])
        for micro_index in range(micro)
    ]
    grad_rows = [
        jnp.where(is_first, backward_outs[micro_index + 1], backward_outs[micro_index])
        for micro_index in range(micro)
    ]
    section_out = jnp.stack(section_rows)[None, :, None]
    input_grad = jnp.stack(grad_rows)[None, :, None]
    return (
        section_out,
        input_grad,
        norm_total[None],
        large_sum[0][None],
        large_sum[1][None],
        large_sum[2][None],
        large_sum[3][None],
        head_totals[0][None],
        head_totals[1][None],
        head_totals[2][None],
        head_totals[3][None],
        head_totals[4][None],
        head_totals[5][None],
        head_totals[6][None],
        head_totals[7][None],
    )


def solution(mesh):
    in_specs = (
        P(None, "dp", "tensor", None),
        P(None, "dp", "tensor", None),
        P("section", None),
        P("section", "dp", None, "tensor"),
        P("section", "dp", "tensor"),
        P("section", "dp", None),
        P("section", "tensor", "dp"),
        P("section", None, "tensor"),
        P("section", "tensor"),
        P("section", None, None),
        P("section", None),
        P("section", "tensor"),
        P("section", "tensor"),
        P("section", "tensor"),
        P("section", "tensor"),
    )
    out_specs = (
        P("section", None, "dp", "tensor", None),
        P("section", None, "dp", "tensor", None),
        P("section", None),
        P("section", "dp", None, "tensor"),
        P("section", "dp", "tensor"),
        P("section", "dp", None),
        P("section", "tensor", "dp"),
        P("section", None, "tensor"),
        P("section", "tensor"),
        P("section", None, None),
        P("section", None),
        P("section", "tensor"),
        P("section", "tensor"),
        P("section", "tensor"),
        P("section", "tensor"),
    )
    return jax.shard_map(local, mesh=mesh, in_specs=in_specs, out_specs=out_specs, check_vma=False)
```

profile of v0, /device:TPU:9, one launch (start us, length us, event | category | flops | bytes accessed | tf_op | source)
XLA Modules:
  0.0 2478.2 jit_solution(6269585169467570114)
XLA Ops:
  28.6 28.5 %all-gather.2 = bf16[1,1536,256]{2,1,0:T(8,128)(2,1)S(1)} all-gather(bf16[1,384,256]{2,1,0:T(8,128)(2,1)S(1)} %copy-done.177), channel_id=4, replica_groups=mesh['section'=2,'dp'=4,'tensor'=4] {'dp'}, dimensions={1}, use_global_device_ids=true | all-gather | bytes 983040 | tf_op jit(solution)/shard_map/all_gather | solution.py:147
  57.1 53.7 %all-gather.34.cloned.1.call-done = bf16[1,1536,2,768]{3,2,0,1:T(2,128)(2,1)} async-done(((bf16[1,384,2,768]{3,2,0,1:T(2,128)(2,1)}), bf16[1,1536,2,768]{3,2,0,1:T(2,128)(2,1)}) %all-gather.34.cloned.1.call-update) | async-done | bytes 4718608 | tf_op jit(solution)/shard_map/all_gather | solution.py:145
  125.8 16.9 all-gather.16.cloned.1.call-done
  266.2 60.1 %reduce-scatter.28.cloned.1.call-done = f32[256,1536]{1,0:T(8,128)} async-done(((f32[1024,1536]{1,0:T(8,128)}), f32[256,1536]{1,0:T(8,128)}) %reduce-scatter.28.cloned.1.call-update) | async-done | bytes 1572880 | tf_op jit(solution)/shard_map/reduce_scatter | solution.py:189
  353.7 27.5 %all-gather.18.cloned.1.call-done = bf16[1024,1536]{1,0:T(8,128)(2,1)} async-done(((bf16[256,1536]{1,0:T(8,128)(2,1)}), bf16[1024,1536]{1,0:T(8,128)(2,1)}) %all-gather.18.cloned.1.call-update) | async-done | bytes 3145744 | tf_op jit(solution)/shard_map/all_gather | solution.py:160
  453.0 16.9 fusion.166
  483.3 22.0 while.144
  530.9 16.4 fusion.39
  634.0 25.3 %while.145 = (s32[]{:T(128)}, f32[12,64,128]{2,1,0:T(8,128)}, f32[4,12]{1,0:T(4,128)}, f32[4,12,64,128]{3,2,1,0:T(8,128)}, f32[4,12,64,128]{3,2,1,0:T(8,128)}, /...) while((s32[]{:T(128)}, f32[12,64,128]{2,1,0:T(8,128)}, ...), condition=%wide.region_35.37_spmd.clone, body=%wide.region_33.36_spmd.clone.sunk | while | flops 589816 | bytes 3146164 | solution.py:55
  665.4 23.2 fusion.54
  954.2 28.0 %all-reduce.84 = (bf16[1024,256]{0,1:T(8,128)(2,1)}, f32[1024]{0:T(1024)S(1)}) all-reduce(f32[1024,256]{0,1:T(8,128)} %pad_add_fusion.15, f32[1024]{0:T(1024)S(1)} %get-tuple-element.1187), channel_id=1, replica_groups=mesh['section'=2,'dp'=4,'tensor'=4] {'tensor'}, use_global_device_ids=true, to_apply=%region_45.47 | all-reduce | flops 263168 | bytes 1581056 | tf_op jit(solution)/shard_map/psum | solution.py:238
  988.6 19.5 collective-permute-done.2
  1076.2 21.4 fusion.56
  1099.5 25.4 %while.147 = (s32[]{:T(128)}, f32[12,64,128]{2,1,0:T(8,128)}, f32[4,12]{1,0:T(4,128)}, f32[4,12,64,128]{3,2,1,0:T(8,128)}, f32[4,12,64,128]{3,2,1,0:T(8,128)}, /...) while((s32[]{:T(128)}, f32[12,64,128]{2,1,0:T(8,128)}, ...), condition=%wide.region_58.60_spmd.clone, body=%wide.region_56.59_spmd.clone.sunk | while | flops 589816 | bytes 3146164 | solution.py:55
  1275.2 44.3 %all-reduce.85 = (bf16[1024,256]{0,1:T(8,128)(2,1)}, f32[1024]{0:T(1024)S(1)}) all-reduce(f32[1024,256]{0,1:T(8,128)} %pad_add_fusion.12, f32[1024]{0:T(1024)S(1)} %get-tuple-element.1308), channel_id=1, replica_groups=mesh['section'=2,'dp'=4,'tensor'=4] {'tensor'}, use_global_device_ids=true, to_apply=%region_68.70 | all-reduce | flops 263168 | bytes 1581056 | tf_op jit(solution)/shard_map/psum | solution.py:238
  1327.6 18.8 collective-permute-done.3
  1348.5 29.2 %all-gather.32.cloned.1.call-done = bf16[1024,1536]{1,0:T(8,128)(2,1)} async-done(((bf16[256,1536]{1,0:T(8,128)(2,1)}), bf16[1024,1536]{1,0:T(8,128)(2,1)}) %all-gather.32.cloned.1.call-update) | async-done | bytes 3145744 | tf_op jit(solution)/shard_map/all_gather | solution.py:215
  1413.9 21.3 fusion.58
  1437.1 25.7 %while.149 = (s32[]{:T(128)}, f32[12,64,128]{2,1,0:T(8,128)}, f32[4,12]{1,0:T(4,128)}, f32[4,12,64,128]{3,2,1,0:T(8,128)}, f32[4,12,64,128]{3,2,1,0:T(8,128)}, /...) while((s32[]{:T(128)}, f32[12,64,128]{2,1,0:T(8,128)}, ...), condition=%wide.region_81.83_spmd.clone, body=%wide.region_79.82_spmd.clone.sunk | while | flops 589816 | bytes 3146164 | solution.py:55
  1555.3 43.2 %all-reduce.86 = bf16[1024,256]{0,1:T(8,128)(2,1)} all-reduce(f32[1024,256]{0,1:T(8,128)} %pad_add_fusion.9), channel_id=1, replica_groups=mesh['section'=2,'dp'=4,'tensor'=4] {'tensor'}, use_global_device_ids=true, to_apply=%region_91.93 | all-reduce | flops 262144 | bytes 1572864 | tf_op jit(solution)/shard_map/psum | solution.py:238
  1875.4 49.0 %reduce-scatter.56.cloned.1.call-done = bf16[384,768]{1,0:T(8,128)(2,1)} async-done(((bf16[1536,768]{1,0:T(8,128)(2,1)}), bf16[384,768]{1,0:T(8,128)(2,1)}) %reduce-scatter.56.cloned.1.call-update) | async-done | bytes 589840
  1927.1 34.4 %psum.201 = f32[1,1536]{1,0:T(1,128)} all-reduce(f32[1,1536]{1,0:T(1,128)S(1)} %broadcast_in_dim.361), channel_id=1, replica_groups=mesh['section'=2,'dp'=4,'tensor'=4] {'dp','tensor'}, use_global_device_ids=true, to_apply=%region_96.98 | all-reduce | flops 1536 | bytes 12288 | tf_op jit(solution)/shard_map/psum | solution.py:330
  1961.4 441.1 %all-reduce.83.cloned.1.call-done = (bf16[1536,2,768]{2,1,0:T(2,128)(2,1)}, bf16[1536,2,768]{2,1,0:T(2,128)(2,1)}, bf16[1536,2,768]{2,1,0:T(2,128)(2,1)}) async-done(((bf16[1536,2,768]{2,1,0:T(2,128)(2,1)}, bf16[1536,2,768]{2,1,0:T(2,128)(2,1)}, bf16[1536,2,768]{2,1,0:T(2,128)(2,1)}), (bf16[1536,2,768]{2,1,0:T(2,128)(2,1)}, bf16[1536,2,768]{2,1,0:T(2,128)(2,1)}, ...) | async-done | bytes 14155792
  2421.1 43.7 %reduce-scatter.32.cloned.1.call-done = f32[256,1536]{1,0:T(8,128)} async-done(((f32[1024,1536]{1,0:T(8,128)}), f32[256,1536]{1,0:T(8,128)}) %reduce-scatter.32.cloned.1.call-update) | async-done | bytes 1572880 | tf_op jit(solution)/shard_map/reduce_scatter | solution.py:189
  (1389 shorter events, 1478.0 us)
Async XLA Ops:
  8.0 134.8 %all-gather.16.cloned.1.call-start = ((), (), s32[]{:S(2)}) async-start(), calls=%async_computation.15 | async-start | bytes 3932160 | tf_op jit(solution)/shard_map/all_gather | solution.py:160
  12.5 245.5 %all-gather.36.cloned.1.call-start = ((), (), s32[]{:S(2)}) async-start(), calls=%async_computation.34 | async-start | bytes 2949120 | tf_op jit(solution)/shard_map/all_gather | solution.py:148
  13.2 313.0 %reduce-scatter.28.cloned.1.call-start = ((), (), s32[]{:S(2)}) async-start(), calls=%async_computation.16 | async-start | bytes 7864320 | tf_op jit(solution)/shard_map/reduce_scatter | solution.py:189
  351.8 236.3 %all-gather.24.cloned.1.call-start = ((), (), s32[]{:S(2)}) async-start(), calls=%async_computation.22 | async-start | bytes 3932160 | tf_op jit(solution)/shard_map/all_gather | solution.py:215
  353.4 335.1 %reduce-scatter.30.cloned.1.call-start = ((), (), s32[]{:S(2)}) async-start(), calls=%async_computation.18 | async-start | bytes 7864320 | tf_op jit(solution)/shard_map/reduce_scatter | solution.py:189
  611.2 131.7 %all-gather.30.cloned.1.call-start = ((), (), s32[]{:S(2)}) async-start(), calls=%async_computation.27 | async-start | bytes 3932160 | tf_op jit(solution)/shard_map/all_gather | solution.py:160
  611.9 154.7 %all-gather.26.cloned.1.call-start = ((), (), s32[]{:S(2)}) async-start(), calls=%async_computation.24 | async-start | bytes 3932160 | tf_op jit(solution)/shard_map/all_gather | solution.py:160
  714.4 267.8 %reduce-scatter.34.cloned.1.call-start = ((), (), s32[]{:S(2)}) async-start(), calls=%async_computation.23 | async-start | bytes 7864320 | tf_op jit(solution)/shard_map/reduce_scatter | solution.py:245
  808.7 230.6 %all-gather.28.cloned.1.call-start = ((), (), s32[]{:S(2)}) async-start(), calls=%async_computation.25 | async-start | bytes 3932160 | tf_op jit(solution)/shard_map/all_gather | solution.py:215
  1010.0 310.1 %reduce-scatter.36.cloned.1.call-start = ((), (), s32[]{:S(2)}) async-start(), calls=%async_computation.26 | async-start | bytes 7864320 | tf_op jit(solution)/shard_map/reduce_scatter | solution.py:245
  1242.7 135.0 %all-gather.32.cloned.1.call-start = ((), (), s32[]{:S(2)}) async-start(), calls=%async_computation.28 | async-start | bytes 3932160 | tf_op jit(solution)/shard_map/all_gather | solution.py:215
  1348.4 254.2 %reduce-scatter.38.cloned.1.call-start = ((), (), s32[]{:S(2)}) async-start(), calls=%async_computation.29 | async-start | bytes 7864320 | tf_op jit(solution)/shard_map/reduce_scatter | solution.py:245
  1525.7 225.0 %all-gather.20.cloned.1.call-start = ((), (), s32[]{:S(2)}) async-start(), calls=%async_computation.19 | async-start | bytes 3932160 | tf_op jit(solution)/shard_map/all_gather | solution.py:160
  1607.9 253.4 %reduce-scatter.52.cloned.1.call-start = ((), (), s32[]{:S(2)}) async-start(), calls=%async_computation.38 | async-start | bytes 2949120
  1619.5 243.3 %reduce-scatter.46.cloned.1.call-start = ((), (), s32[]{:S(2)}) async-start(), calls=%async_computation.35 | async-start | bytes 491520
  1632.4 231.6 %reduce-scatter.48.cloned.1.call-start = ((), (), s32[]{:S(2)}) async-start(), calls=%async_computation.36 | async-start | bytes 491520
  1643.3 221.7 %reduce-scatter.54.cloned.1.call-start = ((), (), s32[]{:S(2)}) async-start(), calls=%async_computation.39 | async-start | bytes 2949120
  1655.1 211.9 %reduce-scatter.50.cloned.1.call-start = ((), (), s32[]{:S(2)}) async-start(), calls=%async_computation.37 | async-start | bytes 491520
  1668.0 200.6 %reduce-scatter.40.cloned.1.call-start = ((), (), s32[]{:S(2)}) async-start(), calls=%async_computation.30 | async-start | bytes 983040 | tf_op jit(solution)/shard_map/reduce_scatter | solution.py:293
  1672.1 196.6 %reduce-scatter.42.cloned.1.call-start = ((), (), s32[]{:S(2)}) async-start(), calls=%async_computation.31 | async-start | bytes 983040 | tf_op jit(solution)/shard_map/reduce_scatter | solution.py:293
  1676.0 197.4 %reduce-scatter.44.cloned.1.call-start = ((), (), s32[]{:S(2)}) async-start(), calls=%async_computation.32 | async-start | bytes 983040 | tf_op jit(solution)/shard_map/reduce_scatter | solution.py:293
  1679.9 244.5 %reduce-scatter.56.cloned.1.call-start = ((), (), s32[]{:S(2)}) async-start(), calls=%async_computation.40 | async-start | bytes 2949120
  1691.2 711.3 %all-reduce.83.cloned.1.call-start = ((), (), s32[]{:S(2)}) async-start(), calls=%async_computation.41 | async-start | bytes 28311552
  1748.3 716.5 %reduce-scatter.32.cloned.1.call-start = ((), (), s32[]{:S(2)}) async-start(), calls=%async_computation.20 | async-start | bytes 7864320 | tf_op jit(solution)/shard_map/reduce_scatter | solution.py:189
  (321 other events, 7112.1 us)
Sparse Core Ops, SparseCore 0:
  9.6 101.0 all-gather.33
  112.8 29.8 all-gather.15
  144.4 48.1 all-gather.35
  266.3 59.9 reduce-scatter.27
  350.2 30.9 all-gather.17
  383.2 28.4 all-gather.21
  413.3 28.5 all-gather.23
  611.3 59.8 reduce-scatter.29
  672.8 29.0 all-gather.29
  714.5 31.6 all-gather.25
  808.9 61.7 reduce-scatter.33
  1010.2 29.1 all-gather.27
  1242.8 77.2 reduce-scatter.35
  1348.5 29.0 all-gather.31
  1525.8 76.8 reduce-scatter.37
  1608.1 29.0 all-gather.19
  1639.3 46.5 reduce-scatter.51
  1727.8 49.8 reduce-scatter.53
  1799.2 23.8 reduce-scatter.39
  1825.3 22.6 reduce-scatter.41
  1850.7 22.6 reduce-scatter.43
  1875.8 48.5 reduce-scatter.55
  1927.1 475.4 all-reduce.82
  2404.9 59.7 reduce-scatter.31
  (3 shorter events, 51.4 us)
where the time goes:
time: 2490 us; the launch traced here: 2480 us
  waiting for transfers between devices  812 us (33%)
  matrix products  559 us (22%)
  local copies, waits for them, and re-layouts  425 us (17%)
  other arithmetic  407 us (16%)
  blocking collectives  242 us (10%)
    unnamed x34, waiting for transfers between devices  493 us
    dot_general x12, matrix products, state_scan(): within = jnp.einsum('ktsh,kshp->kthp', mixing, x_blocks, precision=PRECISE)  196 us
    psum x3, blocking collectives, local(): lax.psum((mixed_grads[2], mixed_grads[6], mixed_grads[7]), 'tensor')  116 us
    reduce_scatter x3, waiting for transfers between devices, local(): lax.psum_scatter(jnp.dot(forward_gate_normed, full_out, preferred_element...  104 us
    unnamed x670, local copies, waits for them, and re-layouts  89.9 us
    dot_general x12, matrix products, state_scan(): jnp.einsum('ksh,kshp,ksn->khpn', to_end, x_blocks, b_blocks, precision=PR...  74.7 us
    another operation x33, other arithmetic  68.7 us
    dot_general x9, matrix products, contract_cols(): lax.dot_general(left, right, (((1,), (1,)), ((), ())), preferred_element_...  63.7 us
  transfers between devices with their start and end apart: 31, of which 17 were waited for; matrix products, arithmetic and copies ran while one was open for 37% of the time, Pallas kernels for 0%

commit v1 on v0

v1 whole, which is shorter than its diff:
```python
import functools

import jax
import jax.numpy as jnp
from jax import lax
from jax.sharding import PartitionSpec as P
from jax.experimental import pallas as pl
from jax.experimental.pallas import tpu as pltpu
BF=jnp.bfloat16; F32=jnp.float32
NS=128; Q=128; CONV=4

def dot(a,b): return jnp.dot(a,b,preferred_element_type=F32)
def dot_nt(a,b): return lax.dot_general(a,b,(((1,),(1,)),((),())),preferred_element_type=F32)
def dot_tn(a,b): return lax.dot_general(a,b,(((0,),(0,)),((),())),preferred_element_type=F32)
def dot_hi(a,b): return lax.dot_general(a,b,(((1,),(0,)),((),())),preferred_element_type=F32,precision=lax.Precision.HIGHEST)

def expand(v, spread_ref):
    hi = v.astype(BF)
    lo = (v - hi.astype(F32)).astype(BF)
    return dot(jnp.concatenate([hi, lo], axis=1), spread_ref[...])

def front_chunk(width, pre_ref, par_ref, ext, first):
    taps = [par_ref[k:k+1, :] for k in range(CONV)]
    conv = par_ref[4:5, :] + taps[0]*ext[5:5+Q, :]
    for k in range(1, CONV):
        conv = conv + taps[k]*ext[5+k:5+k+Q, :]
    return conv

def head_rows(pre_ref, par_ref, width):
    raw = pre_ref[:, 2*width+2*NS:] + par_ref[7:8, :NS]
    dt = jnp.maximum(raw, 0.0) + jnp.log1p(jnp.exp(-jnp.abs(raw)))
    rate = -jnp.exp(par_ref[8:9, :NS])
    row = lax.broadcasted_iota(jnp.int32, (Q, Q), 0)
    col = lax.broadcasted_iota(jnp.int32, (Q, Q), 1)
    lower = (row >= col)
    cum = dot_hi(lower.astype(F32), dt*rate)
    return raw, dt, rate, lower, cum

def fwd_kernel(width, pre_ref, par_ref, spread_ref, yn_ref, sq_ref, st_ref, ext, state, ex_dt, ex_e, ex_w):
    step = pl.program_id(0)
    pairs = width//128
    @pl.when(step == 0)
    def _():
        ext[0:8, :] = jnp.zeros((8, ext.shape[1]), F32)
        state[...] = jnp.zeros_like(state)
    ext[8:, :] = pre_ref[:, width:2*width+2*NS]
    conv = front_chunk(width, pre_ref, par_ref, ext, None)
    act = conv*jax.nn.sigmoid(conv)
    ext[0:8, :] = ext[Q:Q+8, :]
    bm = act[:, width:width+NS].astype(BF)
    cm = act[:, width+NS:].astype(BF)
    raw, dt, rate, lower, cum = head_rows(pre_ref, par_ref, width)
    cum_t = cum.T
    ex_dt[...] = expand(dt, spread_ref)
    ex_e[...] = expand(jnp.exp(cum), spread_ref)
    ex_w[...] = expand(jnp.exp(cum[Q-1:Q, :]-cum), spread_ref)
    scores = dot_nt(cm, bm)
    st_ref[0] = state[...].astype(st_ref.dtype)
    bm_t = bm.T
    lane = lax.broadcasted_iota(jnp.int32, (Q, 128), 1)
    squares = jnp.zeros((Q, 128), F32)
    for p in range(pairs):
        sl = slice(128*p, 128*p+128)
        x = act[:, sl]
        xd = x*ex_dt[:, sl]
        st = state[:, sl]
        mixes = []
        for h in (2*p, 2*p+1):
            gap = cum[:, h:h+1]-cum_t[h:h+1, :]
            mixes.append((jnp.exp(jnp.where(lower, gap, -1e30))*scores).astype(BF))
        xdb = xd.astype(BF)
        zero = jnp.zeros_like(xdb)
        both = jnp.concatenate([jnp.where(lane < 64, xdb, zero), jnp.where(lane < 64, zero, xdb)], axis=0)
        y = dot(jnp.concatenate(mixes, axis=1), both)
        y = y + ex_e[:, sl]*dot(cm, st.astype(BF)) + par_ref[6:7, sl]*x
        z = pre_ref[:, sl]
        yg = y*(z*jax.nn.sigmoid(z))
        squares = squares + yg*yg
        yn_ref[:, sl] = (yg*par_ref[5:6, sl]).astype(BF)
        state[:, sl] = ex_e[Q-1:Q, sl]*st + dot(bm_t, (ex_w[:, sl]*xd).astype(BF))
    sq_ref[...] = jnp.sum(squares, axis=1, keepdims=True)

def mixer_fwd(pre, par, spread, width):
    T = pre.shape[0]; n = T//Q
    pw = pre.shape[1]
    return pl.pallas_call(
        functools.partial(fwd_kernel, width),
        grid=(n,),
        in_specs=[pl.BlockSpec((Q, pw), lambda i: (i, 0)),
                  pl.BlockSpec(par.shape, lambda i: (0, 0)),
                  pl.BlockSpec(spread.shape, lambda i: (0, 0))],
        out_specs=[pl.BlockSpec((Q, width), lambda i: (i, 0)),
                   pl.BlockSpec((Q, 1), lambda i: (i, 0)),
                   pl.BlockSpec((1, NS, width), lambda i: (i, 0, 0))],
        out_shape=[jax.ShapeDtypeStruct((T, width), BF), jax.ShapeDtypeStruct((T, 1), F32),
                   jax.ShapeDtypeStruct((n, NS, width), F32)],
        scratch_shapes=[pltpu.VMEM((Q+8, width+2*NS), F32), pltpu.VMEM((NS, width), F32)]
            + [pltpu.VMEM((Q, width), F32)]*3,
        compiler_params=pltpu.CompilerParams(dimension_semantics=("arbitrary",), vmem_limit_bytes=48<<20),
        name="mixer_fwd",
    )(pre, par, spread)

def fold8(v):
    return jnp.sum(v.reshape(v.shape[0]//8, 8, v.shape[1]), axis=0)

def bwd_kernel(width, n_heads, pre_ref, halo_ref, par_ref, spread_ref, gather_ref, st_ref, dh_ref, kap_ref,
               gp_ref, acc_out, ext, dext, dstate, ex_dt, ex_e, ex_w, acc, dact, sums):
    step = pl.program_id(0)
    steps = pl.num_programs(0)
    pairs = width//128
    @pl.when(step == 0)
    def _():
        dext[Q:, :] = jnp.zeros((8, dext.shape[1]), F32)
        dstate[...] = jnp.zeros_like(dstate)
        acc[...] = jnp.zeros_like(acc)
    ext[8:, :] = pre_ref[:, width:2*width+2*NS]
    halo = halo_ref[:, width:2*width+2*NS]
    ext[0:8, :] = jnp.where(step == steps-1, 0.0, halo)
    conv = front_chunk(width, pre_ref, par_ref, ext, None)
    sg = jax.nn.sigmoid(conv)
    act = conv*sg
    bm = act[:, width:width+NS].astype(BF)
    cm = act[:, width+NS:].astype(BF)
    raw, dt, rate, lower, cum = head_rows(pre_ref, par_ref, width)
    cum_t = cum.T
    e_head = jnp.exp(cum)
    ex_dt[...] = expand(dt, spread_ref)
    ex_e[...] = expand(e_head, spread_ref)
    ex_w[...] = expand(jnp.exp(cum[Q-1:Q, :]-cum), spread_ref)
    scores = dot_nt(cm, bm)
    cm_t = cm.T
    lane = lax.broadcasted_iota(jnp.int32, (Q, 128), 1)
    kap = kap_ref[...]
    dscores = jnp.zeros((Q, Q), F32)
    row_sums = jnp.zeros((Q, 128), F32)
    col_rows = []
    dC = jnp.zeros((Q, NS), F32)
    dB = jnp.zeros((Q, NS), F32)
    w_sum = jnp.zeros((Q, 128), F32)
    e_sum = jnp.zeros((Q, 128), F32)
    t_sum = jnp.zeros((Q, 128), F32)
    f_sum = jnp.zeros((8, 128), F32)
    orow = lax.broadcasted_iota(jnp.int32, (2*Q, 128), 0)
    ocol = lax.broadcasted_iota(jnp.int32, (2*Q, 128), 1)
    for p in range(pairs):
        sl = slice(128*p, 128*p+128)
        x = act[:, sl]
        xdt = ex_dt[:, sl]
        xd = x*xdt
        xdb = xd.astype(BF)
        st = st_ref[0, :, sl]
        stb = st.astype(BF)
        zero = jnp.zeros_like(xdb)
        decays, mixes = [], []
        for h in (2*p, 2*p+1):
            gap = cum[:, h:h+1]-cum_t[h:h+1, :]
            decay = jnp.exp(jnp.where(lower, gap, -1e30))
            decays.append(decay)
            mixes.append(decay*scores)
        mixb = [m.astype(BF) for m in mixes]
        both = jnp.concatenate([jnp.where(lane < 64, xdb, zero), jnp.where(lane < 64, zero, xdb)], axis=0)
        y = dot(jnp.concatenate(mixb, axis=1), both)
        e = ex_e[:, sl]
        carried = e*dot(cm, stb)
        y = y + carried + par_ref[6:7, sl]*x
        z = pre_ref[:, sl]
        sz = jax.nn.sigmoid(z)
        silz = z*sz
        yg = y*silz
        dh = dh_ref[:, sl]
        dyg = par_ref[5:6, sl]*dh - yg*kap
        acc[40:48, sl] += fold8(dh*yg)
        dy = dyg*silz
        gp_ref[:, sl] = (dyg*y*(sz+silz*(1.0-sz))).astype(BF)
        acc[48:56, sl] += fold8(dy*x)
        dyb = dy.astype(BF)
        dstack = jnp.concatenate([jnp.where(lane < 64, dyb, zero), jnp.where(lane < 64, zero, dyb)], axis=0)
        dmix = dot_nt(dstack, xdb)
        rbs = []
        for j in range(2):
            dm = dmix[Q*j:Q*j+Q]
            dscores = dscores + decays[j]*dm
            rb = (mixes[j]*dm).astype(BF)
            rbs.append(rb)
            col_rows.append(jnp.sum(rb.astype(F32), axis=0, keepdims=True))
        pick = (ocol == 2*p + (orow >= Q).astype(jnp.int32)).astype(BF)
        row_sums = row_sums + dot(jnp.concatenate(rbs, axis=1), pick)
        dxd = dot_tn(jnp.concatenate(mixb, axis=0), dstack)
        ds = dstate[:, sl]
        dsb = ds.astype(BF)
        w = ex_w[:, sl]
        from_state = w*dot(bm, dsb)
        gat = gather_ref[sl, :]
        w_sum = w_sum + dot((xd*from_state).astype(BF), gat)
        e_sum = e_sum + dot((dy*carried).astype(BF), gat)
        dxd = dxd + from_state
        t_sum = t_sum + dot((x*dxd).astype(BF), gat)
        f_sum = f_sum + dot_hi(ex_e[Q-1:Q, sl]*fold8(st*ds), gat.astype(F32))
        dact[:, sl] = xdt*dxd + par_ref[6:7, sl]*dy
        edy = (e*dy).astype(BF)
        dC = dC + dot_nt(edy, stb)
        dB = dB + dot_nt((w*xd).astype(BF), dsb)
        dstate[:, sl] = ex_e[Q-1:Q, sl]*ds + dot(cm_t, edy)
    dsc = dscores.astype(BF)
    dact[:, width:width+NS] = dB + dot_tn(dsc, cm)
    dact[:, width+NS:] = dC + dot(dsc, bm)
    cols = jnp.concatenate(col_rows + [jnp.zeros((128-len(col_rows), Q), F32)], axis=0).T
    upper = jnp.logical_not(lower) | (lax.broadcasted_iota(jnp.int32, (Q, Q), 0) == lax.broadcasted_iota(jnp.int32, (Q, Q), 1))
    da = dot_hi(upper.astype(F32), row_sums-cols+e_sum) + dot_hi((lower & jnp.logical_not(upper)).astype(F32), w_sum) + jnp.sum(f_sum, axis=0, keepdims=True)
    keep = lane < n_heads
    ddt = da*rate + t_sum
    draw = jnp.where(keep, ddt*jax.nn.sigmoid(raw), 0.0)
    gp_ref[:, 2*width+2*NS:] = draw.astype(BF)
    acc[56:64, 0:128] += fold8(draw)
    acc[56:64, 128:256] += fold8(jnp.where(keep, da*dt*rate, 0.0))
    dconv = dact[...]*(sg+act*(1.0-sg))
    dext[0:Q, :] = dconv
    dpre = par_ref[3:4, :]*dconv
    for k in range(CONV-1):
        dpre = dpre + par_ref[k:k+1, :]*dext[3-k:3-k+Q, :]
    gp_ref[:, width:2*width+2*NS] = dpre.astype(BF)
    for k in range(CONV):
        acc[8*k:8*k+8, :] += fold8(dconv*ext[5+k:5+k+Q, :])
    acc[32:40, :] += fold8(dconv)
    dext[Q:, :] = dext[0:8, :]
    @pl.when(step == steps-1)
    def _():
        rows = [jnp.sum(acc[8*k:8*k+8, :], axis=0, keepdims=True) for k in range(8)]
        acc_out[...] = jnp.concatenate(rows, axis=0)

def mixer_bwd(pre, par, spread, gather, states, dh, kap, width, n_heads):
    T = pre.shape[0]; n = T//Q; pw = pre.shape[1]
    rev = lambda i: n-1-i
    return pl.pallas_call(
        functools.partial(bwd_kernel, width, n_heads),
        grid=(n,),
        in_specs=[pl.BlockSpec((Q, pw), lambda i: (n-1-i, 0)),
                  pl.BlockSpec((8, pw), lambda i: (jnp.maximum((n-1-i)*(Q//8)-1, 0), 0)),
                  pl.BlockSpec(par.shape, lambda i: (0, 0)),
                  pl.BlockSpec(spread.shape, lambda i: (0, 0)),
                  pl.BlockSpec(gather.shape, lambda i: (0, 0)),
                  pl.BlockSpec((1, NS, width), lambda i: (n-1-i, 0, 0)),
                  pl.BlockSpec((Q, width), lambda i: (n-1-i, 0)),
                  pl.BlockSpec((Q, 1), lambda i: (n-1-i, 0))],
        out_specs=[pl.BlockSpec((Q, pw), lambda i: (n-1-i, 0)),
                   pl.BlockSpec((8, width+2*NS), lambda i: (0, 0))],
        out_shape=[jax.ShapeDtypeStruct((T, pw), BF), jax.ShapeDtypeStruct((8, width+2*NS), F32)],
        scratch_shapes=[pltpu.VMEM((Q+8, width+2*NS), F32), pltpu.VMEM((Q+8, width+2*NS), F32), pltpu.VMEM((NS, width), F32)]
            + [pltpu.VMEM((Q, width), F32)]*3
            + [pltpu.VMEM((64, width+2*NS), F32), pltpu.VMEM((Q, width+2*NS), F32), pltpu.VMEM((8, 128), F32)],
        compiler_params=pltpu.CompilerParams(dimension_semantics=("arbitrary",), vmem_limit_bytes=56<<20),
        name="mixer_bwd",
    )(pre, pre, par, spread, gather, states, dh, kap)


EPSILON = 1e-05
HEAD_PAD = 128


def swap_sections(value):
    count = lax.axis_size("section")
    return lax.ppermute(value, "section", [(i, (i + 1) % count) for i in range(count)])


def token_gather(value):
    return lax.all_gather(value, "tensor", axis=0, tiled=True)


def token_scatter(value):
    return lax.psum_scatter(value, "tensor", scatter_dimension=0, tiled=True)


def weight_gather(own, is_first):
    half = own.shape[0] // 2
    low, high = own[:half], own[half:]
    got = swap_sections(jnp.where(is_first, high, low))
    first_piece = jnp.where(is_first, low, got)
    second_piece = jnp.where(is_first, got, high)
    return tuple(
        lax.all_gather(piece, ("dp", "section"), axis=0, tiled=True)
        for piece in (first_piece, second_piece)
    )


def grad_scatter(value):
    return lax.psum_scatter(
        value.astype(BF), ("dp", "section"), scatter_dimension=0, tiled=True
    )


def join_halves(first_part, second_part, is_first):
    own = jnp.where(is_first, first_part, second_part)
    got = swap_sections(jnp.where(is_first, second_part, first_part))
    low = jnp.where(is_first, own, got)
    high = jnp.where(is_first, got, own)
    return jnp.concatenate([low, high], axis=0).astype(F32)


def local(
    stream, cotangent, norm_gain, in_zx, in_dt, in_bc, out_proj, conv_x, conv_x_bias,
    conv_bc, conv_bc_bias, dt_bias, a_log, d_skip, gate_gain,
):
    section = lax.axis_index("section")
    is_first = section == 0
    model = stream.shape[3]
    rows = stream.shape[2]
    width = conv_x.shape[2]
    heads = dt_bias.shape[1]
    shard = in_zx.shape[1]
    total_inner = width * lax.axis_size("tensor")
    wide = width + 2 * NS
    row_start = lax.axis_index("tensor") * rows

    def padded(value):
        return jnp.pad(value, (0, wide - value.shape[0]))[None]

    gain_rows = -(-model // wide)
    own_par = jnp.concatenate(
        [
            jnp.concatenate([conv_x[0], conv_bc[0]], axis=1),
            jnp.concatenate([conv_x_bias[0], conv_bc_bias[0]])[None],
            padded(gate_gain[0]),
            padded(jnp.repeat(d_skip[0], width // heads)),
            padded(dt_bias[0]),
            padded(a_log[0]),
            jnp.pad(norm_gain[0], (0, gain_rows * wide - model)).reshape(gain_rows, wide),
            jnp.zeros((7 - gain_rows, wide), F32),
        ],
        axis=0,
    )
    other_par = swap_sections(own_par)
    pars = (jnp.where(is_first, own_par, other_par), jnp.where(is_first, other_par, own_par))
    gains = tuple(par[9 : 9 + gain_rows].reshape(-1)[:model] for par in pars)

    own_in = jnp.concatenate(
        [
            in_zx[0].reshape(shard, 2 * width),
            in_bc[0],
            jnp.pad(in_dt[0], ((0, 0), (0, HEAD_PAD - heads))),
        ],
        axis=1,
    )
    own_out = out_proj[0].T
    w_in = weight_gather(own_in, is_first)
    w_out = weight_gather(own_out, is_first)

    head_of = jnp.arange(width) // (width // heads)
    spread = (jnp.arange(2 * HEAD_PAD)[:, None] % HEAD_PAD == head_of[None, :]).astype(BF)
    gather = (head_of[:, None] == jnp.arange(HEAD_PAD)[None, :]).astype(BF)

    def forward(layer, u):
        inv = lax.rsqrt(jnp.mean(u * u, axis=1, keepdims=True) + EPSILON)
        xn = token_gather((u * inv * gains[layer][None, :]).astype(BF))
        pre = dot(xn, w_in[layer])
        yn, squares, states = mixer_fwd(pre, pars[layer], spread, width)
        partial = dot_nt(yn, w_out[layer])
        total = token_scatter(partial)
        squares = lax.dynamic_slice_in_dim(lax.psum(squares[:, 0], "tensor"), row_start, rows)
        q = lax.rsqrt(squares / total_inner + EPSILON)[:, None]
        projected = total * q
        return (u + projected).astype(BF), (u, inv, xn, pre, yn, states, q, projected)

    def backward(layer, g, kept):
        u, inv, xn, pre, yn, states, q, projected = kept
        gq = token_gather((g * q).astype(BF))
        kappa = q * q / total_inner * jnp.sum(g * projected, axis=1, keepdims=True)
        kappa = token_gather(kappa)
        dh = dot(gq, w_out[layer])
        gp, acc = mixer_bwd(pre, pars[layer], spread, gather, states, dh, kappa, width, heads)
        dxn = token_scatter(dot_nt(gp, w_in[layer]))
        g_in = dot_tn(xn, gp)
        g_out = dot_tn(gq, yn)
        scaled = dxn * gains[layer][None, :]
        dots = jnp.sum(scaled * u, axis=1, keepdims=True)
        du = g + inv * scaled - u * (inv * inv * inv) * dots / model
        g_gain = jnp.sum(dxn * u * inv, axis=0)
        return du.astype(BF), g_in, g_out, acc, g_gain

    u0 = lax.dynamic_index_in_dim(stream[:, 0], section, 0, False).astype(F32)
    out0, kept0 = forward(0, u0)
    out1, kept1 = forward(1, out0.astype(F32))
    g1 = lax.dynamic_index_in_dim(cotangent[:, 0], section, 0, False).astype(F32)
    du1, g_in1, g_out1, acc1, gain1 = backward(1, g1, kept1)
    half_in1 = grad_scatter(g_in1)
    half_out1 = grad_scatter(g_out1)
    du0, g_in0, g_out0, acc0, gain0 = backward(0, du1.astype(F32), kept0)
    half_in0 = grad_scatter(g_in0)
    half_out0 = grad_scatter(g_out0)
    g_in = join_halves(half_in0, half_in1, is_first)
    g_out = join_halves(half_out0, half_out1, is_first)

    def by_batch(first_value, second_value):
        own = jnp.where(is_first, first_value, second_value)
        got = swap_sections(jnp.where(is_first, second_value, first_value))
        stacked = jnp.stack([jnp.where(is_first, own, got), jnp.where(is_first, got, own)])
        return stacked[None, :, None]

    def minor(acc, gain):
        return jnp.concatenate(
            [acc, jnp.pad(gain, (0, gain_rows * wide - model)).reshape(gain_rows, wide)], axis=0
        )

    both = lax.psum(jnp.stack([minor(acc0, gain0), minor(acc1, gain1)]), ("dp", "section"))
    mine = jnp.where(is_first, both[0], both[1])
    shared_bc, shared_gain, bc_rows = lax.psum(
        (mine[0:5, width:], mine[8:], g_in[:, 2 * width : 2 * width + 2 * NS]), "tensor"
    )
    return (
        by_batch(out0, out1),
        by_batch(du0, du1),
        shared_gain.reshape(-1)[:model][None],
        g_in[:, : 2 * width].reshape(shard, 2, width)[None],
        g_in[:, 2 * width + 2 * NS : 2 * width + 2 * NS + heads][None],
        bc_rows[None],
        g_out.T[None],
        mine[0:4, :width][None],
        mine[4, :width][None],
        shared_bc[0:4][None],
        shared_bc[4][None],
        mine[7, :heads][None],
        mine[7, HEAD_PAD : HEAD_PAD + heads][None],
        mine[6, :width].reshape(heads, -1).sum(axis=1)[None],
        mine[5, :width][None],
    )


def solution(mesh):
    in_specs = (
        P(None, "dp", "tensor", None),
        P(None, "dp", "tensor", None),
        P("section", None),
        P("section", "dp", None, "tensor"),
        P("section", "dp", "tensor"),
        P("section", "dp", None),
        P("section", "tensor", "dp"),
        P("section", None, "tensor"),
        P("section", "tensor"),
        P("section", None, None),
        P("section", None),
        P("section", "tensor"),
        P("section", "tensor"),
        P("section", "tensor"),
        P("section", "tensor"),
    )
    out_specs = (
        P("section", None, "dp", "tensor", None),
        P("section", None, "dp", "tensor", None),
        P("section", None),
        P("section", "dp", None, "tensor"),
        P("section", "dp", "tensor"),
        P("section", "dp", None),
        P("section", "tensor", "dp"),
        P("section", None, "tensor"),
        P("section", "tensor"),
        P("section", None, None),
        P("section", None),
        P("section", "tensor"),
        P("section", "tensor"),
        P("section", "tensor"),
        P("section", "tensor"),
    )
    return jax.shard_map(local, mesh=mesh, in_specs=in_specs, out_specs=out_specs, check_vma=False)
```

time: 2490 us -> 1260 us (0.51)
  matrix products: 559 us -> 108 us
  local copies, waits for them, and re-layouts: 425 us -> 25.4 us
  other arithmetic: 407 us -> 40.5 us
  blocking collectives: 242 us -> 37.4 us
  Pallas kernels: 0 us -> 109 us
  waiting for transfers between devices: 812 us -> 905 us
    unnamed x34 -> x18, waiting for transfers between devices: 493 us -> 1.49 us
    dot_general x75 -> x12, matrix products: 559 us -> 108 us  [the longest x4 37.2 us: dot_nt(): lax.dot_general(a, b, (((1,), (1,)), ((), ())), preferred_element_type=F32)]
    reduce_scatter x9 -> x8, waiting for transfers between devices: 113 us -> 447 us  [the longest x4 252 us: grad_scatter(): lax.psum_scatter(value.astype(BF), ('dp', 'section'), scatter_dimension=0...]
    psum x11 -> x3, blocking collectives: 202 us -> 25.9 us  [the longest x2 13.7 us: forward(): lax.psum(squares[:, 0], 'tensor')]
    all_gather x11 -> x8, waiting for transfers between devices: 149 us -> 318 us  [the longest x4 237 us: weight_gather(): lax.all_gather(piece, ('dp', 'section'), axis=0, tiled=True)]
    reduce_sum x41 -> x7, other arithmetic: 144 us -> 13.3 us  [the longest x2 5.28 us: backward(): kappa = q * q / total_inner * jnp.sum(g * projected, axis=1, keepdims=True)]
    pallas_call x0 -> x4, Pallas kernels: none -> 109 us  [the longest x2 84.3 us: mixer_bwd(): pl.pallas_call(functools.partial(bwd_kernel, width, n_heads), grid=(n,),...]
    reshape x56 -> x4, local copies, waits for them, and re-layouts: 87.7 us -> 0.11 us  [the longest x1 0.07 us: local(): jnp.repeat(d_skip[0], width // heads)]
  transfers between devices with their start and end apart: 31 -> 25, of which waited for: 17 -> 22; matrix products, arithmetic and copies ran while one was open for 37% -> 9% of each run, Pallas kernels for 0% -> 5%
where the time goes in v1:
time: 1260 us; the launch traced here: 1250 us
  waiting for transfers between devices  905 us (72%)
  Pallas kernels  109 us (9%)
  matrix products  108 us (9%)
  other arithmetic  40.5 us (3%)
  blocking collectives  37.4 us (3%)
  local copies, waits for them, and re-layouts  25.4 us (2%)
  between operations  15 us (1%)
    reduce_scatter x4, waiting for transfers between devices, grad_scatter(): lax.psum_scatter(value.astype(BF), ('dp', 'section'), scatter_dimension=0...  252 us
    all_gather x4, waiting for transfers between devices, weight_gather(): lax.all_gather(piece, ('dp', 'section'), axis=0, tiled=True)  237 us
    reduce_scatter x4, waiting for transfers between devices, token_scatter(): return lax.psum_scatter(value, 'tensor', scatter_dimension=0, tiled=True)  195 us
    pallas_call x2, Pallas kernels, mixer_bwd(): pl.pallas_call(functools.partial(bwd_kernel, width, n_heads), grid=(n,),...  84.3 us
    all_gather x4, waiting for transfers between devices, token_gather(): return lax.all_gather(value, 'tensor', axis=0, tiled=True)  80.6 us
    psum x1, waiting for transfers between devices, local(): lax.psum(jnp.stack([minor(acc0, gain0), minor(acc1, gain1)]), ('dp', 'sec...  64.5 us
    ppermute x7, waiting for transfers between devices, swap_sections(): lax.ppermute(value, 'section', [(i, (i + 1) % count) for i in range(count)])  56.5 us
    dot_general x4, matrix products, dot_nt(): lax.dot_general(a, b, (((1,), (1,)), ((), ())), preferred_element_type=F32)  37.2 us
  transfers between devices with their start and end apart: 25, of which 22 were waited for; matrix products, arithmetic and copies ran while one was open for 9% of the time, Pallas kernels for 5%

profile of v1, /device:TPU:9, one launch (start us, length us, event | category | flops | bytes accessed | tf_op | source)
XLA Modules:
  0.0 1250.0 jit_solution(7614660240861165130)
XLA Ops:
  21.0 15.1 %collective-permute-done.1 = bf16[192,1920]{1,0:T(8,128)(2,1)S(1)} collective-permute-done((bf16[192,1920]{1,0:T(8,128)(2,1)S(1)}, bf16[192,1920]{1,0:T(8,128)(2,1)S(1)}, u32[]{:S(2)}, u32[]{:S(2)}) %collective-permute-start.1) | collective-permute-done | bytes 737312 | tf_op jit(solution)/shard_map/ppermute | solution.py:262
  49.9 93.7 %all-gather.15.cloned.1.call-done = bf16[1536,1920]{1,0:T(8,128)(2,1)} async-done(((bf16[192,1920]{1,0:T(8,128)(2,1)}), bf16[1536,1920]{1,0:T(8,128)(2,1)}) %all-gather.15.cloned.1.call-update) | async-done | bytes 5898256 | tf_op jit(solution)/shard_map/all_gather | solution.py:280
  155.5 12.4 mixer_fwd.2
  169.6 27.8 %all-gather.17.cloned.1.call-done = bf16[1536,768]{1,0:T(8,128)(2,1)} async-done(((bf16[192,768]{1,0:T(8,128)(2,1)}), bf16[1536,768]{1,0:T(8,128)(2,1)}) %all-gather.17.cloned.1.call-update) | async-done | bytes 2359312 | tf_op jit(solution)/shard_map/all_gather | solution.py:280
  211.4 50.7 %reduce-scatter.9.cloned.1.call-done = f32[256,1536]{1,0:T(8,128)} async-done(((f32[1024,1536]{1,0:T(8,128)}), f32[256,1536]{1,0:T(8,128)}) %reduce-scatter.9.cloned.1.call-update) | async-done | bytes 1572880 | tf_op jit(solution)/shard_map/reduce_scatter | solution.py:270
  266.4 89.8 %all-gather.21.cloned.1.call-done = bf16[1536,1920]{1,0:T(8,128)(2,1)} async-done(((bf16[192,1920]{1,0:T(8,128)(2,1)}), bf16[1536,1920]{1,0:T(8,128)(2,1)}) %all-gather.21.cloned.1.call-update) | async-done | bytes 5898256 | tf_op jit(solution)/shard_map/all_gather | solution.py:280
  356.2 31.7 %all-gather.19.cloned.1.call-done = bf16[1024,1536]{1,0:T(8,128)(2,1)} async-done(((bf16[256,1536]{1,0:T(8,128)(2,1)}), bf16[1024,1536]{1,0:T(8,128)(2,1)}) %all-gather.19.cloned.1.call-update) | async-done | bytes 3145744 | tf_op jit(solution)/shard_map/all_gather | solution.py:266
  399.8 12.4 mixer_fwd.3
  415.0 26.1 %all-gather.23.cloned.1.call-done = bf16[1536,768]{1,0:T(8,128)(2,1)} async-done(((bf16[192,768]{1,0:T(8,128)(2,1)}), bf16[1536,768]{1,0:T(8,128)(2,1)}) %all-gather.23.cloned.1.call-update) | async-done | bytes 2359312 | tf_op jit(solution)/shard_map/all_gather | solution.py:280
  455.7 51.3 %reduce-scatter.11.cloned.1.call-done = f32[256,1536]{1,0:T(8,128)} async-done(((f32[1024,1536]{1,0:T(8,128)}), f32[256,1536]{1,0:T(8,128)}) %reduce-scatter.11.cloned.1.call-update) | async-done | bytes 1572880 | tf_op jit(solution)/shard_map/reduce_scatter | solution.py:270
  517.9 21.2 %all-gather.25.cloned.1.call-done = bf16[1024,1536]{1,0:T(8,128)(2,1)} async-done(((bf16[256,1536]{1,0:T(8,128)(2,1)}), bf16[1024,1536]{1,0:T(8,128)(2,1)}) %all-gather.25.cloned.1.call-update) | async-done | bytes 3145744 | tf_op jit(solution)/shard_map/all_gather | solution.py:266
  545.9 42.0 %mixer_bwd.2 = (bf16[1024,1920]{1,0:T(8,128)(2,1)}, f32[8,1024]{1,0:T(8,128)}) custom-call(f32[1024,1920]{1,0:T(8,128)} %fusion.39.pre_ref.halo_ref, f32[1024,1920]{1,0:T(8,128)} %fusion.39.pre_ref.halo_ref, f32[16,1024]{1,0:T(8,128)} %copy-done.4, bf16[256,768]{1,0:T(8,128)(2,1)} %copy-done, bf16[768,128]{1,0:T(8,128)(2,1)} %fusion.28.gather_ref, ...), custom_call_target="tpu_custom_call" | custom-call | tf_op jit(solution)/shard_map/mixer_bwd/pallas_call | solution.py:234
  599.7 58.4 %reduce-scatter.13.cloned.1.call-done = f32[256,1536]{1,0:T(8,128)} async-done(((f32[1024,1536]{1,0:T(8,128)}), f32[256,1536]{1,0:T(8,128)}) %reduce-scatter.13.cloned.1.call-update) | async-done | bytes 1572880 | tf_op jit(solution)/shard_map/reduce_scatter | solution.py:270
  671.0 22.7 %all-gather.27.cloned.1.call-done = bf16[1024,1536]{1,0:T(8,128)(2,1)} async-done(((bf16[256,1536]{1,0:T(8,128)(2,1)}), bf16[1024,1536]{1,0:T(8,128)(2,1)}) %all-gather.27.cloned.1.call-update) | async-done | bytes 3145744 | tf_op jit(solution)/shard_map/all_gather | solution.py:266
  723.6 42.2 %mixer_bwd.3 = (bf16[1024,1920]{1,0:T(8,128)(2,1)}, f32[8,1024]{1,0:T(8,128)}) custom-call(f32[1024,1920]{1,0:T(8,128)} %fusion.37.pre_ref.halo_ref, f32[1024,1920]{1,0:T(8,128)} %fusion.37.pre_ref.halo_ref, f32[16,1024]{1,0:T(8,128)} %copy-done.3, bf16[256,768]{1,0:T(8,128)(2,1)} %copy-done, bf16[768,128]{1,0:T(8,128)(2,1)} %fusion.28.gather_ref, ...), custom_call_target="tpu_custom_call" | custom-call | tf_op jit(solution)/shard_map/mixer_bwd/pallas_call | solution.py:234
  791.6 24.0 %collective-permute-done.3 = bf16[256,1536]{1,0:T(8,128)(2,1)S(1)} collective-permute-done((bf16[256,1536]{1,0:T(8,128)(2,1)S(1)}, bf16[256,1536]{1,0:T(8,128)(2,1)S(1)}, u32[]{:S(2)}, u32[]{:S(2)}) %collective-permute-start.3) | collective-permute-done | bytes 786464 | tf_op jit(solution)/shard_map/ppermute | solution.py:262
  817.1 22.9 %reduce-scatter.21.cloned.1.call-done = bf16[192,768]{1,0:T(8,128)(2,1)} async-done(((bf16[1536,768]{1,0:T(8,128)(2,1)}), bf16[192,768]{1,0:T(8,128)(2,1)}) %reduce-scatter.21.cloned.1.call-update) | async-done | bytes 294928 | tf_op jit(solution)/shard_map/reduce_scatter | solution.py:286
  842.4 114.2 %reduce-scatter.19.cloned.1.call-done = bf16[192,1920]{1,0:T(8,128)(2,1)} async-done(((bf16[1536,1920]{1,0:T(8,128)(2,1)}), bf16[192,1920]{1,0:T(8,128)(2,1)}) %reduce-scatter.19.cloned.1.call-update) | async-done | bytes 737296 | tf_op jit(solution)/shard_map/reduce_scatter | solution.py:286
  956.6 115.3 %reduce-scatter.17.cloned.1.call-done = bf16[192,1920]{1,0:T(8,128)(2,1)} async-done(((bf16[1536,1920]{1,0:T(8,128)(2,1)}), bf16[192,1920]{1,0:T(8,128)(2,1)}) %reduce-scatter.17.cloned.1.call-update) | async-done | bytes 737296 | tf_op jit(solution)/shard_map/reduce_scatter | solution.py:286
  1078.2 12.0 collective-permute-done.5
  1098.5 34.6 %reduce-scatter.15.cloned.1.call-done = f32[256,1536]{1,0:T(8,128)} async-done(((f32[1024,1536]{1,0:T(8,128)}), f32[256,1536]{1,0:T(8,128)}) %reduce-scatter.15.cloned.1.call-update) | async-done | bytes 1572880 | tf_op jit(solution)/shard_map/reduce_scatter | solution.py:270
  1140.4 64.5 %all-reduce.12.cloned.1.call-done = f32[2,10,1024]{2,1,0:T(8,128)} async-done(((f32[2,10,1024]{2,1,0:T(8,128)}), f32[2,10,1024]{2,1,0:T(8,128)}) %all-reduce.12.cloned.1.call-update) | async-done | bytes 81936 | tf_op jit(solution)/shard_map/psum | solution.py:403
  1206.7 12.2 all-reduce.8
  1224.5 16.7 %all-reduce.14.cloned.1.call-done = f32[1,384,256]{2,1,0:T(8,128)} async-done(((f32[1,384,256]{2,1,0:T(8,128)}), f32[1,384,256]{2,1,0:T(8,128)}) %all-reduce.14.cloned.1.call-update) | async-done | bytes 393232 | tf_op jit(solution)/shard_map/psum | solution.py:405
  (204 shorter events, 220.9 us)
Async XLA Ops:
  7.2 42.7 %all-gather.13.cloned.1.call-start = ((), (), s32[]{:S(2)}) async-start(), calls=%async_computation.8 | async-start | bytes 3932160 | tf_op jit(solution)/shard_map/all_gather | solution.py:266
  18.6 125.0 %all-gather.15.cloned.1.call-start = ((), (), s32[]{:S(2)}) async-start(), calls=%async_computation.9 | async-start | bytes 6635520 | tf_op jit(solution)/shard_map/all_gather | solution.py:280
  19.7 16.4 %collective-permute-start.1 = (bf16[192,1920]{1,0:T(8,128)(2,1)S(1)}, bf16[192,1920]{1,0:T(8,128)(2,1)S(1)}, u32[]{:S(2)}, u32[]{:S(2)}) collective-permute-start(bf16[192,1920]{1,0:T(8,128)(2,1)S(1)} %broadcast_select_fusion.10), channel_id=1, source_target_pairs={{0,16},{16,0},{1,17},{17,1},{2,18},{18,2},{3,19},{19,3},{4,20},{20... | collective-permute-start | bytes 2211848 | tf_op jit(solution)/shard_map/ppermute | solution.py:262
  37.4 160.0 %all-gather.17.cloned.1.call-start = ((), (), s32[]{:S(2)}) async-start(), calls=%async_computation.10 | async-start | bytes 2654208 | tf_op jit(solution)/shard_map/all_gather | solution.py:280
  37.7 6.2 collective-permute-start.2
  44.8 217.4 %reduce-scatter.9.cloned.1.call-start = ((), (), s32[]{:S(2)}) async-start(), calls=%async_computation.11 | async-start | bytes 7864320 | tf_op jit(solution)/shard_map/reduce_scatter | solution.py:270
  203.6 152.6 %all-gather.21.cloned.1.call-start = ((), (), s32[]{:S(2)}) async-start(), calls=%async_computation.13 | async-start | bytes 6635520 | tf_op jit(solution)/shard_map/all_gather | solution.py:280
  204.2 183.7 %all-gather.19.cloned.1.call-start = ((), (), s32[]{:S(2)}) async-start(), calls=%async_computation.12 | async-start | bytes 3932160 | tf_op jit(solution)/shard_map/all_gather | solution.py:266
  265.4 175.7 %all-gather.23.cloned.1.call-start = ((), (), s32[]{:S(2)}) async-start(), calls=%async_computation.14 | async-start | bytes 2654208 | tf_op jit(solution)/shard_map/all_gather | solution.py:280
  266.1 240.9 %reduce-scatter.11.cloned.1.call-start = ((), (), s32[]{:S(2)}) async-start(), calls=%async_computation.15 | async-start | bytes 7864320 | tf_op jit(solution)/shard_map/reduce_scatter | solution.py:270
  448.5 90.6 %all-gather.25.cloned.1.call-start = ((), (), s32[]{:S(2)}) async-start(), calls=%async_computation.16 | async-start | bytes 3932160 | tf_op jit(solution)/shard_map/all_gather | solution.py:266
  509.9 148.2 %reduce-scatter.13.cloned.1.call-start = ((), (), s32[]{:S(2)}) async-start(), calls=%async_computation.17 | async-start | bytes 7864320 | tf_op jit(solution)/shard_map/reduce_scatter | solution.py:270
  599.7 94.0 %all-gather.27.cloned.1.call-start = ((), (), s32[]{:S(2)}) async-start(), calls=%async_computation.18 | async-start | bytes 3932160 | tf_op jit(solution)/shard_map/all_gather | solution.py:266
  664.5 152.6 %reduce-scatter.23.cloned.1.call-start = ((), (), s32[]{:S(2)}) async-start(), calls=%async_computation.25 | async-start | bytes 2654208 | tf_op jit(solution)/shard_map/reduce_scatter | solution.py:286
  671.0 168.9 %reduce-scatter.21.cloned.1.call-start = ((), (), s32[]{:S(2)}) async-start(), calls=%async_computation.24 | async-start | bytes 2654208 | tf_op jit(solution)/shard_map/reduce_scatter | solution.py:286
  699.8 256.8 %reduce-scatter.19.cloned.1.call-start = ((), (), s32[]{:S(2)}) async-start(), calls=%async_computation.22 | async-start | bytes 6635520 | tf_op jit(solution)/shard_map/reduce_scatter | solution.py:286
  711.1 360.8 %reduce-scatter.17.cloned.1.call-start = ((), (), s32[]{:S(2)}) async-start(), calls=%async_computation.21 | async-start | bytes 6635520 | tf_op jit(solution)/shard_map/reduce_scatter | solution.py:286
  776.4 356.7 %reduce-scatter.15.cloned.1.call-start = ((), (), s32[]{:S(2)}) async-start(), calls=%async_computation.19 | async-start | bytes 7864320 | tf_op jit(solution)/shard_map/reduce_scatter | solution.py:270
  788.4 416.5 %all-reduce.12.cloned.1.call-start = ((), (), s32[]{:S(2)}) async-start(), calls=%async_computation.20 | async-start | bytes 262144 | tf_op jit(solution)/shard_map/psum | solution.py:403
  790.4 25.2 %collective-permute-start.3 = (bf16[256,1536]{1,0:T(8,128)(2,1)S(1)}, bf16[256,1536]{1,0:T(8,128)(2,1)S(1)}, u32[]{:S(2)}, u32[]{:S(2)}) collective-permute-start(bf16[256,1536]{1,0:T(8,128)(2,1)S(1)} %broadcast_select_fusion.2), channel_id=1, source_target_pairs={{0,16},{16,0},{1,17},{17,1},{2,18},{18,2},{3,19},{19,3},{4,20},{20... | collective-permute-start | bytes 2359304 | tf_op jit(solution)/shard_map/ppermute | solution.py:262
  840.9 234.8 %collective-permute-start.6 = (bf16[192,768]{1,0:T(8,128)(2,1)S(1)}, bf16[192,768]{1,0:T(8,128)(2,1)}, u32[]{:S(2)}, u32[]{:S(2)}) collective-permute-start(bf16[192,768]{1,0:T(8,128)(2,1)S(1)} %broadcast_select_fusion.13), channel_id=1, source_target_pairs={{0,16},{16,0},{1,17},{17,1},{2,18},{18,2},{3,19},{19,3},{4,20},{20... | collective-permute-start | bytes 884744 | tf_op jit(solution)/shard_map/ppermute | solution.py:262
  1073.1 17.2 %collective-permute-start.5 = (bf16[192,1920]{1,0:T(8,128)(2,1)S(1)}, bf16[192,1920]{1,0:T(8,128)(2,1)}, u32[]{:S(2)}, u32[]{:S(2)}) collective-permute-start(bf16[192,1920]{1,0:T(8,128)(2,1)S(1)} %broadcast_select_fusion.6), channel_id=1, source_target_pairs={{0,16},{16,0},{1,17},{17,1},{2,18},{18,2},{3,19},{19,3},{4,20},{20... | collective-permute-start | bytes 2211848 | tf_op jit(solution)/shard_map/ppermute | solution.py:262
  1135.9 105.3 %all-reduce.14.cloned.1.call-start = ((), (), s32[]{:S(2)}) async-start(), calls=%async_computation.23 | async-start | bytes 786432 | tf_op jit(solution)/shard_map/psum | solution.py:405
  1139.1 83.9 %collective-permute-start.4 = (bf16[256,1536]{1,0:T(8,128)(2,1)S(1)}, bf16[256,1536]{1,0:T(8,128)(2,1)S(1)}, u32[]{:S(2)}, u32[]{:S(2)}) collective-permute-start(bf16[256,1536]{1,0:T(8,128)(2,1)S(1)} %get-tuple-element.86), channel_id=1, source_target_pairs={{0,16},{16,0},{1,17},{17,1},{2,18},{18,2},{3,19},{19,3},{4,20},{20... | collective-permute-start | bytes 2359304 | tf_op jit(solution)/shard_map/ppermute | solution.py:262
  (26 other events, 1675.1 us)
Sparse Core Ops, SparseCore 0:
  18.7 31.2 all-gather.12
  52.7 90.8 all-gather.14
  145.8 51.5 all-gather.16
  203.8 58.3 reduce-scatter.8
  264.7 91.4 all-gather.20
  358.2 29.6 all-gather.18
  390.7 50.2 all-gather.22
  448.6 58.3 reduce-scatter.10
  510.0 29.0 all-gather.24
  599.8 58.2 reduce-scatter.12
  664.6 29.0 all-gather.26
  697.6 66.9 reduce-scatter.22
  768.1 71.8 reduce-scatter.20
  843.5 113.1 reduce-scatter.18
  960.1 111.7 reduce-scatter.16
  1074.3 58.7 reduce-scatter.14
  1136.9 67.9 all-reduce.11
  1207.7 33.5 all-reduce.13

commit v2 on v1

--- a/solution.py
+++ b/solution.py
@@ -78,7 +78,10 @@
         squares = squares + yg*yg
         yn_ref[:, sl] = (yg*par_ref[5:6, sl]).astype(BF)
         state[:, sl] = ex_e[Q-1:Q, sl]*st + dot(bm_t, (ex_w[:, sl]*xd).astype(BF))
-    sq_ref[...] = jnp.sum(squares, axis=1, keepdims=True)
+    sq_ref[...] = lax.dot_general(
+        jnp.ones((8, 128), F32), squares, (((1,), (1,)), ((), ())),
+        preferred_element_type=F32, precision=lax.Precision.HIGHEST,
+    )
 
 def mixer_fwd(pre, par, spread, width):
     T = pre.shape[0]; n = T//Q
@@ -90,9 +93,9 @@
                   pl.BlockSpec(par.shape, lambda i: (0, 0)),
                   pl.BlockSpec(spread.shape, lambda i: (0, 0))],
         out_specs=[pl.BlockSpec((Q, width), lambda i: (i, 0)),
-                   pl.BlockSpec((Q, 1), lambda i: (i, 0)),
+                   pl.BlockSpec((8, Q), lambda i: (i, 0)),
                    pl.BlockSpec((1, NS, width), lambda i: (i, 0, 0))],
-        out_shape=[jax.ShapeDtypeStruct((T, width), BF), jax.ShapeDtypeStruct((T, 1), F32),
+        out_shape=[jax.ShapeDtypeStruct((T, width), BF), jax.ShapeDtypeStruct((8*n, Q), F32),
                    jax.ShapeDtypeStruct((n, NS, width), F32)],
         scratch_shapes=[pltpu.VMEM((Q+8, width+2*NS), F32), pltpu.VMEM((NS, width), F32)]
             + [pltpu.VMEM((Q, width), F32)]*3,
@@ -130,7 +133,7 @@
     scores = dot_nt(cm, bm)
     cm_t = cm.T
     lane = lax.broadcasted_iota(jnp.int32, (Q, 128), 1)
-    kap = kap_ref[...]
+    kap = kap_ref[:, 0:1].astype(F32) + kap_ref[:, 1:2].astype(F32)
     dscores = jnp.zeros((Q, Q), F32)
     row_sums = jnp.zeros((Q, 128), F32)
     col_rows = []
@@ -241,7 +244,7 @@
                   pl.BlockSpec(gather.shape, lambda i: (0, 0)),
                   pl.BlockSpec((1, NS, width), lambda i: (n-1-i, 0, 0)),
                   pl.BlockSpec((Q, width), lambda i: (n-1-i, 0)),
-                  pl.BlockSpec((Q, 1), lambda i: (n-1-i, 0))],
+                  pl.BlockSpec((Q, 128), lambda i: (n-1-i, 0))],
         out_specs=[pl.BlockSpec((Q, pw), lambda i: (n-1-i, 0)),
                    pl.BlockSpec((8, width+2*NS), lambda i: (0, 0))],
         out_shape=[jax.ShapeDtypeStruct((T, pw), BF), jax.ShapeDtypeStruct((8, width+2*NS), F32)],
@@ -253,8 +256,607 @@
     )(pre, pre, par, spread, gather, states, dh, kap)
 
 
+MESH_ID = pl.DeviceIdType.MESH
+
+
+def peer(axis, index):
+    return {axis: index}
+
+
+def greet(peers):
+    barrier = pltpu.get_barrier_semaphore()
+    for where in peers:
+        pl.semaphore_signal(barrier, inc=1, device_id=where, device_id_type=MESH_ID)
+    pl.semaphore_wait(barrier, len(peers))
+
+
+def remote(src, dst, send_sem, recv_sem, where):
+    return pltpu.make_async_remote_copy(
+        src_ref=src, dst_ref=dst, send_sem=send_sem, recv_sem=recv_sem,
+        device_id=where, device_id_type=MESH_ID,
+    )
+
+
+PIECES = 2
+
+
+def token_gather_kernel(count, *refs):
+    ins, outs = refs[:count], refs[count : 2 * count]
+    send_sem, recv_sem, own_sem = refs[2 * count :]
+    me = lax.axis_index("tensor")
+    near, far = me ^ 1, me ^ 2
+    greet((peer("tensor", near), peer("tensor", far)))
+
+    def copies(index):
+        source, target = ins[index], outs[index]
+        rows = source.shape[0]
+        parts = PIECES if index == 0 else 1
+        size = rows // parts
+        for part in range(parts):
+            here = pl.ds(part * size, size)
+            own = pl.ds(pl.multiple_of(me * rows + part * size, 16), size)
+            other = pl.ds(pl.multiple_of(far * rows + part * size, 16), size)
+            to_far = remote(source.at[here], target.at[own], send_sem.at[index, part, 0],
+                            recv_sem.at[index, part, 0], peer("tensor", far))
+            to_near = remote(source.at[here], target.at[own], send_sem.at[index, part, 1],
+                             recv_sem.at[index, part, 1], peer("tensor", near))
+            relay = remote(target.at[other], target.at[other], send_sem.at[index, part, 2],
+                           recv_sem.at[index, part, 2], peer("tensor", near))
+            yield to_far, to_near, relay
+
+    every = [triple for index in range(count) for triple in copies(index)]
+    for to_far, _, _ in every:
+        to_far.start()
+    for _, to_near, _ in every:
+        to_near.start()
+    locals_ = []
+    for index in range(count):
+        rows = ins[index].shape[0]
+        local_copy = pltpu.make_async_copy(
+            ins[index], outs[index].at[pl.ds(pl.multiple_of(me * rows, 16), rows)], own_sem.at[index]
+        )
+        local_copy.start()
+        locals_.append(local_copy)
+    for to_far, _, relay in every:
+        to_far.wait_recv()
+        relay.start()
+    for to_far, to_near, relay in every:
+        to_near.wait_recv()
+        relay.wait_recv()
+        to_far.wait_send()
+        to_near.wait_send()
+        relay.wait_send()
+    for local_copy in locals_:
+        local_copy.wait()
+
+
+def token_gather(values, group_id):
+    count = len(values)
+    n = lax.axis_size("tensor")
+    return pl.pallas_call(
+        functools.partial(token_gather_kernel, count),
+        out_shape=[jax.ShapeDtypeStruct((n * v.shape[0],) + v.shape[1:], v.dtype) for v in values],
+        in_specs=[pl.BlockSpec(memory_space=pltpu.VMEM)] * count,
+        out_specs=[pl.BlockSpec(memory_space=pl.ANY)] * count,
+        scratch_shapes=[
+            pltpu.SemaphoreType.DMA((count, PIECES, 3)),
+            pltpu.SemaphoreType.DMA((count, PIECES, 3)),
+            pltpu.SemaphoreType.DMA((count,)),
+        ],
+        compiler_params=pltpu.CompilerParams(collective_id=group_id, has_side_effects=True),
+        name="token_gather",
+    )(*values)
+
+
+RS_PIECES = 2
+
+
+def token_scatter_kernel(with_side, *refs):
+    if with_side:
+        value_ref, side_ref, out_ref, side_out = refs[:4]
+        rest = refs[4:]
+    else:
+        value_ref, out_ref = refs[:2]
+        rest = refs[2:]
+    from_near, to_far_buf, from_far, send_sem, recv_sem = rest[:5]
+    me = lax.axis_index("tensor")
+    near, far, cross = me ^ 1, me ^ 2, me ^ 3
+    greet((peer("tensor", near), peer("tensor", far)))
+    rows = out_ref.shape[0]
+    size = rows // RS_PIECES
+
+    def block(index, part):
+        return pl.ds(pl.multiple_of(index * rows + part * size, 16), size)
+
+    first, second, third = [], [], []
+    for part in range(RS_PIECES):
+        here = pl.ds(part * size, size)
+        first.append(remote(value_ref.at[block(cross, part)], from_near.at[0, here], send_sem.at[part, 0],
+                            recv_sem.at[part, 0], peer("tensor", near)))
+        second.append(remote(value_ref.at[block(near, part)], from_near.at[1, here], send_sem.at[part, 1],
+                             recv_sem.at[part, 1], peer("tensor", near)))
+        third.append(remote(to_far_buf.at[here], from_far.at[here], send_sem.at[part, 2],
+                            recv_sem.at[part, 2], peer("tensor", far)))
+    for copy in first:
+        copy.start()
+    if with_side:
+        side_near, side_buf, side_far, side_send, side_recv = rest[5:]
+        srows = side_out.shape[0]
+
+        def side_block(index):
+            return pl.ds(pl.multiple_of(index * srows, 8), srows)
+
+        s1 = remote(side_ref.at[side_block(cross)], side_near.at[0], side_send.at[0], side_recv.at[0], peer("tensor", near))
+        s2 = remote(side_ref.at[side_block(near)], side_near.at[1], side_send.at[1], side_recv.at[1], peer("tensor", near))
+        s3 = remote(side_buf, side_far, side_send.at[2], side_recv.at[2], peer("tensor", far))
+        s1.start()
+        s2.start()
+    for copy in second:
+        copy.start()
+    if with_side:
+        s1.wait_recv()
+        side_buf[...] = side_ref[side_block(far), :] + side_near[0]
+        s3.start()
+    for part in range(RS_PIECES):
+        here = pl.ds(part * size, size)
+        first[part].wait_recv()
+        to_far_buf[here, :] = (
+            value_ref[block(far, part), :].astype(F32) + from_near[0, here, :].astype(F32)
+        ).astype(to_far_buf.dtype)
+        third[part].start()
+    if with_side:
+        s2.wait_recv()
+        s3.wait_recv()
+        side_out[...] = side_ref[side_block(me), :] + side_near[1] + side_far[...]
+        s1.wait_send()
+        s2.wait_send()
+        s3.wait_send()
+    for part in range(RS_PIECES):
+        here = pl.ds(part * size, size)
+        second[part].wait_recv()
+        out_ref[here, :] = value_ref[block(me, part), :].astype(F32) + from_near[1, here, :].astype(F32)
+    for part in range(RS_PIECES):
+        here = pl.ds(part * size, size)
+        third[part].wait_recv()
+        out_ref[here, :] = out_ref[here, :] + from_far[here, :].astype(F32)
+    for copy in first + second + third:
+        copy.wait_send()
+
+
+def token_scatter(value, group_id, side=None):
+    n = lax.axis_size("tensor")
+    rows, cols = value.shape[0] // n, value.shape[1]
+    operands = [value]
+    out_shape = [jax.ShapeDtypeStruct((rows, cols), F32)]
+    scratch = [
+        pltpu.VMEM((2, rows, cols), value.dtype),
+        pltpu.VMEM((rows, cols), value.dtype),
+        pltpu.VMEM((rows, cols), value.dtype),
+        pltpu.SemaphoreType.DMA((RS_PIECES, 3)),
+        pltpu.SemaphoreType.DMA((RS_PIECES, 3)),
+    ]
+    if side is not None:
+        srows, scols = side.shape[0] // n, side.shape[1]
+        operands.append(side)
+        out_shape.append(jax.ShapeDtypeStruct((srows, scols), F32))
+        scratch += [
+            pltpu.VMEM((2, srows, scols), F32),
+            pltpu.VMEM((srows, scols), F32),
+            pltpu.VMEM((srows, scols), F32),
+            pltpu.SemaphoreType.DMA((3,)),
+            pltpu.SemaphoreType.DMA((3,)),
+        ]
+    return pl.pallas_call(
+        functools.partial(token_scatter_kernel, side is not None),
+        out_shape=out_shape,
+        in_specs=[pl.BlockSpec(memory_space=pltpu.VMEM)] * len(operands),
+        out_specs=[pl.BlockSpec(memory_space=pltpu.VMEM)] * len(operands),
+        scratch_shapes=scratch,
+        compiler_params=pltpu.CompilerParams(collective_id=group_id, has_side_effects=True, vmem_limit_bytes=40 << 20),
+        name="token_scatter",
+    )(*operands)
+
+
+def open_kernel(n, pieces, in_ref, out_ref, xn_ref, fin_ref, fout_ref, xall_ref,
+                x_ss, x_rs, z_ss, z_rs, own_sem, t_ss, t_rs):
+    sec, z, ten = lax.axis_index("section"), lax.axis_index("dp"), lax.axis_index("tensor")
+    across = peer("section", 1 - sec)
+    near, far = peer("tensor", ten ^ 1), peer("tensor", ten ^ 2)
+    barrier = pltpu.get_barrier_semaphore()
+    for where in (across, near, far):
+        pl.semaphore_signal(barrier, inc=1, device_id=where, device_id_type=MESH_ID)
+
+    @pl.when(z > 0)
+    def _():
+        pl.semaphore_signal(barrier, inc=1, device_id=peer("dp", z - 1), device_id_type=MESH_ID)
+
+    @pl.when(z < n - 1)
+    def _():
+        pl.semaphore_signal(barrier, inc=1, device_id=peer("dp", z + 1), device_id_type=MESH_ID)
+
+    pl.semaphore_wait(barrier, 3 + jnp.where(z > 0, 1, 0) + jnp.where(z < n - 1, 1, 0))
+    sources, fulls = (in_ref, out_ref), (fin_ref, fout_ref)
+    rows = in_ref.shape[0]
+    trows = xn_ref.shape[0]
+
+    def place(p, s):
+        array, offset, count, _ = pieces[p]
+        return fulls[array].at[pl.ds(pl.multiple_of(s * rows + offset, 16), count)]
+
+    def own(p):
+        array, offset, count, _ = pieces[p]
+        return sources[array].at[pl.ds(offset, count)]
+
+    def to_x(p, s, source):
+        return remote(source, place(p, s), x_ss.at[p, s], x_rs.at[p, s], across)
+
+    def to_z(p, s, step, source):
+        side = 0 if step > 0 else 1
+        return remote(source, place(p, s), z_ss.at[side, p, s], z_rs.at[side, p, s], peer("dp", z + step))
+
+    def got_z(p, s, side):
+        remote(own(p), place(p, s), z_ss.at[side, p, 0], z_rs.at[side, p, s], across).wait_recv()
+
+    def spread(p, s, source, right=True, left=True):
+        if right:
+            @pl.when(z < n - 1)
+            def _():
+                to_z(p, s, 1, source).start()
+        if left:
+            @pl.when(z > 0)
+            def _():
+                to_z(p, s, -1, source).start()
+
+    every = range(len(pieces))
+    via = [piece[3] for piece in pieces]
+    me = pl.ds(pl.multiple_of(ten * trows, 16), trows)
+    other = pl.ds(pl.multiple_of((ten ^ 2) * trows, 16), trows)
+    tok_far = remote(xn_ref, xall_ref.at[me], t_ss.at[0], t_rs.at[0], far)
+    tok_near = remote(xn_ref, xall_ref.at[me], t_ss.at[1], t_rs.at[1], near)
+    tok_relay = remote(xall_ref.at[other], xall_ref.at[other], t_ss.at[2], t_rs.at[2], near)
+    tok_own = pltpu.make_async_copy(xn_ref, xall_ref.at[me], own_sem.at[0])
+    tok_far.start()
+    tok_near.start()
+    tok_own.start()
+
+    @pl.when(sec == 0)
+    def _():
+        for p in every:
+            if via[p] == 1:
+                to_x(p, z, own(p)).start()
+            else:
+                spread(p, z, own(p))
+        for p in every:
+            if via[p] == 0:
+                to_x(p, z, own(p)).start()
+        for array in (0, 1):
+            whole = fulls[array].at[pl.ds(pl.multiple_of(z * rows, 16), rows)]
+            pltpu.make_async_copy(sources[array], whole, own_sem.at[1 + array]).start()
+        for d in range(1, n):
+            for p in every:
+                if via[p] == 0:
+                    @pl.when(z - d >= 0)
+                    def _():
+                        got_z(p, z - d, 0)
+                        spread(p, z - d, place(p, z - d), left=False)
+                        to_x(p, z - d, place(p, z - d)).start()
+
+                    @pl.when(z + d < n)
+                    def _():
+                        got_z(p, z + d, 1)
+                        spread(p, z + d, place(p, z + d), right=False)
+                        to_x(p, z + d, place(p, z + d)).start()
+        for d in range(1, n):
+            s = lax.rem(z + d, n)
+            for p in every:
+                if via[p] == 1:
+                    to_x(p, s, place(p, s)).wait_recv()
+
+    @pl.when(sec == 1)
+    def _():
+        for p in every:
+            if via[p] == 1:
+                to_x(p, z, place(p, z)).wait_recv()
+                spread(p, z, place(p, z))
+        for d in range(1, n):
+            for p in every:
+                if via[p] == 1:
+                    @pl.when(z - d >= 0)
+                    def _():
+                        got_z(p, z - d, 0)
+                        spread(p, z - d, place(p, z - d), left=False)
+                        to_x(p, z - d, place(p, z - d)).start()
+
+                    @pl.when(z + d < n)
+                    def _():
+                        got_z(p, z + d, 1)
+                        spread(p, z + d, place(p, z + d), right=False)
+                        to_x(p, z + d, place(p, z + d)).start()
+        for d in range(n):
+            s = lax.rem(z + d, n)
+            for p in every:
+                if via[p] == 0:
+                    to_x(p, s, place(p, s)).wait_recv()
+
+    tok_far.wait_recv()
+    tok_relay.start()
+    tok_near.wait_recv()
+    tok_relay.wait_recv()
+    for copy in (tok_far, tok_near, tok_relay):
+        copy.wait_send()
+    tok_own.wait()
+
+    @pl.when(sec == 0)
+    def _():
+        for array in (0, 1):
+            whole = fulls[array].at[pl.ds(pl.multiple_of(z * rows, 16), rows)]
+            pltpu.make_async_copy(sources[array], whole, own_sem.at[1 + array]).wait()
+
+    for p in every:
+        for d in range(n):
+            s = lax.rem(z + d, n)
+            mine = sec == via[p]
+            if d == 0:
+                sent_x = jnp.logical_or(sec == 0, False)
+            else:
+                sent_x = mine
+
+            @pl.when(sent_x)
+            def _():
+                to_x(p, s, place(p, s)).wait_send()
+
+            @pl.when(mine & (s <= z) & (z < n - 1))
+            def _():
+                to_z(p, s, 1, place(p, s)).wait_send()
+
+            @pl.when(mine & (s >= z) & (z > 0))
+            def _():
+                to_z(p, s, -1, place(p, s)).wait_send()
+
+
+def open_gather(own_in, own_out, xn, group_id):
+    n = lax.axis_size("dp")
+    rows = own_in.shape[0]
+    third = rows // 3
+    pieces = (
+        (0, third, third, 1), (0, 2 * third, third, 1), (0, 0, third, 0),
+        (1, third, 2 * third, 1), (1, 0, third, 0),
+    )
+    count = len(pieces)
+    sem = lambda *shape: pltpu.SemaphoreType.DMA(shape)
+    return pl.pallas_call(
+        functools.partial(open_kernel, n, pieces),
+        out_shape=[
+            jax.ShapeDtypeStruct((n * rows, own_in.shape[1]), BF),
+            jax.ShapeDtypeStruct((n * rows, own_out.shape[1]), BF),
+            jax.ShapeDtypeStruct((lax.axis_size("tensor") * xn.shape[0], xn.shape[1]), BF),
+        ],
+        in_specs=[pl.BlockSpec(memory_space=pltpu.VMEM)] * 3,
+        out_specs=[pl.BlockSpec(memory_space=pl.ANY)] * 3,
+        scratch_shapes=[sem(count, n), sem(count, n), sem(2, count, n), sem(2, count, n), sem(3), sem(3), sem(3)],
+        compiler_params=pltpu.CompilerParams(collective_id=group_id, has_side_effects=True),
+        name="weights_open",
+    )(own_in, own_out, xn)
+
+
+CHUNK_ROWS = 16
+
+
+def by_rows(count, body):
+    @pl.loop(0, count // CHUNK_ROWS)
+    def _(index):
+        body(pl.multiple_of(index * CHUNK_ROWS, CHUNK_ROWS))
+
+
+def finish_kernel(
+    n, shared, g_ref, half_ref, own_ref, send_ref, small_ref,
+    gin_ref, gout_ref, small_x_ref, small_t_ref, bc_ref,
+    x_recv, z_recv, z_send, last_buf, last_recv, join_recv, out_recv,
+    small_recv, small_all, small_ten, bc_own, bc_far, bc_mid, bc_near,
+    x_ss, x_rs, z_ss, z_rs, m_ss, m_rs, d_ss, d_rs, t_ss, t_rs,
+):
+    sec, z, ten = lax.axis_index("section"), lax.axis_index("dp"), lax.axis_index("tensor")
+    half = half_ref.shape[0]
+    rows = 2 * half
+    mine, theirs = sec * half, (1 - sec) * half
+    across = peer("section", 1 - sec)
+    near, far = peer("tensor", ten ^ 1), peer("tensor", ten ^ 2)
+    others = [lax.rem(z + d, n) for d in range(1, n)]
+    mates = [ten ^ d for d in range(1, 4)]
+    greet([across] + [peer("dp", o) for o in others] + [peer("tensor", t) for t in mates])
+    srows = small_recv.shape[0]
+
+    def own_rows(s, offset):
+        return pl.ds(pl.multiple_of(s * rows + offset, 16), half)
+
+    small_x = remote(small_ref.at[pl.ds(pl.multiple_of((1 - sec) * srows, 8), srows)], small_recv,
+                     m_ss.at[0], m_rs.at[0], across)
+    small_x.start()
+    order = [i // 2 if i % 2 else n - 1 - i // 2 for i in range(n)]
+    x_copies = {}
+    for s in order:
+        x_copies[s] = remote(g_ref.at[own_rows(s, theirs)], x_recv.at[s], x_ss.at[s], x_rs.at[s], across)
+        x_copies[s].start()
+    join = remote(half_ref, join_recv, m_ss.at[1], m_rs.at[1], across)
+    last = remote(last_buf, last_recv, m_ss.at[2], m_rs.at[2], across)
+    out_copy = remote(send_ref, out_recv, m_ss.at[3], m_rs.at[3], across)
+    out_copy.start()
+
+    @pl.when(sec == 0)
+    def _():
+        join.start()
+
+    small_x.wait_recv()
+    small_all[z] = small_ref[pl.ds(pl.multiple_of(sec * srows, 8), srows), :] + small_recv[...]
+    to_dp = [remote(small_all.at[z], small_all.at[z], d_ss.at[d], d_rs.at[z], peer("dp", o)) for d, o in enumerate(others)]
+    for copy in to_dp:
+        copy.start()
+
+    def z_copy(s):
+        right = s > z
+        side = jnp.where(right, 0, 1)
+        down = z + jnp.where(right, 1, -1)
+        return remote(z_send.at[s], z_recv.at[side, s], z_ss.at[s], z_rs.at[side, s], peer("dp", down))
+
+    def arrived(side, s):
+        remote(z_send.at[0], z_recv.at[side, s], z_ss.at[0], z_rs.at[side, s], across).wait_recv()
+
+    for s in order:
+        x_copies[s].wait_recv()
+
+        @pl.when(s != z)
+        def _():
+            right = s > z
+            side = jnp.where(right, 0, 1)
+            upstream = jnp.where(right, z > 0, z < n - 1)
+
+            @pl.when(upstream)
+            def _():
+                arrived(side, s)
+
+                def body(r):
+                    z_send[s, pl.ds(r, CHUNK_ROWS), :] = (
+                        g_ref[pl.ds(pl.multiple_of(s * rows + mine + r, 16), CHUNK_ROWS), :].astype(F32)
+                        + x_recv[s, pl.ds(r, CHUNK_ROWS), :].astype(F32)
+                        + z_recv[side, s, pl.ds(r, CHUNK_ROWS), :].astype(F32)
+                    ).astype(BF)
+
+                by_rows(half, body)
+
+            @pl.when(jnp.logical_not(upstream))
+            def _():
+                def body(r):
+                    z_send[s, pl.ds(r, CHUNK_ROWS), :] = (
+                        g_ref[pl.ds(pl.multiple_of(s * rows + mine + r, 16), CHUNK_ROWS), :].astype(F32)
+                        + x_recv[s, pl.ds(r, CHUNK_ROWS), :].astype(F32)
+                    ).astype(BF)
+
+                by_rows(half, body)
+
+            z_copy(s).start()
+
+    for d, o in enumerate(others):
+        remote(small_all.at[o], small_all.at[o], d_ss.at[d], d_rs.at[o], across).wait_recv()
+    total = small_all[0]
+    for k in range(1, n):
+        total = total + small_all[k]
+    small_x_ref[...] = total
+    small_ten[ten] = total
+    to_ten = [remote(small_ten.at[ten], small_ten.at[ten], t_ss.at[d], t_rs.at[ten], peer("tensor", t)) for d, t in enumerate(mates)]
+    for copy in to_ten:
+        copy.start()
+
+    out_copy.wait_recv()
+
+    def put_out(r):
+        gout_ref[pl.ds(pl.multiple_of(mine + r, 16), CHUNK_ROWS), :] = own_ref[pl.ds(r, CHUNK_ROWS), :].astype(F32)
+        gout_ref[pl.ds(pl.multiple_of(theirs + r, 16), CHUNK_ROWS), :] = out_recv[pl.ds(r, CHUNK_ROWS), :].astype(F32)
+
+    by_rows(half, put_out)
+
+    def base(r):
+        gin_ref[pl.ds(r, CHUNK_ROWS), :] = (
+            g_ref[pl.ds(pl.multiple_of(z * rows + mine + r, 16), CHUNK_ROWS), :].astype(F32)
+            + x_recv[z, pl.ds(r, CHUNK_ROWS), :].astype(F32)
+        )
+
+    by_rows(half, base)
+    for side, there in ((0, z > 0), (1, z < n - 1)):
+
+        @pl.when(there)
+        def _():
+            arrived(side, z)
+
+            def more(r):
+                gin_ref[pl.ds(r, CHUNK_ROWS), :] += z_recv[side, z, pl.ds(r, CHUNK_ROWS), :].astype(F32)
+
+            by_rows(half, more)
+
+    @pl.when(sec == 1)
+    def _():
+        def out(r):
+            last_buf[pl.ds(r, CHUNK_ROWS), :] = gin_ref[pl.ds(r, CHUNK_ROWS), :].astype(BF)
+
+        by_rows(half, out)
+        last.start()
+        join.wait_recv()
+
+        def put(r):
+            gin_ref[pl.ds(r, CHUNK_ROWS), :] = join_recv[pl.ds(r, CHUNK_ROWS), :].astype(F32)
+            gin_ref[pl.ds(pl.multiple_of(half + r, 16), CHUNK_ROWS), :] = half_ref[pl.ds(r, CHUNK_ROWS), :].astype(F32)
+
+        by_rows(half, put)
+        last.wait_send()
+
+    @pl.when(sec == 0)
+    def _():
+        last.wait_recv()
+
+        def put(r):
+            gin_ref[pl.ds(pl.multiple_of(half + r, 16), CHUNK_ROWS), :] = last_recv[pl.ds(r, CHUNK_ROWS), :].astype(F32)
+
+        by_rows(half, put)
+        join.wait_send()
+
+    bc_own[...] = gin_ref[:, shared : shared + 2 * NS].astype(BF)
+    to_far = remote(bc_own, bc_far, t_ss.at[3], t_rs.at[4], far)
+    to_far.start()
+    for d, t in enumerate(mates):
+        remote(small_ten.at[t], small_ten.at[t], t_ss.at[d], t_rs.at[t], near).wait_recv()
+    total = small_ten[0]
+    for k in range(1, 4):
+        total = total + small_ten[k]
+    small_t_ref[...] = total
+    to_far.wait_recv()
+    bc_mid[...] = (bc_own[...].astype(F32) + bc_far[...].astype(F32)).astype(BF)
+    to_near = remote(bc_mid, bc_near, t_ss.at[4], t_rs.at[5], near)
+    to_near.start()
+    to_near.wait_recv()
+    bc_ref[...] = bc_mid[...].astype(F32) + bc_near[...].astype(F32)
+    for s in order:
+        x_copies[s].wait_send()
+
+        @pl.when(s != z)
+        def _():
+            z_copy(s).wait_send()
+
+    for copy in [small_x, out_copy, to_far, to_near] + to_dp + to_ten:
+        copy.wait_send()
+
+
+def finish(grads, half_other, out_own, out_send, smalls, shared, group_id):
+    n = lax.axis_size("dp")
+    half, wide = half_other.shape
+    owide = out_own.shape[1]
+    srows, swide = smalls.shape[0] // 2, smalls.shape[1]
+    vm = lambda shape, dtype: pltpu.VMEM(shape, dtype)
+    sem = lambda *shape: pltpu.SemaphoreType.DMA(shape)
+    return pl.pallas_call(
+        functools.partial(finish_kernel, n, shared),
+        out_shape=[
+            jax.ShapeDtypeStruct((2 * half, wide), F32),
+            jax.ShapeDtypeStruct((2 * half, owide), F32),
+            jax.ShapeDtypeStruct((srows, swide), F32),
+            jax.ShapeDtypeStruct((srows, swide), F32),
+            jax.ShapeDtypeStruct((2 * half, 2 * NS), F32),
+        ],
+        in_specs=[pl.BlockSpec(memory_space=pltpu.VMEM)] * 5,
+        out_specs=[pl.BlockSpec(memory_space=pltpu.VMEM)] * 5,
+        scratch_shapes=[
+            vm((n, half, wide), BF), vm((2, n, half, wide), BF), vm((n, half, wide), BF),
+            vm((half, wide), BF), vm((half, wide), BF), vm((half, wide), BF), vm((half, owide), BF),
+            vm((srows, swide), F32), vm((n, srows, swide), F32), vm((4, srows, swide), F32),
+            vm((2 * half, 2 * NS), BF), vm((2 * half, 2 * NS), BF), vm((2 * half, 2 * NS), BF), vm((2 * half, 2 * NS), BF),
+            sem(n), sem(n), sem(n), sem(2, n), sem(4), sem(4), sem(n), sem(n), sem(5), sem(6),
+        ],
+        compiler_params=pltpu.CompilerParams(collective_id=group_id, has_side_effects=True, vmem_limit_bytes=60 << 20),
+        name="grad_finish",
+    )(grads, half_other, out_own, out_send, smalls)
+
+
 EPSILON = 1e-05
 HEAD_PAD = 128
+SMALL_ROWS = 16
 
 
 def swap_sections(value):
@@ -262,38 +864,16 @@
     return lax.ppermute(value, "section", [(i, (i + 1) % count) for i in range(count)])
 
 
-def token_gather(value):
-    return lax.all_gather(value, "tensor", axis=0, tiled=True)
-
-
-def token_scatter(value):
-    return lax.psum_scatter(value, "tensor", scatter_dimension=0, tiled=True)
-
-
-def weight_gather(own, is_first):
+def later_gather(own, is_first, after):
     half = own.shape[0] // 2
     low, high = own[:half], own[half:]
-    got = swap_sections(jnp.where(is_first, high, low))
-    first_piece = jnp.where(is_first, low, got)
-    second_piece = jnp.where(is_first, got, high)
-    return tuple(
-        lax.all_gather(piece, ("dp", "section"), axis=0, tiled=True)
-        for piece in (first_piece, second_piece)
-    )
+    got = lax.ppermute(low, "section", [(1, 0)])
+    piece, after = lax.optimization_barrier((jnp.where(is_first, got, high), after))
+    return lax.all_gather(piece, ("dp", "section"), axis=0, tiled=True), after
 
 
 def grad_scatter(value):
-    return lax.psum_scatter(
-        value.astype(BF), ("dp", "section"), scatter_dimension=0, tiled=True
-    )
-
-
-def join_halves(first_part, second_part, is_first):
-    own = jnp.where(is_first, first_part, second_part)
-    got = swap_sections(jnp.where(is_first, second_part, first_part))
-    low = jnp.where(is_first, own, got)
-    high = jnp.where(is_first, got, own)
-    return jnp.concatenate([low, high], axis=0).astype(F32)
+    return lax.psum_scatter(value, ("dp", "section"), scatter_dimension=0, tiled=True)
 
 
 def local(
@@ -309,7 +889,6 @@
     shard = in_zx.shape[1]
     total_inner = width * lax.axis_size("tensor")
     wide = width + 2 * NS
-    row_start = lax.axis_index("tensor") * rows
 
     def padded(value):
         return jnp.pad(value, (0, wide - value.shape[0]))[None]
@@ -341,35 +920,36 @@
         axis=1,
     )
     own_out = out_proj[0].T
-    w_in = weight_gather(own_in, is_first)
-    w_out = weight_gather(own_out, is_first)
 
     head_of = jnp.arange(width) // (width // heads)
     spread = (jnp.arange(2 * HEAD_PAD)[:, None] % HEAD_PAD == head_of[None, :]).astype(BF)
     gather = (head_of[:, None] == jnp.arange(HEAD_PAD)[None, :]).astype(BF)
 
-    def forward(layer, u):
+    def normed(layer, u):
         inv = lax.rsqrt(jnp.mean(u * u, axis=1, keepdims=True) + EPSILON)
-        xn = token_gather((u * inv * gains[layer][None, :]).astype(BF))
-        pre = dot(xn, w_in[layer])
+        return inv, (u * inv * gains[layer][None, :]).astype(BF)
+
+    def forward(layer, u, inv, xn, w_in, w_out):
+        pre = dot(xn, w_in)
         yn, squares, states = mixer_fwd(pre, pars[layer], spread, width)
-        partial = dot_nt(yn, w_out[layer])
-        total = token_scatter(partial)
-        squares = lax.dynamic_slice_in_dim(lax.psum(squares[:, 0], "tensor"), row_start, rows)
-        q = lax.rsqrt(squares / total_inner + EPSILON)[:, None]
+        partial = dot_nt(yn, w_out).astype(BF)
+        total, squares = token_scatter(partial, 3 + layer, squares)
+        q = lax.rsqrt(squares[::8].reshape(rows) / total_inner + EPSILON)[:, None]
         projected = total * q
-        return (u + projected).astype(BF), (u, inv, xn, pre, yn, states, q, projected)
+        return (u + projected).astype(BF), (u, inv, xn, pre, yn, states, q, projected, w_in, w_out)
 
     def backward(layer, g, kept):
-        u, inv, xn, pre, yn, states, q, projected = kept
-        gq = token_gather((g * q).astype(BF))
+        u, inv, xn, pre, yn, states, q, projected, w_in, w_out = kept
         kappa = q * q / total_inner * jnp.sum(g * projected, axis=1, keepdims=True)
-        kappa = token_gather(kappa)
-        dh = dot(gq, w_out[layer])
-        gp, acc = mixer_bwd(pre, pars[layer], spread, gather, states, dh, kappa, width, heads)
-        dxn = token_scatter(dot_nt(gp, w_in[layer]))
-        g_in = dot_tn(xn, gp)
-        g_out = dot_tn(gq, yn)
+        high = kappa.astype(BF)
+        low = (kappa - high.astype(F32)).astype(BF)
+        side = jnp.pad(jnp.concatenate([high, low], axis=1), ((0, 0), (0, 126)))
+        gq, side = token_gather([(g * q).astype(BF), side], 5 + layer)
+        dh = dot(gq, w_out)
+        gp, acc = mixer_bwd(pre, pars[layer], spread, gather, states, dh, side, width, heads)
+        g_out = dot_tn(gq, yn).astype(BF)
+        g_in = dot_tn(xn, gp).astype(BF)
+        (dxn,) = token_scatter(dot_nt(gp, w_in).astype(BF), 7 + layer)
         scaled = dxn * gains[layer][None, :]
         dots = jnp.sum(scaled * u, axis=1, keepdims=True)
         du = g + inv * scaled - u * (inv * inv * inv) * dots / model
@@ -377,17 +957,22 @@
         return du.astype(BF), g_in, g_out, acc, g_gain
 
     u0 = lax.dynamic_index_in_dim(stream[:, 0], section, 0, False).astype(F32)
-    out0, kept0 = forward(0, u0)
-    out1, kept1 = forward(1, out0.astype(F32))
+    inv0, xn0 = normed(0, u0)
+    w_in0, w_out0, xn0 = open_gather(own_in, own_out, xn0, 1)
+    full_in1, w_in0 = later_gather(own_in, is_first, w_in0)
+    full_out1, w_in0 = later_gather(own_out, is_first, w_in0)
+
+    out0, kept0 = forward(0, u0, inv0, xn0, w_in0, w_out0)
+    u1 = out0.astype(F32)
+    inv1, xn1 = normed(1, u1)
+    (xn1,) = token_gather([xn1], 2)
+    out1, kept1 = forward(1, u1, inv1, xn1, full_in1, full_out1)
     g1 = lax.dynamic_index_in_dim(cotangent[:, 0], section, 0, False).astype(F32)
     du1, g_in1, g_out1, acc1, gain1 = backward(1, g1, kept1)
+    half_out1 = grad_scatter(g_out1)
     half_in1 = grad_scatter(g_in1)
-    half_out1 = grad_scatter(g_out1)
     du0, g_in0, g_out0, acc0, gain0 = backward(0, du1.astype(F32), kept0)
-    half_in0 = grad_scatter(g_in0)
     half_out0 = grad_scatter(g_out0)
-    g_in = join_halves(half_in0, half_in1, is_first)
-    g_out = join_halves(half_out0, half_out1, is_first)
 
     def by_batch(first_value, second_value):
         own = jnp.where(is_first, first_value, second_value)
@@ -397,26 +982,31 @@
 
     def minor(acc, gain):
         return jnp.concatenate(
-            [acc, jnp.pad(gain, (0, gain_rows * wide - model)).reshape(gain_rows, wide)], axis=0
+            [
+                acc,
+                jnp.pad(gain, (0, gain_rows * wide - model)).reshape(gain_rows, wide),
+                jnp.zeros((SMALL_ROWS - 8 - gain_rows, wide), F32),
+            ],
+            axis=0,
         )
 
-    both = lax.psum(jnp.stack([minor(acc0, gain0), minor(acc1, gain1)]), ("dp", "section"))
-    mine = jnp.where(is_first, both[0], both[1])
-    shared_bc, shared_gain, bc_rows = lax.psum(
-        (mine[0:5, width:], mine[8:], g_in[:, 2 * width : 2 * width + 2 * NS]), "tensor"
+    smalls = jnp.concatenate([minor(acc0, gain0), minor(acc1, gain1)])
+    g_in, g_out, mine, shared, bc_rows = finish(
+        g_in0, half_in1, jnp.where(is_first, half_out0, half_out1),
+        jnp.where(is_first, half_out1, half_out0), smalls, 2 * width, 9,
     )
     return (
         by_batch(out0, out1),
         by_batch(du0, du1),
-        shared_gain.reshape(-1)[:model][None],
+        shared[8 : 8 + gain_rows].reshape(-1)[:model][None],
         g_in[:, : 2 * width].reshape(shard, 2, width)[None],
         g_in[:, 2 * width + 2 * NS : 2 * width + 2 * NS + heads][None],
         bc_rows[None],
         g_out.T[None],
         mine[0:4, :width][None],
         mine[4, :width][None],
-        shared_bc[0:4][None],
-        shared_bc[4][None],
+        shared[0:4, width:][None],
+        shared[4, width:][None],
         mine[7, :heads][None],
         mine[7, HEAD_PAD : HEAD_PAD + heads][None],
         mine[6, :width].reshape(heads, -1).sum(axis=1)[None],

time: 1260 us -> 820 us (0.65)
  waiting for transfers between devices: 905 us -> 103 us
  Pallas kernels: 109 us -> 527 us
  blocking collectives: 37.4 us -> 0 us
    pallas_call x0 -> x9, Pallas kernels: none -> 415 us  [the longest x1 129 us: open_gather(): pl.pallas_call(functools.partial(open_kernel, n, pieces), out_shape=[jax....]
    reduce_scatter x8 -> x3, waiting for transfers between devices: 447 us -> 54.5 us  [grad_scatter(): lax.psum_scatter(value, ('dp', 'section'), scatter_dimension=0, tiled=True)]
    all_gather x8 -> x2, waiting for transfers between devices: 318 us -> 27.5 us  [later_gather(): return (lax.all_gather(piece, ('dp', 'section'), axis=0, tiled=True), after)]
    psum x2 -> x0, waiting for transfers between devices: 81.2 us -> none  [the longest x1 64.5 us: local(): lax.psum(jnp.stack([minor(acc0, gain0), minor(acc1, gain1)]), ('dp', 'sec...]
    ppermute x7 -> x3, waiting for transfers between devices: 56.5 us -> 13.1 us  [swap_sections(): lax.ppermute(value, 'section', [(i, (i + 1) % count) for i in range(count)])]
    psum x3 -> x0, blocking collectives: 25.9 us -> none  [the longest x2 13.7 us: forward(): lax.psum(squares[:, 0], 'tensor')]
  transfers between devices with their start and end apart: 25 -> 10, of which waited for: 22 -> 5; matrix products, arithmetic and copies ran while one was open for 9% -> 14% of each run, Pallas kernels for 5% -> 43%
where the time goes in v2:
time: 820 us; the launch traced here: 815 us
  Pallas kernels  527 us (64%)
  waiting for transfers between devices  103 us (13%)
  matrix products  98 us (12%)
  local copies, waits for them, and re-layouts  35.1 us (4%)
  other arithmetic  31.3 us (4%)
  between operations  14.7 us (2%)
    pallas_call x1, Pallas kernels, open_gather(): pl.pallas_call(functools.partial(open_kernel, n, pieces), out_shape=[jax....  129 us
    pallas_call x1, Pallas kernels, finish(): pl.pallas_call(functools.partial(finish_kernel, n, shared), out_shape=[ja...  125 us
    pallas_call x4, Pallas kernels, token_scatter(): pl.pallas_call(functools.partial(token_scatter_kernel, side is not None),...  89.9 us
    pallas_call x2, Pallas kernels, mixer_bwd(): pl.pallas_call(functools.partial(bwd_kernel, width, n_heads), grid=(n,),...  84.5 us
    pallas_call x3, Pallas kernels, token_gather(): pl.pallas_call(functools.partial(token_gather_kernel, count), out_shape=[...  70.7 us
    reduce_scatter x3, waiting for transfers between devices, grad_scatter(): lax.psum_scatter(value, ('dp', 'section'), scatter_dimension=0, tiled=True)  54.5 us
    dot_general x4, matrix products, dot(): return jnp.dot(a, b, preferred_element_type=F32)  37.7 us
    dot_general x4, matrix products, dot_tn(): lax.dot_general(a, b, (((0,), (0,)), ((), ())), preferred_element_type=F32)  32.3 us
  transfers between devices with their start and end apart: 10, of which 5 were waited for; matrix products, arithmetic and copies ran while one was open for 14% of the time, Pallas kernels for 43%

profile of v2, /device:TPU:9, one launch (start us, length us, event | category | flops | bytes accessed | tf_op | source)
XLA Modules:
  0.0 814.8 jit_solution(17936004876292877028)
XLA Ops:
  22.7 129.3 %weights_open.1 = (bf16[1536,1920]{1,0:T(8,128)(2,1)}, bf16[1536,768]{1,0:T(8,128)(2,1)}, bf16[1024,1536]{1,0:T(8,128)(2,1)}) custom-call(bf16[384,1920]{1,0:T(8,128)(2,1)} %copy-done.13, bf16[384,768]{1,0:T(8,128)(2,1)} %bitcast.112, bf16[256,1536]{1,0:T(8,128)(2,1)} %fusion.20.xn_ref), custom_call_target="tpu_custom_call" | custom-call | tf_op jit(solution)/shard_map/weights_open/pallas_call | solution.py:627
  156.6 8.0 collective-permute-done.1
  165.7 11.9 %fusion.39.pre_ref.halo_ref = f32[1024,1920]{1,0:T(8,128)} fusion(bf16[1024,1536]{1,0:T(8,128)(2,1)} %get-tuple-element.45, bf16[1536,1920]{1,0:T(8,128)(2,1)} %get-tuple-element.48), kind=kOutput, calls=%fused_computation.112 | convolution fusion | flops 6039797760 | bytes 16908288 | tf_op jit(solution)/shard_map/dot_general | solution.py:12
  177.6 13.2 %mixer_fwd.2 = (bf16[1024,768]{1,0:T(8,128)(2,1)S(1)}, f32[64,128]{1,0:T(8,128)S(1)}, f32[8,128,768]{2,1,0:T(8,128)S(1)}) custom-call(f32[1024,1920]{1,0:T(8,128)} %fusion.39.pre_ref.halo_ref, f32[16,1024]{1,0:T(8,128)S(1)} %get-tuple-element.139.par_ref, bf16[256,768]{1,0:T(8,128)(2,1)S(1)} %compare_convert_fusion.spread_ref), custom_call_target="tpu_custom_call" | custom-call | tf_op jit(solution)/shard_map/mixer_fwd/pallas_call | solution.py:89
  193.8 23.0 %token_scatter.4 = (f32[256,1536]{1,0:T(8,128)S(1)}, f32[16,128]{1,0:T(8,128)S(1)}) custom-call(bf16[1024,1536]{1,0:T(8,128)(2,1)S(1)} %convolution_convert_fusion.5.refs_0_, f32[64,128]{1,0:T(8,128)S(1)} %get-tuple-element.51.refs_1_), custom_call_target="tpu_custom_call" | custom-call | tf_op jit(solution)/shard_map/token_scatter/pallas_call | solution.py:449
  219.7 22.9 %token_gather.3 = bf16[1024,1536]{1,0:T(8,128)(2,1)} custom-call(bf16[256,1536]{1,0:T(8,128)(2,1)} %fusion.11.refs_0_), custom_call_target="tpu_custom_call" | custom-call | tf_op jit(solution)/shard_map/token_gather/pallas_call | solution.py:336
  245.3 11.9 %fusion.40.pre_ref.halo_ref = f32[1024,1920]{1,0:T(8,128)} fusion(bf16[1024,1536]{1,0:T(8,128)(2,1)} %token_gather.3, bf16[1536,1920]{1,0:T(8,128)(2,1)} %all-gather.3.cloned.1.call-done), kind=kOutput, calls=%fused_computation.113 | convolution fusion | flops 6039797760 | bytes 16908288 | tf_op jit(solution)/shard_map/dot_general | solution.py:12
  257.2 13.7 %mixer_fwd.3 = (bf16[1024,768]{1,0:T(8,128)(2,1)S(1)}, f32[64,128]{1,0:T(8,128)S(1)}, f32[8,128,768]{2,1,0:T(8,128)S(1)}) custom-call(f32[1024,1920]{1,0:T(8,128)} %fusion.40.pre_ref.halo_ref, f32[16,1024]{1,0:T(8,128)S(1)} %get-tuple-element.138.par_ref, bf16[256,768]{1,0:T(8,128)(2,1)S(1)} %compare_convert_fusion.spread_ref), custom_call_target="tpu_custom_call" | custom-call | tf_op jit(solution)/shard_map/mixer_fwd/pallas_call | solution.py:89
  274.3 24.8 %all-gather.5.cloned.1.call-done = bf16[1536,768]{1,0:T(8,128)(2,1)} async-done(((bf16[192,768]{1,0:T(8,128)(2,1)}), bf16[1536,768]{1,0:T(8,128)(2,1)}) %all-gather.5.cloned.1.call-update) | async-done | bytes 2359312 | tf_op jit(solution)/shard_map/all_gather | solution.py:872
  303.9 23.8 %token_scatter.5 = (f32[256,1536]{1,0:T(8,128)S(1)}, f32[16,128]{1,0:T(8,128)S(1)}) custom-call(bf16[1024,1536]{1,0:T(8,128)(2,1)S(1)} %convolution_convert_fusion.4.refs_0_, f32[64,128]{1,0:T(8,128)S(1)} %copy-done.6), custom_call_target="tpu_custom_call" | custom-call | tf_op jit(solution)/shard_map/token_scatter/pallas_call | solution.py:449
  330.9 23.9 %token_gather.4 = (bf16[1024,1536]{1,0:T(8,128)(2,1)}, bf16[1024,128]{1,0:T(8,128)(2,1)}) custom-call(bf16[256,1536]{1,0:T(8,128)(2,1)} %get-tuple-element.135.refs_0_, bf16[256,128]{1,0:T(8,128)(2,1)} %pad.41.refs_1_), custom_call_target="tpu_custom_call" | custom-call | tf_op jit(solution)/shard_map/token_gather/pallas_call | solution.py:336
  361.3 7.0 fusion.41.dh_ref
  368.3 42.4 %mixer_bwd.2 = (bf16[1024,1920]{1,0:T(8,128)(2,1)}, f32[8,1024]{1,0:T(8,128)}) custom-call(f32[1024,1920]{1,0:T(8,128)} %fusion.40.pre_ref.halo_ref, f32[1024,1920]{1,0:T(8,128)} %fusion.40.pre_ref.halo_ref, f32[16,1024]{1,0:T(8,128)} %copy-done.4, bf16[256,768]{1,0:T(8,128)(2,1)} %copy-done, bf16[768,128]{1,0:T(8,128)(2,1)} %fusion.28.gather_ref, ...), custom_call_target="tpu_custom_call" | custom-call | tf_op jit(solution)/shard_map/mixer_bwd/pallas_call | solution.py:237
  410.6 9.9 %convolution_convert_fusion.3.refs_0_ = bf16[1024,1536]{1,0:T(8,128)(2,1)S(1)} fusion(bf16[1024,1920]{1,0:T(8,128)(2,1)} %get-tuple-element.63, bf16[1536,1920]{1,0:T(8,128)(2,1)} %all-gather.3.cloned.1.call-done), kind=kOutput, calls=%fused_computation.3 | convolution fusion | flops 6041370624 | bytes 12976128 | tf_op jit(solution)/shard_map/dot_general | solution.py:13
  420.6 21.3 %token_scatter.6 = f32[256,1536]{1,0:T(8,128)S(1)} custom-call(bf16[1024,1536]{1,0:T(8,128)(2,1)S(1)} %convolution_convert_fusion.3.refs_0_), custom_call_target="tpu_custom_call" | custom-call | tf_op jit(solution)/shard_map/token_scatter/pallas_call | solution.py:449
  448.0 23.9 %token_gather.5 = (bf16[1024,1536]{1,0:T(8,128)(2,1)}, bf16[1024,128]{1,0:T(8,128)(2,1)}) custom-call(bf16[256,1536]{1,0:T(8,128)(2,1)} %fusion.1.refs_0_, bf16[256,128]{1,0:T(8,128)(2,1)} %pad.42.refs_1_), custom_call_target="tpu_custom_call" | custom-call | tf_op jit(solution)/shard_map/token_gather/pallas_call | solution.py:336
  477.9 11.4 %convolution_convert_fusion = bf16[1536,1920]{1,0:T(8,128)(2,1)} fusion(bf16[1024,1536]{1,0:T(8,128)(2,1)} %token_gather.3, bf16[1024,1920]{1,0:T(8,128)(2,1)} %get-tuple-element.63), kind=kOutput, calls=%fused_computation | convolution fusion | flops 6042746880 | bytes 12976128 | tf_op jit(solution)/shard_map/dot_general | solution.py:14
  498.9 42.2 %mixer_bwd.3 = (bf16[1024,1920]{1,0:T(8,128)(2,1)}, f32[8,1024]{1,0:T(8,128)}) custom-call(f32[1024,1920]{1,0:T(8,128)} %fusion.39.pre_ref.halo_ref, f32[1024,1920]{1,0:T(8,128)} %fusion.39.pre_ref.halo_ref, f32[16,1024]{1,0:T(8,128)} %copy-done.3, bf16[256,768]{1,0:T(8,128)(2,1)} %copy-done, bf16[768,128]{1,0:T(8,128)(2,1)} %fusion.28.gather_ref, ...), custom_call_target="tpu_custom_call" | custom-call | tf_op jit(solution)/shard_map/mixer_bwd/pallas_call | solution.py:237
  541.1 10.4 %convolution_convert_fusion.2.refs_0_ = bf16[1024,1536]{1,0:T(8,128)(2,1)S(1)} fusion(bf16[1024,1920]{1,0:T(8,128)(2,1)} %get-tuple-element.67, bf16[1536,1920]{1,0:T(8,128)(2,1)} %get-tuple-element.48), kind=kOutput, calls=%fused_computation.2 | convolution fusion | flops 6041370624 | bytes 12976128 | tf_op jit(solution)/shard_map/dot_general | solution.py:13
  551.5 21.9 %token_scatter.7 = f32[256,1536]{1,0:T(8,128)S(1)} custom-call(bf16[1024,1536]{1,0:T(8,128)(2,1)S(1)} %convolution_convert_fusion.2.refs_0_), custom_call_target="tpu_custom_call" | custom-call | tf_op jit(solution)/shard_map/token_scatter/pallas_call | solution.py:449
  573.4 8.4 %convolution_convert_fusion.1.g_ref = bf16[1536,1920]{1,0:T(8,128)(2,1)} fusion(bf16[1024,1536]{1,0:T(8,128)(2,1)S(1)} %copy-done.27, bf16[1024,1920]{1,0:T(8,128)(2,1)S(1)} %copy-done.26), kind=kOutput, calls=%fused_computation.1 | convolution fusion | flops 6042746880 | bytes 12976128 | tf_op jit(solution)/shard_map/dot_general | solution.py:14
  593.2 13.1 %collective-permute-done.4 = bf16[256,1536]{1,0:T(8,128)(2,1)S(1)} collective-permute-done((bf16[256,1536]{1,0:T(8,128)(2,1)}, bf16[256,1536]{1,0:T(8,128)(2,1)S(1)}, u32[]{:S(2)}, u32[]{:S(2)}) %collective-permute-start.4) | collective-permute-done | bytes 786464 | tf_op jit(solution)/shard_map/ppermute | solution.py:864
  609.7 54.5 %reduce-scatter.4.cloned.1.call-done.half_ref = bf16[192,1920]{1,0:T(8,128)(2,1)} async-done(((bf16[1536,1920]{1,0:T(8,128)(2,1)}), bf16[192,1920]{1,0:T(8,128)(2,1)}) %reduce-scatter.4.cloned.1.call-update) | async-done | bytes 737296 | tf_op jit(solution)/shard_map/reduce_scatter | solution.py:876
  664.2 125.3 %grad_finish.1 = (f32[384,1920]{1,0:T(8,128)}, f32[384,768]{1,0:T(8,128)}, f32[16,1024]{1,0:T(8,128)}, f32[16,1024]{1,0:T(8,128)}, f32[384,256]{1,0:T(8,128)}) custom-call(bf16[1536,1920]{1,0:T(8,128)(2,1)} %convolution_convert_fusion.1.g_ref, bf16[192,1920]{1,0:T(8,128)(2,1)} %reduce-scatter.4.cloned.1.call-done.half_ref, ...), custom_call_target="tpu_custom_call" | custom-call | tf_op jit(solution)/shard_map/grad_finish/pallas_call | solution.py:834
  (167 shorter events, 102.2 us)
Async XLA Ops:
  7.2 9.4 %copy-start.23 = (bf16[1,384,256]{2,1,0:T(8,128)(2,1)S(1)}, bf16[1,384,256]{2,1,0:T(8,128)(2,1)}, u32[]{:S(2)}) copy-start(bf16[1,384,256]{2,1,0:T(8,128)(2,1)} %param.20) | copy-start | bytes 589828
  7.2 238.1 %all-gather.3.cloned.1.call-start = ((), (), s32[]{:S(2)}) async-start(), calls=%async_computation.3 | async-start | bytes 6635520 | tf_op jit(solution)/shard_map/all_gather | solution.py:872
  13.1 8.5 %collective-permute-start = (f32[16,1024]{1,0:T(8,128)S(1)}, f32[16,1024]{1,0:T(8,128)S(1)}, u32[]{:S(2)}, u32[]{:S(2)}) collective-permute-start(f32[16,1024]{1,0:T(8,128)S(1)} %concatenate.24), channel_id=1, source_target_pairs={{0,16},{16,0},{1,17},{17,1},{2,18},{18,2},{3,19},{19,3},{4,20},{20... | collective-permute-start | bytes 196616 | tf_op jit(solution)/shard_map/ppermute | solution.py:864
  17.7 134.3 %collective-permute-start.2 = (bf16[192,1920]{1,0:T(8,128)(2,1)}, bf16[192,1920]{1,0:T(8,128)(2,1)}, u32[]{:S(2)}, u32[]{:S(2)}) collective-permute-start(bf16[192,1920]{1,0:T(8,128)(2,1)} %slice.92), channel_id=1, source_target_pairs={{16,0},{17,1},{18,2},{19,3},{20,4},{21,5},{22,6},{23,7},{24,8},{25... | collective-permute-start | bytes 2211848 | tf_op jit(solution)/shard_map/ppermute | solution.py:870
  21.5 156.1 %copy-start.3 = (f32[16,1024]{1,0:T(8,128)}, f32[16,1024]{1,0:T(8,128)S(1)}, u32[]{:S(2)}) copy-start(f32[16,1024]{1,0:T(8,128)S(1)} %get-tuple-element.139.par_ref) | copy-start | bytes 196612
  21.5 235.6 %copy-start.4 = (f32[16,1024]{1,0:T(8,128)}, f32[16,1024]{1,0:T(8,128)S(1)}, u32[]{:S(2)}) copy-start(f32[16,1024]{1,0:T(8,128)S(1)} %get-tuple-element.138.par_ref) | copy-start | bytes 196612
  22.7 129.3 %copy-start.14 = (bf16[384,1920]{1,0:T(8,128)(2,1)S(1)}, bf16[384,1920]{1,0:T(8,128)(2,1)}, u32[]{:S(2)}) copy-start(bf16[384,1920]{1,0:T(8,128)(2,1)} %copy-done.13) | copy-start | bytes 4423684
  154.2 144.9 %all-gather.5.cloned.1.call-start = ((), (), s32[]{:S(2)}) async-start(), calls=%async_computation.4 | async-start | bytes 2654208 | tf_op jit(solution)/shard_map/all_gather | solution.py:872
  154.2 10.3 %collective-permute-start.1 = (bf16[192,768]{1,0:T(8,128)(2,1)S(1)}, bf16[192,768]{1,0:T(8,128)(2,1)S(1)}, u32[]{:S(2)}, u32[]{:S(2)}) collective-permute-start(bf16[192,768]{1,0:T(8,128)(2,1)S(1)} %slice.90), channel_id=1, source_target_pairs={{16,0},{17,1},{18,2},{19,3},{20,4},{21,5},{22,6},{23,7},{24,8},{25... | collective-permute-start | bytes 884744 | tf_op jit(solution)/shard_map/ppermute | solution.py:870
  156.6 100.6 %copy-start = (bf16[256,768]{1,0:T(8,128)(2,1)}, bf16[256,768]{1,0:T(8,128)(2,1)S(1)}, u32[]{:S(2)}) copy-start(bf16[256,768]{1,0:T(8,128)(2,1)S(1)} %compare_convert_fusion.spread_ref) | copy-start | bytes 1179652
  165.4 442.5 %reduce-scatter.8.cloned.1.call-start = ((), (), s32[]{:S(2)}) async-start(), calls=%async_computation.7 | async-start | bytes 2654208 | tf_op jit(solution)/shard_map/reduce_scatter | solution.py:876
  177.6 13.3 %copy-start.28 = (bf16[1536,768]{1,0:T(8,128)(2,1)S(1)}, bf16[1536,768]{1,0:T(8,128)(2,1)}, u32[]{:S(2)}) copy-start(bf16[1536,768]{1,0:T(8,128)(2,1)} %get-tuple-element.50) | copy-start | bytes 7077892
  218.5 24.1 %copy-start.10 = (bf16[256,1536]{1,0:T(8,128)(2,1)}, bf16[256,1536]{1,0:T(8,128)(2,1)S(1)}, u32[]{:S(2)}) copy-start(bf16[256,1536]{1,0:T(8,128)(2,1)S(1)} %get-tuple-element.129) | copy-start | bytes 2359300
  361.3 246.6 %reduce-scatter.6.cloned.1.call-start = ((), (), s32[]{:S(2)}) async-start(), calls=%async_computation.6 | async-start | bytes 2654208 | tf_op jit(solution)/shard_map/reduce_scatter | solution.py:876
  420.6 21.3 %copy-start.11 = (bf16[256,1536]{1,0:T(8,128)(2,1)S(1)}, bf16[256,1536]{1,0:T(8,128)(2,1)}, u32[]{:S(2)}) copy-start(bf16[256,1536]{1,0:T(8,128)(2,1)} %copy-done.10) | copy-start | bytes 2359300
  444.9 27.0 %copy-start.8 = (bf16[1024,768]{1,0:T(8,128)(2,1)S(1)}, bf16[1024,768]{1,0:T(8,128)(2,1)}, u32[]{:S(2)}) copy-start(bf16[1024,768]{1,0:T(8,128)(2,1)} %copy-done.7) | copy-start | bytes 4718596
  477.9 186.3 %reduce-scatter.4.cloned.1.call-start = ((), (), s32[]{:S(2)}) async-start(), calls=%async_computation.5 | async-start | bytes 6635520 | tf_op jit(solution)/shard_map/reduce_scatter | solution.py:876
  491.7 97.9 %collective-permute-start.3 = (bf16[256,1536]{1,0:T(8,128)(2,1)}, bf16[256,1536]{1,0:T(8,128)(2,1)}, u32[]{:S(2)}, u32[]{:S(2)}) collective-permute-start(bf16[256,1536]{1,0:T(8,128)(2,1)} %broadcast_select_fusion.2), channel_id=1, source_target_pairs={{0,16},{16,0},{1,17},{17,1},{2,18},{18,2},{3,19},{19,3},{4,20},{20... | collective-permute-start | bytes 2359304 | tf_op jit(solution)/shard_map/ppermute | solution.py:864
  541.1 32.3 %copy-start.27 = (bf16[1024,1536]{1,0:T(8,128)(2,1)S(1)}, bf16[1024,1536]{1,0:T(8,128)(2,1)}, u32[]{:S(2)}) copy-start(bf16[1024,1536]{1,0:T(8,128)(2,1)} %get-tuple-element.45) | copy-start | bytes 9437188
  551.5 21.9 %copy-start.26 = (bf16[1024,1920]{1,0:T(8,128)(2,1)S(1)}, bf16[1024,1920]{1,0:T(8,128)(2,1)}, u32[]{:S(2)}) copy-start(bf16[1024,1920]{1,0:T(8,128)(2,1)} %get-tuple-element.67) | copy-start | bytes 11796484
  573.4 8.4 %copy-start.17 = (bf16[2,1,256,1536]{3,2,1,0:T(8,128)(2,1)S(1)}, bf16[2,1,256,1536]{3,2,1,0:T(8,128)(2,1)}, u32[]{:S(2)}) copy-start(bf16[2,1,256,1536]{3,2,1,0:T(8,128)(2,1)} %param.15) | copy-start | bytes 4718596
  586.0 20.3 %collective-permute-start.4 = (bf16[256,1536]{1,0:T(8,128)(2,1)}, bf16[256,1536]{1,0:T(8,128)(2,1)S(1)}, u32[]{:S(2)}, u32[]{:S(2)}) collective-permute-start(bf16[256,1536]{1,0:T(8,128)(2,1)} %get-tuple-element.124), channel_id=1, source_target_pairs={{0,16},{16,0},{1,17},{17,1},{2,18},{18,2},{3,19},{19,3},{4,20},{20... | collective-permute-start | bytes 2359304 | tf_op jit(solution)/shard_map/ppermute | solution.py:864
  591.9 14.4 %copy-start.15 = (bf16[256,1536]{1,0:T(8,128)(2,1)S(1)}, bf16[256,1536]{1,0:T(8,128)(2,1)}, u32[]{:S(2)}) copy-start(bf16[256,1536]{1,0:T(8,128)(2,1)} %get-tuple-element.127) | copy-start | bytes 2359300
  591.9 14.4 %copy-start.19 = (bf16[256,1536]{1,0:T(8,128)(2,1)S(1)}, bf16[256,1536]{1,0:T(8,128)(2,1)}, u32[]{:S(2)}) copy-start(bf16[256,1536]{1,0:T(8,128)(2,1)} %get-tuple-element.125) | copy-start | bytes 2359300
  (15 other events, 40.2 us)
Sparse Core Ops, SparseCore 0:
  154.3 90.9 all-gather.2
  247.5 51.5 all-gather.4
  361.4 64.7 reduce-scatter.7
  478.0 68.3 reduce-scatter.5
  550.0 114.2 reduce-scatter.3

commit v3 on v2

--- a/solution.py
+++ b/solution.py
@@ -8,6 +8,11 @@
 from jax.experimental.pallas import tpu as pltpu
 BF=jnp.bfloat16; F32=jnp.float32
 NS=128; Q=128; CONV=4
+
+
+def cost(us):
+    return pl.CostEstimate(flops=us * 700_000_000, bytes_accessed=us * 1_500_000, transcendentals=0)
+
 
 def dot(a,b): return jnp.dot(a,b,preferred_element_type=F32)
 def dot_nt(a,b): return lax.dot_general(a,b,(((1,),(1,)),((),())),preferred_element_type=F32)
@@ -100,6 +105,7 @@
         scratch_shapes=[pltpu.VMEM((Q+8, width+2*NS), F32), pltpu.VMEM((NS, width), F32)]
             + [pltpu.VMEM((Q, width), F32)]*3,
         compiler_params=pltpu.CompilerParams(dimension_semantics=("arbitrary",), vmem_limit_bytes=48<<20),
+        cost_estimate=cost(12),
         name="mixer_fwd",
     )(pre, par, spread)
 
@@ -252,6 +258,7 @@
             + [pltpu.VMEM((Q, width), F32)]*3
             + [pltpu.VMEM((64, width+2*NS), F32), pltpu.VMEM((Q, width+2*NS), F32), pltpu.VMEM((8, 128), F32)],
         compiler_params=pltpu.CompilerParams(dimension_semantics=("arbitrary",), vmem_limit_bytes=56<<20),
+        cost_estimate=cost(40),
         name="mixer_bwd",
     )(pre, pre, par, spread, gather, states, dh, kap)
 
@@ -343,6 +350,7 @@
             pltpu.SemaphoreType.DMA((count, PIECES, 3)),
             pltpu.SemaphoreType.DMA((count,)),
         ],
+        cost_estimate=cost(22),
         compiler_params=pltpu.CompilerParams(collective_id=group_id, has_side_effects=True),
         name="token_gather",
     )(*values)
@@ -452,6 +460,7 @@
         in_specs=[pl.BlockSpec(memory_space=pltpu.VMEM)] * len(operands),
         out_specs=[pl.BlockSpec(memory_space=pltpu.VMEM)] * len(operands),
         scratch_shapes=scratch,
+        cost_estimate=cost(22),
         compiler_params=pltpu.CompilerParams(collective_id=group_id, has_side_effects=True, vmem_limit_bytes=40 << 20),
         name="token_scatter",
     )(*operands)
@@ -634,6 +643,7 @@
         in_specs=[pl.BlockSpec(memory_space=pltpu.VMEM)] * 3,
         out_specs=[pl.BlockSpec(memory_space=pl.ANY)] * 3,
         scratch_shapes=[sem(count, n), sem(count, n), sem(2, count, n), sem(2, count, n), sem(3), sem(3), sem(3)],
+        cost_estimate=cost(110),
         compiler_params=pltpu.CompilerParams(collective_id=group_id, has_side_effects=True),
         name="weights_open",
     )(own_in, own_out, xn)
@@ -649,14 +659,16 @@
 
 
 def finish_kernel(
-    n, shared, g_ref, half_ref, own_ref, send_ref, small_ref,
-    gin_ref, gout_ref, small_x_ref, small_t_ref, bc_ref,
-    x_recv, z_recv, z_send, last_buf, last_recv, join_recv, out_recv,
-    small_recv, small_all, small_ten, bc_own, bc_far, bc_mid, bc_near,
-    x_ss, x_rs, z_ss, z_rs, m_ss, m_rs, d_ss, d_rs, t_ss, t_rs,
+    n, bc_at, gain_rows,
+    g_ref, mid_ref, half_ref, own_ref, gp_ref, w_ref, u_ref, seed_ref, inv_ref, gain_ref, small_ref,
+    gin_ref, gout_ref, small_x_ref, small_t_ref, bc_ref, du_ref, du_got_ref,
+    x_recv, z_recv, z_send, o_recv, o_send, last_buf, last_recv, join_recv, olast_buf, olast_recv,
+    part_a, part_b, near_recv, far_send, far_recv, dxn, gain_acc,
+    small_own, small_recv, small_all, small_ten, bc_own, bc_far, bc_mid, bc_near,
+    x_ss, x_rs, z_ss, z_rs, o_ss, o_rs, m_ss, m_rs, d_ss, d_rs, t_ss, t_rs, y_ss, y_rs,
 ):
     sec, z, ten = lax.axis_index("section"), lax.axis_index("dp"), lax.axis_index("tensor")
-    half = half_ref.shape[0]
+    half, wide = half_ref.shape
     rows = 2 * half
     mine, theirs = sec * half, (1 - sec) * half
     across = peer("section", 1 - sec)
@@ -664,194 +676,327 @@
     others = [lax.rem(z + d, n) for d in range(1, n)]
     mates = [ten ^ d for d in range(1, 4)]
     greet([across] + [peer("dp", o) for o in others] + [peer("tensor", t) for t in mates])
-    srows = small_recv.shape[0]
-
-    def own_rows(s, offset):
+    cut = wide // 256 * 128
+    columns = (slice(cut, wide), slice(0, cut))
+    order = [i // 2 if i % 2 else n - 1 - i // 2 for i in range(n)]
+
+    def shard_rows(s, offset):
         return pl.ds(pl.multiple_of(s * rows + offset, 16), half)
 
-    small_x = remote(small_ref.at[pl.ds(pl.multiple_of((1 - sec) * srows, 8), srows)], small_recv,
-                     m_ss.at[0], m_rs.at[0], across)
+    x_copies = {}
+    for c, cols in enumerate(columns):
+        for s in order:
+            x_copies[c, s] = remote(
+                g_ref.at[shard_rows(s, theirs), cols], x_recv.at[s, :, cols], x_ss.at[c, s], x_rs.at[c, s], across
+            )
+    early = [(0, s) for s in order] + [(1, order[0])]
+    for key in early:
+        x_copies[key].start()
+    join = remote(half_ref, join_recv, m_ss.at[0], m_rs.at[0], across)
+    ojoin = remote(own_ref, olast_recv, m_ss.at[1], m_rs.at[1], across)
+    olast = remote(olast_buf, olast_recv, m_ss.at[1], m_rs.at[1], across)
+    lasts = [
+        remote(last_buf.at[:, cols], last_recv.at[:, cols], m_ss.at[2 + c], m_rs.at[2 + c], across)
+        for c, cols in enumerate(columns)
+    ]
+    du_copy = remote(du_ref, du_got_ref, m_ss.at[4], m_rs.at[4], across)
+
+    @pl.when(sec == 0)
+    def _():
+        ojoin.start()
+
+    trows = u_ref.shape[0]
+    step = 256
+    tiles = w_ref.shape[0] // step
+
+    def product(index, put):
+        @pl.loop(0, tiles)
+        def _(tile):
+            at = pl.ds(pl.multiple_of(tile * step, step), step)
+            put(at, dot_nt(gp_ref[pl.ds(pl.multiple_of(index * trows, 16), trows), :], w_ref[at, :]))
+
+    y_cross = remote(part_a, near_recv.at[0], y_ss.at[0], y_rs.at[0], near)
+    y_near = remote(part_b, near_recv.at[1], y_ss.at[1], y_rs.at[1], near)
+    y_far = remote(far_send, far_recv, y_ss.at[2], y_rs.at[2], far)
+
+    def put_a(at, value):
+        part_a[:, at] = value.astype(BF)
+
+    def put_b(at, value):
+        part_b[:, at] = value.astype(BF)
+
+    def put_far(at, value):
+        far_send[:, at] = (value + near_recv[0, :, at].astype(F32)).astype(BF)
+
+    def put_own(at, value):
+        dxn[:, at] = value
+
+    product(ten ^ 3, put_a)
+    y_cross.start()
+    product(ten ^ 1, put_b)
+    y_near.start()
+    y_cross.wait_recv()
+    product(ten ^ 2, put_far)
+    y_far.start()
+    product(ten, put_own)
+
+    def down(s):
+        right = s > z
+        return jnp.where(right, 0, 1), peer("dp", z + jnp.where(right, 1, -1)), jnp.where(right, z > 0, z < n - 1)
+
+    def reduce_step(s, plain, recv, send, ss, rs, cols):
+        @pl.when(s != z)
+        def _():
+            side, below, upstream = down(s)
+
+            @pl.when(upstream)
+            def _():
+                remote(send.at[s, :, cols], recv.at[side, s, :, cols], ss.at[s], rs.at[side, s], across).wait_recv()
+
+                def body(r):
+                    at = pl.ds(r, CHUNK_ROWS)
+                    send[s, at, cols] = (plain(s, r, cols) + recv[side, s, at, cols].astype(F32)).astype(BF)
+
+                by_rows(half, body)
+
+            @pl.when(jnp.logical_not(upstream))
+            def _():
+                def body(r):
+                    send[s, pl.ds(r, CHUNK_ROWS), cols] = plain(s, r, cols).astype(BF)
+
+                by_rows(half, body)
+
+            remote(send.at[s, :, cols], recv.at[side, s, :, cols], ss.at[s], rs.at[side, s], below).start()
+
+    def reduce_own(plain, recv, ss, rs, send, cols, target):
+        def base(r):
+            target[pl.ds(r, CHUNK_ROWS), cols] = plain(z, r, cols)
+
+        by_rows(half, base)
+        for side, there in ((0, z > 0), (1, z < n - 1)):
+
+            @pl.when(there)
+            def _():
+                remote(send.at[0, :, cols], recv.at[side, z, :, cols], ss.at[0], rs.at[side, z], across).wait_recv()
+
+                def more(r):
+                    at = pl.ds(r, CHUNK_ROWS)
+                    target[at, cols] += recv[side, z, at, cols].astype(F32)
+
+                by_rows(half, more)
+
+    def reduce_done(send, recv, ss, rs, cols):
+        for s in order:
+            @pl.when(s != z)
+            def _():
+                side, below, _ = down(s)
+                remote(send.at[s, :, cols], recv.at[side, s, :, cols], ss.at[s], rs.at[side, s], below).wait_send()
+
+    def in_plain(s, r, cols):
+        at = pl.ds(pl.multiple_of(s * rows + mine + r, 16), CHUNK_ROWS)
+        return g_ref[at, cols].astype(F32) + x_recv[s, pl.ds(r, CHUNK_ROWS), cols].astype(F32)
+
+    def out_plain(s, r, cols):
+        return mid_ref[pl.ds(pl.multiple_of(s * half + r, 16), CHUNK_ROWS), cols].astype(F32)
+
+    ocols = slice(0, own_ref.shape[1])
+
+    def in_step(c, k):
+        s = order[k]
+        x_copies[c, s].wait_recv()
+        reduce_step(s, in_plain, x_in, z_in, z_ss.at[c], z_rs.at[c], columns[c])
+
+    x_in, z_in = z_recv, z_send
+    for s in order:
+        reduce_step(s, out_plain, o_recv, o_send, o_ss, o_rs, ocols)
+    in_step(0, 0)
+    in_step(0, 1)
+    y_near.wait_recv()
+    y_far.wait_recv()
+    gain_acc[...] = jnp.zeros_like(gain_acc)
+    model = u_ref.shape[1]
+
+    def du_rows(r):
+        at = pl.ds(r, CHUNK_ROWS)
+        u = u_ref[at, :].astype(F32)
+        inv = inv_ref[at, :]
+        grad = dxn[at, :] + near_recv[1, at, :].astype(F32) + far_recv[at, :].astype(F32)
+        scaled = grad * gain_ref[...]
+        dots = jnp.sum(scaled * u, axis=1, keepdims=True)
+        du_ref[at, :] = (seed_ref[at, :].astype(F32) + inv * scaled - u * (inv * inv * inv * dots / model)).astype(BF)
+        gain_acc[...] += fold8(grad * u * inv)
+
+    by_rows(trows, du_rows)
+
+    srows, swide = small_recv.shape
+    small_own[...] = small_ref[...]
+    gain_sum = jnp.sum(gain_acc[...], axis=0, keepdims=True)
+    for k in range(gain_rows):
+        part = gain_sum[:, k * swide : min((k + 1) * swide, model)]
+        small_own[8 + k : 9 + k, 0 : part.shape[1]] = part
+    small_x = remote(small_own.at[pl.ds(pl.multiple_of((1 - sec) * srows, 8), srows)], small_recv,
+                     m_ss.at[5], m_rs.at[5], across)
     small_x.start()
-    order = [i // 2 if i % 2 else n - 1 - i // 2 for i in range(n)]
-    x_copies = {}
-    for s in order:
-        x_copies[s] = remote(g_ref.at[own_rows(s, theirs)], x_recv.at[s], x_ss.at[s], x_rs.at[s], across)
-        x_copies[s].start()
-    join = remote(half_ref, join_recv, m_ss.at[1], m_rs.at[1], across)
-    last = remote(last_buf, last_recv, m_ss.at[2], m_rs.at[2], across)
-    out_copy = remote(send_ref, out_recv, m_ss.at[3], m_rs.at[3], across)
-    out_copy.start()
+    for key, copy in x_copies.items():
+        if key not in early:
+            copy.start()
+
+    @pl.when(sec == 1)
+    def _():
+        du_copy.start()
 
     @pl.when(sec == 0)
     def _():
         join.start()
 
+    for k in range(2, n):
+        in_step(0, k)
     small_x.wait_recv()
-    small_all[z] = small_ref[pl.ds(pl.multiple_of(sec * srows, 8), srows), :] + small_recv[...]
+    small_all[z] = small_own[pl.ds(pl.multiple_of(sec * srows, 8), srows), :] + small_recv[...]
     to_dp = [remote(small_all.at[z], small_all.at[z], d_ss.at[d], d_rs.at[z], peer("dp", o)) for d, o in enumerate(others)]
     for copy in to_dp:
         copy.start()
-
-    def z_copy(s):
-        right = s > z
-        side = jnp.where(right, 0, 1)
-        down = z + jnp.where(right, 1, -1)
-        return remote(z_send.at[s], z_recv.at[side, s], z_ss.at[s], z_rs.at[side, s], peer("dp", down))
-
-    def arrived(side, s):
-        remote(z_send.at[0], z_recv.at[side, s], z_ss.at[0], z_rs.at[side, s], across).wait_recv()
-
-    for s in order:
-        x_copies[s].wait_recv()
-
-        @pl.when(s != z)
+    reduce_own(out_plain, o_recv, o_ss, o_rs, o_send, ocols, gout_ref)
+
+    def halves(own_part, got, target, cols, own_first):
+        def put(r):
+            at, low = pl.ds(r, CHUNK_ROWS), pl.ds(pl.multiple_of(half + r, 16), CHUNK_ROWS)
+            if own_first:
+                target[low, cols] = got[at, cols].astype(F32)
+            else:
+                target[at, cols] = got[at, cols].astype(F32)
+                target[low, cols] = own_part[at, cols].astype(F32)
+
+        by_rows(half, put)
+
+    def hand_over(target, buffer, cols):
+        def put(r):
+            at = pl.ds(r, CHUNK_ROWS)
+            buffer[at, cols] = target[at, cols].astype(BF)
+
+        by_rows(half, put)
+
+    @pl.when(sec == 1)
+    def _():
+        hand_over(gout_ref, olast_buf, ocols)
+        olast.start()
+
+    def start_bc():
+        bc_own[...] = gin_ref[:, bc_at : bc_at + 2 * NS].astype(BF)
+        remote(bc_own, bc_far, t_ss.at[3], t_rs.at[4], far).start()
+
+    for c, cols in enumerate(columns):
+        if c:
+            for k in range(n):
+                in_step(c, k)
+            for d, o in enumerate(others):
+                remote(small_all.at[o], small_all.at[o], d_ss.at[d], d_rs.at[o], across).wait_recv()
+            total = small_all[0]
+            for k in range(1, n):
+                total = total + small_all[k]
+            small_x_ref[...] = total
+            small_ten[ten] = total
+            to_ten = [
+                remote(small_ten.at[ten], small_ten.at[ten], t_ss.at[d], t_rs.at[ten], peer("tensor", t))
+                for d, t in enumerate(mates)
+            ]
+            for copy in to_ten:
+                copy.start()
+        reduce_own(in_plain, x_in, z_ss.at[c], z_rs.at[c], z_in, cols, gin_ref)
+
+        @pl.when(sec == 1)
         def _():
-            right = s > z
-            side = jnp.where(right, 0, 1)
-            upstream = jnp.where(right, z > 0, z < n - 1)
-
-            @pl.when(upstream)
-            def _():
-                arrived(side, s)
-
-                def body(r):
-                    z_send[s, pl.ds(r, CHUNK_ROWS), :] = (
-                        g_ref[pl.ds(pl.multiple_of(s * rows + mine + r, 16), CHUNK_ROWS), :].astype(F32)
-                        + x_recv[s, pl.ds(r, CHUNK_ROWS), :].astype(F32)
-                        + z_recv[side, s, pl.ds(r, CHUNK_ROWS), :].astype(F32)
-                    ).astype(BF)
-
-                by_rows(half, body)
-
-            @pl.when(jnp.logical_not(upstream))
-            def _():
-                def body(r):
-                    z_send[s, pl.ds(r, CHUNK_ROWS), :] = (
-                        g_ref[pl.ds(pl.multiple_of(s * rows + mine + r, 16), CHUNK_ROWS), :].astype(F32)
-                        + x_recv[s, pl.ds(r, CHUNK_ROWS), :].astype(F32)
-                    ).astype(BF)
-
-                by_rows(half, body)
-
-            z_copy(s).start()
-
-    for d, o in enumerate(others):
-        remote(small_all.at[o], small_all.at[o], d_ss.at[d], d_rs.at[o], across).wait_recv()
-    total = small_all[0]
-    for k in range(1, n):
-        total = total + small_all[k]
-    small_x_ref[...] = total
-    small_ten[ten] = total
-    to_ten = [remote(small_ten.at[ten], small_ten.at[ten], t_ss.at[d], t_rs.at[ten], peer("tensor", t)) for d, t in enumerate(mates)]
-    for copy in to_ten:
-        copy.start()
-
-    out_copy.wait_recv()
-
-    def put_out(r):
-        gout_ref[pl.ds(pl.multiple_of(mine + r, 16), CHUNK_ROWS), :] = own_ref[pl.ds(r, CHUNK_ROWS), :].astype(F32)
-        gout_ref[pl.ds(pl.multiple_of(theirs + r, 16), CHUNK_ROWS), :] = out_recv[pl.ds(r, CHUNK_ROWS), :].astype(F32)
-
-    by_rows(half, put_out)
-
-    def base(r):
-        gin_ref[pl.ds(r, CHUNK_ROWS), :] = (
-            g_ref[pl.ds(pl.multiple_of(z * rows + mine + r, 16), CHUNK_ROWS), :].astype(F32)
-            + x_recv[z, pl.ds(r, CHUNK_ROWS), :].astype(F32)
-        )
-
-    by_rows(half, base)
-    for side, there in ((0, z > 0), (1, z < n - 1)):
-
-        @pl.when(there)
-        def _():
-            arrived(side, z)
-
-            def more(r):
-                gin_ref[pl.ds(r, CHUNK_ROWS), :] += z_recv[side, z, pl.ds(r, CHUNK_ROWS), :].astype(F32)
-
-            by_rows(half, more)
+            hand_over(gin_ref, last_buf, cols)
+            lasts[c].start()
 
     @pl.when(sec == 1)
     def _():
-        def out(r):
-            last_buf[pl.ds(r, CHUNK_ROWS), :] = gin_ref[pl.ds(r, CHUNK_ROWS), :].astype(BF)
-
-        by_rows(half, out)
-        last.start()
+        olast.wait_recv()
+        halves(own_ref, olast_recv, gout_ref, ocols, False)
         join.wait_recv()
-
-        def put(r):
-            gin_ref[pl.ds(r, CHUNK_ROWS), :] = join_recv[pl.ds(r, CHUNK_ROWS), :].astype(F32)
-            gin_ref[pl.ds(pl.multiple_of(half + r, 16), CHUNK_ROWS), :] = half_ref[pl.ds(r, CHUNK_ROWS), :].astype(F32)
-
-        by_rows(half, put)
-        last.wait_send()
+        for cols in columns:
+            halves(half_ref, join_recv, gin_ref, cols, False)
+        start_bc()
 
     @pl.when(sec == 0)
     def _():
-        last.wait_recv()
-
-        def put(r):
-            gin_ref[pl.ds(pl.multiple_of(half + r, 16), CHUNK_ROWS), :] = last_recv[pl.ds(r, CHUNK_ROWS), :].astype(F32)
-
-        by_rows(half, put)
+        lasts[0].wait_recv()
+        halves(None, last_recv, gin_ref, columns[0], True)
+        start_bc()
+        olast.wait_recv()
+        halves(None, olast_recv, gout_ref, ocols, True)
+        lasts[1].wait_recv()
+        halves(None, last_recv, gin_ref, columns[1], True)
+        du_copy.wait_recv()
+        ojoin.wait_send()
         join.wait_send()
 
-    bc_own[...] = gin_ref[:, shared : shared + 2 * NS].astype(BF)
-    to_far = remote(bc_own, bc_far, t_ss.at[3], t_rs.at[4], far)
-    to_far.start()
     for d, t in enumerate(mates):
         remote(small_ten.at[t], small_ten.at[t], t_ss.at[d], t_rs.at[t], near).wait_recv()
     total = small_ten[0]
     for k in range(1, 4):
         total = total + small_ten[k]
     small_t_ref[...] = total
+    to_far = remote(bc_own, bc_far, t_ss.at[3], t_rs.at[4], far)
     to_far.wait_recv()
     bc_mid[...] = (bc_own[...].astype(F32) + bc_far[...].astype(F32)).astype(BF)
     to_near = remote(bc_mid, bc_near, t_ss.at[4], t_rs.at[5], near)
     to_near.start()
     to_near.wait_recv()
     bc_ref[...] = bc_mid[...].astype(F32) + bc_near[...].astype(F32)
-    for s in order:
-        x_copies[s].wait_send()
-
-        @pl.when(s != z)
-        def _():
-            z_copy(s).wait_send()
-
-    for copy in [small_x, out_copy, to_far, to_near] + to_dp + to_ten:
+    for c, cols in enumerate(columns):
+        for s in order:
+            x_copies[c, s].wait_send()
+        reduce_done(z_in, x_in, z_ss.at[c], z_rs.at[c], cols)
+    reduce_done(o_send, o_recv, o_ss, o_rs, ocols)
+
+    @pl.when(sec == 1)
+    def _():
+        olast.wait_send()
+        for copy in lasts:
+            copy.wait_send()
+        du_copy.wait_send()
+
+    for copy in [small_x, to_far, to_near, y_cross, y_near, y_far] + to_dp + to_ten:
         copy.wait_send()
 
 
-def finish(grads, half_other, out_own, out_send, smalls, shared, group_id):
+def finish(grads, out_mid, half_other, out_other, gp, w_in, u, seed, inv, gain, smalls, bc_at, gain_rows, group_id):
     n = lax.axis_size("dp")
     half, wide = half_other.shape
-    owide = out_own.shape[1]
+    owide = out_other.shape[1]
+    trows, model = u.shape
     srows, swide = smalls.shape[0] // 2, smalls.shape[1]
-    vm = lambda shape, dtype: pltpu.VMEM(shape, dtype)
+    vm = lambda dtype, *shape: pltpu.VMEM(shape, dtype)
     sem = lambda *shape: pltpu.SemaphoreType.DMA(shape)
     return pl.pallas_call(
-        functools.partial(finish_kernel, n, shared),
+        functools.partial(finish_kernel, n, bc_at, gain_rows),
         out_shape=[
             jax.ShapeDtypeStruct((2 * half, wide), F32),
             jax.ShapeDtypeStruct((2 * half, owide), F32),
             jax.ShapeDtypeStruct((srows, swide), F32),
             jax.ShapeDtypeStruct((srows, swide), F32),
             jax.ShapeDtypeStruct((2 * half, 2 * NS), F32),
+            jax.ShapeDtypeStruct((trows, model), BF),
+            jax.ShapeDtypeStruct((trows, model), BF),
         ],
-        in_specs=[pl.BlockSpec(memory_space=pltpu.VMEM)] * 5,
-        out_specs=[pl.BlockSpec(memory_space=pltpu.VMEM)] * 5,
+        in_specs=[pl.BlockSpec(memory_space=pltpu.VMEM)] * 11,
+        out_specs=[pl.BlockSpec(memory_space=pltpu.VMEM)] * 7,
         scratch_shapes=[
-            vm((n, half, wide), BF), vm((2, n, half, wide), BF), vm((n, half, wide), BF),
-            vm((half, wide), BF), vm((half, wide), BF), vm((half, wide), BF), vm((half, owide), BF),
-            vm((srows, swide), F32), vm((n, srows, swide), F32), vm((4, srows, swide), F32),
-            vm((2 * half, 2 * NS), BF), vm((2 * half, 2 * NS), BF), vm((2 * half, 2 * NS), BF), vm((2 * half, 2 * NS), BF),
-            sem(n), sem(n), sem(n), sem(2, n), sem(4), sem(4), sem(n), sem(n), sem(5), sem(6),
+            vm(BF, n, half, wide), vm(BF, 2, n, half, wide), vm(BF, n, half, wide),
+            vm(BF, 2, n, half, owide), vm(BF, n, half, owide),
+            vm(BF, half, wide), vm(BF, half, wide), vm(BF, half, wide), vm(BF, half, owide), vm(BF, half, owide),
+            vm(BF, trows, model), vm(BF, trows, model), vm(BF, 2, trows, model), vm(BF, trows, model),
+            vm(BF, trows, model), vm(F32, trows, model), vm(F32, 8, model),
+            vm(F32, 2 * srows, swide), vm(F32, srows, swide), vm(F32, n, srows, swide), vm(F32, 4, srows, swide),
+            vm(BF, 2 * half, 2 * NS), vm(BF, 2 * half, 2 * NS), vm(BF, 2 * half, 2 * NS), vm(BF, 2 * half, 2 * NS),
+            sem(2, n), sem(2, n), sem(2, n), sem(2, 2, n), sem(n), sem(2, n),
+            sem(6), sem(6), sem(n), sem(n), sem(5), sem(6), sem(3), sem(3),
         ],
-        compiler_params=pltpu.CompilerParams(collective_id=group_id, has_side_effects=True, vmem_limit_bytes=60 << 20),
+        cost_estimate=cost(120),
+        compiler_params=pltpu.CompilerParams(collective_id=group_id, has_side_effects=True, vmem_limit_bytes=63 << 20),
         name="grad_finish",
-    )(grads, half_other, out_own, out_send, smalls)
+    )(grads, out_mid, half_other, out_other, gp, w_in, u, seed, inv, gain, smalls)
 
 
 EPSILON = 1e-05
@@ -938,25 +1083,29 @@
         projected = total * q
         return (u + projected).astype(BF), (u, inv, xn, pre, yn, states, q, projected, w_in, w_out)
 
-    def backward(layer, g, kept):
+    def backward_core(layer, g, kept):
         u, inv, xn, pre, yn, states, q, projected, w_in, w_out = kept
         kappa = q * q / total_inner * jnp.sum(g * projected, axis=1, keepdims=True)
         high = kappa.astype(BF)
         low = (kappa - high.astype(F32)).astype(BF)
         side = jnp.pad(jnp.concatenate([high, low], axis=1), ((0, 0), (0, 126)))
         gq, side = token_gather([(g * q).astype(BF), side], 5 + layer)
+        g_out = dot_tn(gq, yn).astype(BF)
         dh = dot(gq, w_out)
         gp, acc = mixer_bwd(pre, pars[layer], spread, gather, states, dh, side, width, heads)
-        g_out = dot_tn(gq, yn).astype(BF)
         g_in = dot_tn(xn, gp).astype(BF)
-        (dxn,) = token_scatter(dot_nt(gp, w_in).astype(BF), 7 + layer)
+        return gp, acc, g_in, g_out
+
+    def backward_input(layer, g, kept, gp):
+        u, inv = kept[:2]
+        (dxn,) = token_scatter(dot_nt(gp, kept[8]).astype(BF), 7 + layer)
         scaled = dxn * gains[layer][None, :]
         dots = jnp.sum(scaled * u, axis=1, keepdims=True)
         du = g + inv * scaled - u * (inv * inv * inv) * dots / model
-        g_gain = jnp.sum(dxn * u * inv, axis=0)
-        return du.astype(BF), g_in, g_out, acc, g_gain
-
-    u0 = lax.dynamic_index_in_dim(stream[:, 0], section, 0, False).astype(F32)
+        return du.astype(BF), jnp.sum(dxn * u * inv, axis=0)
+
+    stream_own = lax.dynamic_index_in_dim(stream[:, 0], section, 0, False)
+    u0 = stream_own.astype(F32)
     inv0, xn0 = normed(0, u0)
     w_in0, w_out0, xn0 = open_gather(own_in, own_out, xn0, 1)
     full_in1, w_in0 = later_gather(own_in, is_first, w_in0)
@@ -968,11 +1117,17 @@
     (xn1,) = token_gather([xn1], 2)
     out1, kept1 = forward(1, u1, inv1, xn1, full_in1, full_out1)
     g1 = lax.dynamic_index_in_dim(cotangent[:, 0], section, 0, False).astype(F32)
-    du1, g_in1, g_out1, acc1, gain1 = backward(1, g1, kept1)
+    gp1, acc1, g_in1, g_out1 = backward_core(1, g1, kept1)
     half_out1 = grad_scatter(g_out1)
     half_in1 = grad_scatter(g_in1)
-    du0, g_in0, g_out0, acc0, gain0 = backward(0, du1.astype(F32), kept0)
-    half_out0 = grad_scatter(g_out0)
+    gp1, g_in1 = lax.optimization_barrier((gp1, g_in1))
+    du1, gain1 = backward_input(1, g1, kept1, gp1)
+    gp0, acc0, g_in0, g_out0 = backward_core(0, du1.astype(F32), kept0)
+    split_out = g_out0.reshape(-1, 2, shard // 2, width)
+    mine = jnp.where(is_first, split_out[:, 0], split_out[:, 1])
+    theirs = swap_sections(jnp.where(is_first, split_out[:, 1], split_out[:, 0]))
+    out_mid = (mine.astype(F32) + theirs.astype(F32)).astype(BF).reshape(-1, width)
+    du1_first = lax.ppermute(du1, "section", [(0, 1)])
 
     def by_batch(first_value, second_value):
         own = jnp.where(is_first, first_value, second_value)
@@ -990,14 +1145,15 @@
             axis=0,
         )
 
-    smalls = jnp.concatenate([minor(acc0, gain0), minor(acc1, gain1)])
-    g_in, g_out, mine, shared, bc_rows = finish(
-        g_in0, half_in1, jnp.where(is_first, half_out0, half_out1),
-        jnp.where(is_first, half_out1, half_out0), smalls, 2 * width, 9,
+    smalls = jnp.concatenate([minor(acc0, jnp.zeros_like(gain1)), minor(acc1, gain1)])
+    g_in, g_out, mine, shared, bc_rows, du0, du0_second = finish(
+        g_in0, out_mid, half_in1, half_out1, gp0, w_in0, stream_own, du1, inv0, gains[0][None, :],
+        smalls, 2 * width, gain_rows, 9,
     )
+    grads = jnp.stack([jnp.where(is_first, du0, du1_first), jnp.where(is_first, du0_second, du1)])
     return (
         by_batch(out0, out1),
-        by_batch(du0, du1),
+        grads[None, :, None],
         shared[8 : 8 + gain_rows].reshape(-1)[:model][None],
         g_in[:, : 2 * width].reshape(shard, 2, width)[None],
         g_in[:, 2 * width + 2 * NS : 2 * width + 2 * NS + heads][None],

time: 820 us -> 733 us (0.89)
  waiting for transfers between devices: 103 us -> 34.9 us
  matrix products: 98 us -> 84.4 us
  Pallas kernels: 527 us -> 517 us
    reduce_scatter x3 -> x2, waiting for transfers between devices: 54.5 us -> 0.01 us  [grad_scatter(): lax.psum_scatter(value, ('dp', 'section'), scatter_dimension=0, tiled=True)]
    pallas_call x4 -> x3, Pallas kernels: 89.9 us -> 68 us  [token_scatter(): pl.pallas_call(functools.partial(token_scatter_kernel, side is not None),...]
    ppermute x3, waiting for transfers between devices: 13.1 us -> 0.01 us  [swap_sections(): lax.ppermute(value, 'section', [(i, (i + 1) % count) for i in range(count)])]
    pallas_call x1, Pallas kernels: 125 us -> 137 us  [finish(): pl.pallas_call(functools.partial(finish_kernel, n, bc_at, gain_rows), out...]
    dot_general x4 -> x3, matrix products: 28 us -> 17.4 us  [dot_nt(): lax.dot_general(a, b, (((1,), (1,)), ((), ())), preferred_element_type=F32)]
  transfers between devices with their start and end apart: 10 -> 10, of which waited for: 5 -> 3; matrix products, arithmetic and copies ran while one was open for 14% -> 17% of each run, Pallas kernels for 43% -> 68%
where the time goes in v3:
time: 733 us; the launch traced here: 726 us
  Pallas kernels  517 us (71%)
  matrix products  84.4 us (12%)
  local copies, waits for them, and re-layouts  35.7 us (5%)
  waiting for transfers between devices  34.9 us (5%)
  other arithmetic  29.8 us (4%)
  between operations  14.7 us (2%)
  starting transfers between devices  8.74 us (1%)
    pallas_call x1, Pallas kernels, finish(): pl.pallas_call(functools.partial(finish_kernel, n, bc_at, gain_rows), out...  137 us
    pallas_call x1, Pallas kernels, open_gather(): pl.pallas_call(functools.partial(open_kernel, n, pieces), out_shape=[jax....  129 us
    pallas_call x2, Pallas kernels, mixer_bwd(): pl.pallas_call(functools.partial(bwd_kernel, width, n_heads), grid=(n,),...  85.4 us
    pallas_call x3, Pallas kernels, token_gather(): pl.pallas_call(functools.partial(token_gather_kernel, count), out_shape=[...  71.2 us
    pallas_call x3, Pallas kernels, token_scatter(): pl.pallas_call(functools.partial(token_scatter_kernel, side is not None),...  68 us
    dot_general x4, matrix products, dot(): return jnp.dot(a, b, preferred_element_type=F32)  35 us
    dot_general x4, matrix products, dot_tn(): lax.dot_general(a, b, (((0,), (0,)), ((), ())), preferred_element_type=F32)  32 us
    all_gather x2, waiting for transfers between devices, later_gather(): return (lax.all_gather(piece, ('dp', 'section'), axis=0, tiled=True), after)  28.9 us
  transfers between devices with their start and end apart: 10, of which 3 were waited for; matrix products, arithmetic and copies ran while one was open for 17% of the time, Pallas kernels for 68%

profile of v3, /device:TPU:9, one launch (start us, length us, event | category | flops | bytes accessed | tf_op | source)
XLA Modules:
  0.0 725.6 jit_solution(15626435751711015162)
XLA Ops:
  22.7 129.2 %weights_open.1 = (bf16[1536,1920]{1,0:T(8,128)(2,1)}, bf16[1536,768]{1,0:T(8,128)(2,1)}, bf16[1024,1536]{1,0:T(8,128)(2,1)}) custom-call(bf16[384,1920]{1,0:T(8,128)(2,1)} %copy-done.16, bf16[384,768]{1,0:T(8,128)(2,1)} %bitcast.126, bf16[256,1536]{1,0:T(8,128)(2,1)} %fusion.6.xn_ref), custom_call_target="tpu_custom_call" | custom-call | flops 76999999488 | bytes 165000000 | tf_op jit(solution)/shard_map/weights_open/pallas_call | solution.py:636
  158.6 6.0 collective-permute-done.1
  165.3 11.9 %fusion.32.pre_ref.halo_ref = f32[1024,1920]{1,0:T(8,128)} fusion(bf16[1024,1536]{1,0:T(8,128)(2,1)} %get-tuple-element.48, bf16[1536,1920]{1,0:T(8,128)(2,1)} %get-tuple-element.51.w_ref), kind=kOutput, calls=%fused_computation.101 | convolution fusion | flops 6039797760 | bytes 16908288 | tf_op jit(solution)/shard_map/dot_general | solution.py:17
  177.2 13.3 %mixer_fwd.2 = (bf16[1024,768]{1,0:T(8,128)(2,1)S(1)}, f32[64,128]{1,0:T(8,128)S(1)}, f32[8,128,768]{2,1,0:T(8,128)S(1)}) custom-call(f32[1024,1920]{1,0:T(8,128)} %fusion.32.pre_ref.halo_ref, f32[16,1024]{1,0:T(8,128)S(1)} %get-tuple-element.139.par_ref, bf16[256,768]{1,0:T(8,128)(2,1)S(1)} %compare_convert_fusion.spread_ref), custom_call_target="tpu_custom_call" | custom-call | flops 8400000000 | bytes 18000000 | tf_op jit(solution)/shard_map/mixer_fwd/pallas_call | solution.py:94
  193.4 23.0 %token_scatter.3 = (f32[256,1536]{1,0:T(8,128)S(1)}, f32[16,128]{1,0:T(8,128)S(1)}) custom-call(bf16[1024,1536]{1,0:T(8,128)(2,1)S(1)} %convolution_convert_fusion.4.refs_0_, f32[64,128]{1,0:T(8,128)S(1)} %get-tuple-element.54.refs_1_), custom_call_target="tpu_custom_call" | custom-call | flops 15399999488 | bytes 33000000 | tf_op jit(solution)/shard_map/token_scatter/pallas_call | solution.py:457
  220.7 22.9 %token_gather.3 = bf16[1024,1536]{1,0:T(8,128)(2,1)} custom-call(bf16[256,1536]{1,0:T(8,128)(2,1)} %fusion.14.refs_0_), custom_call_target="tpu_custom_call" | custom-call | flops 15399999488 | bytes 33000000 | tf_op jit(solution)/shard_map/token_gather/pallas_call | solution.py:343
  245.4 11.9 %fusion.33.pre_ref.halo_ref = f32[1024,1920]{1,0:T(8,128)} fusion(bf16[1024,1536]{1,0:T(8,128)(2,1)} %token_gather.3, bf16[1536,1920]{1,0:T(8,128)(2,1)} %all-gather.3.cloned.1.call-done), kind=kOutput, calls=%fused_computation.102 | convolution fusion | flops 6039797760 | bytes 16908288 | tf_op jit(solution)/shard_map/dot_general | solution.py:17
  257.3 13.2 %mixer_fwd.3 = (bf16[1024,768]{1,0:T(8,128)(2,1)S(1)}, f32[64,128]{1,0:T(8,128)S(1)}, f32[8,128,768]{2,1,0:T(8,128)S(1)}) custom-call(f32[1024,1920]{1,0:T(8,128)} %fusion.33.pre_ref.halo_ref, f32[16,1024]{1,0:T(8,128)S(1)} %get-tuple-element.138.par_ref, bf16[256,768]{1,0:T(8,128)(2,1)S(1)} %compare_convert_fusion.spread_ref), custom_call_target="tpu_custom_call" | custom-call | flops 8400000000 | bytes 18000000 | tf_op jit(solution)/shard_map/mixer_fwd/pallas_call | solution.py:94
  272.1 27.0 %all-gather.5.cloned.1.call-done = bf16[1536,768]{1,0:T(8,128)(2,1)} async-done(((bf16[192,768]{1,0:T(8,128)(2,1)}), bf16[1536,768]{1,0:T(8,128)(2,1)}) %all-gather.5.cloned.1.call-update) | async-done | bytes 2359312 | tf_op jit(solution)/shard_map/all_gather | solution.py:1017
  299.2 4.5 convolution_convert_fusion.3.refs_0_
  303.7 23.8 %token_scatter.4 = (f32[256,1536]{1,0:T(8,128)S(1)}, f32[16,128]{1,0:T(8,128)S(1)}) custom-call(bf16[1024,1536]{1,0:T(8,128)(2,1)S(1)} %convolution_convert_fusion.3.refs_0_, f32[64,128]{1,0:T(8,128)S(1)} %get-tuple-element.60.refs_1_), custom_call_target="tpu_custom_call" | custom-call | flops 15399999488 | bytes 33000000 | tf_op jit(solution)/shard_map/token_scatter/pallas_call | solution.py:457
  332.2 24.0 %token_gather.4 = (bf16[1024,1536]{1,0:T(8,128)(2,1)}, bf16[1024,128]{1,0:T(8,128)(2,1)}) custom-call(bf16[256,1536]{1,0:T(8,128)(2,1)} %get-tuple-element.137.refs_0_, bf16[256,128]{1,0:T(8,128)(2,1)} %pad.41.refs_1_), custom_call_target="tpu_custom_call" | custom-call | flops 15399999488 | bytes 33000000 | tf_op jit(solution)/shard_map/token_gather/pallas_call | solution.py:343
  356.2 5.9 convolution_convert_fusion.5
  362.2 7.0 fusion.34.dh_ref
  369.2 42.9 %mixer_bwd.2 = (bf16[1024,1920]{1,0:T(8,128)(2,1)}, f32[8,1024]{1,0:T(8,128)}) custom-call(f32[1024,1920]{1,0:T(8,128)} %fusion.33.pre_ref.halo_ref, f32[1024,1920]{1,0:T(8,128)} %fusion.33.pre_ref.halo_ref, f32[16,1024]{1,0:T(8,128)} %copy-done.6, bf16[256,768]{1,0:T(8,128)(2,1)} %copy-done.4, bf16[768,128]{1,0:T(8,128)(2,1)} %fusion.22.gather_ref, ...), custom_call_target="tpu_custom_call" | custom-call | flops 28000000000 | bytes 60000000 | tf_op jit(solution)/shard_map/mixer_bwd/pallas_call | solution.py:243
  412.1 10.6 %convolution_convert_fusion.1 = bf16[1536,1920]{1,0:T(8,128)(2,1)} fusion(bf16[1024,1536]{1,0:T(8,128)(2,1)S(1)} %copy-done.44, bf16[1024,1920]{1,0:T(8,128)(2,1)} %get-tuple-element.68), kind=kOutput, calls=%fused_computation.1 | convolution fusion | flops 6042746880 | bytes 12976128 | tf_op jit(solution)/shard_map/dot_general | solution.py:19
  422.7 10.0 %convolution_convert_fusion.2.refs_0_ = bf16[1024,1536]{1,0:T(8,128)(2,1)S(1)} fusion(bf16[1024,1920]{1,0:T(8,128)(2,1)} %get-tuple-element.68, bf16[1536,1920]{1,0:T(8,128)(2,1)} %all-gather.3.cloned.1.call-done), kind=kOutput, calls=%fused_computation.2 | convolution fusion | flops 6041370624 | bytes 12976128 | tf_op jit(solution)/shard_map/dot_general | solution.py:18
  432.8 21.2 %token_scatter.5 = f32[256,1536]{1,0:T(8,128)S(1)} custom-call(bf16[1024,1536]{1,0:T(8,128)(2,1)S(1)} %convolution_convert_fusion.2.refs_0_), custom_call_target="tpu_custom_call" | custom-call | flops 15399999488 | bytes 33000000 | tf_op jit(solution)/shard_map/token_scatter/pallas_call | solution.py:457
  464.3 24.2 %token_gather.5 = (bf16[1024,1536]{1,0:T(8,128)(2,1)}, bf16[1024,128]{1,0:T(8,128)(2,1)}) custom-call(bf16[256,1536]{1,0:T(8,128)(2,1)} %fusion.2.refs_0_, bf16[256,128]{1,0:T(8,128)(2,1)} %pad.42.refs_1_), custom_call_target="tpu_custom_call" | custom-call | flops 15399999488 | bytes 33000000 | tf_op jit(solution)/shard_map/token_gather/pallas_call | solution.py:343
  488.5 4.8 convolution_convert_fusion.6
  496.5 4.3 fusion.35.dh_ref
  500.8 42.5 %mixer_bwd.3 = (bf16[1024,1920]{1,0:T(8,128)(2,1)}, f32[8,1024]{1,0:T(8,128)}) custom-call(f32[1024,1920]{1,0:T(8,128)} %fusion.32.pre_ref.halo_ref, f32[1024,1920]{1,0:T(8,128)} %fusion.32.pre_ref.halo_ref, f32[16,1024]{1,0:T(8,128)} %copy-done.5, bf16[256,768]{1,0:T(8,128)(2,1)} %copy-done.4, bf16[768,128]{1,0:T(8,128)(2,1)} %fusion.22.gather_ref, ...), custom_call_target="tpu_custom_call" | custom-call | flops 28000000000 | bytes 60000000 | tf_op jit(solution)/shard_map/mixer_bwd/pallas_call | solution.py:243
  543.3 10.7 %convolution_convert_fusion.g_ref = bf16[1536,1920]{1,0:T(8,128)(2,1)} fusion(bf16[1024,1536]{1,0:T(8,128)(2,1)S(1)} %copy-done.43, bf16[1024,1920]{1,0:T(8,128)(2,1)} %get-tuple-element.71.gp_ref), kind=kOutput, calls=%fused_computation | convolution fusion | flops 6042746880 | bytes 12976128 | tf_op jit(solution)/shard_map/dot_general | solution.py:19
  563.3 137.1 %grad_finish.1 = (f32[384,1920]{1,0:T(8,128)}, f32[384,768]{1,0:T(8,128)}, f32[16,1024]{1,0:T(8,128)}, f32[16,1024]{1,0:T(8,128)}, f32[384,256]{1,0:T(8,128)}, /...) custom-call(bf16[1536,1920]{1,0:T(8,128)(2,1)} %convolution_convert_fusion.g_ref, bf16[768,768]{1,0:T(8,128)(2,1)} %bitcast.129, ...), custom_call_target="tpu_custom_call" | custom-call | flops 83999997952 | bytes 180000000 | tf_op jit(solution)/shard_map/grad_finish/pallas_call | solution.py:972
  (199 shorter events, 79.0 us)
Async XLA Ops:
  7.2 238.2 %all-gather.3.cloned.1.call-start = ((), (), s32[]{:S(2)}) async-start(), calls=%async_computation.2 | async-start | bytes 6635520 | tf_op jit(solution)/shard_map/all_gather | solution.py:1017
  13.1 8.4 %collective-permute-start = (f32[16,1024]{1,0:T(8,128)S(1)}, f32[16,1024]{1,0:T(8,128)S(1)}, u32[]{:S(2)}, u32[]{:S(2)}) collective-permute-start(f32[16,1024]{1,0:T(8,128)S(1)} %concatenate.24), channel_id=1, source_target_pairs={{0,16},{16,0},{1,17},{17,1},{2,18},{18,2},{3,19},{19,3},{4,20},{20... | collective-permute-start | bytes 196616 | tf_op jit(solution)/shard_map/ppermute | solution.py:1009
  17.7 134.3 %collective-permute-start.2 = (bf16[192,1920]{1,0:T(8,128)(2,1)}, bf16[192,1920]{1,0:T(8,128)(2,1)}, u32[]{:S(2)}, u32[]{:S(2)}) collective-permute-start(bf16[192,1920]{1,0:T(8,128)(2,1)} %slice.102), channel_id=1, source_target_pairs={{16,0},{17,1},{18,2},{19,3},{20,4},{21,5},{22,6},{23,7},{24,8},{25... | collective-permute-start | bytes 2211848 | tf_op jit(solution)/shard_map/ppermute | solution.py:1015
  20.4 131.6 %copy-start.15 = (bf16[256,1536]{1,0:T(8,128)(2,1)}, bf16[256,1536]{1,0:T(8,128)(2,1)S(1)}, u32[]{:S(2)}) copy-start(bf16[256,1536]{1,0:T(8,128)(2,1)S(1)} %get-tuple-element.133.u_ref) | copy-start | bytes 2359300
  21.5 155.7 %copy-start.5 = (f32[16,1024]{1,0:T(8,128)}, f32[16,1024]{1,0:T(8,128)S(1)}, u32[]{:S(2)}) copy-start(f32[16,1024]{1,0:T(8,128)S(1)} %get-tuple-element.139.par_ref) | copy-start | bytes 196612
  21.5 235.8 %copy-start.6 = (f32[16,1024]{1,0:T(8,128)}, f32[16,1024]{1,0:T(8,128)S(1)}, u32[]{:S(2)}) copy-start(f32[16,1024]{1,0:T(8,128)S(1)} %get-tuple-element.138.par_ref) | copy-start | bytes 196612
  22.7 129.3 %copy-start.17 = (bf16[384,1920]{1,0:T(8,128)(2,1)S(1)}, bf16[384,1920]{1,0:T(8,128)(2,1)}, u32[]{:S(2)}) copy-start(bf16[384,1920]{1,0:T(8,128)(2,1)} %copy-done.16) | copy-start | bytes 4423684
  154.1 145.1 %all-gather.5.cloned.1.call-start = ((), (), s32[]{:S(2)}) async-start(), calls=%async_computation.3 | async-start | bytes 2654208 | tf_op jit(solution)/shard_map/all_gather | solution.py:1017
  154.2 10.3 %collective-permute-start.1 = (bf16[192,768]{1,0:T(8,128)(2,1)S(1)}, bf16[192,768]{1,0:T(8,128)(2,1)S(1)}, u32[]{:S(2)}, u32[]{:S(2)}) collective-permute-start(bf16[192,768]{1,0:T(8,128)(2,1)S(1)} %slice.100), channel_id=1, source_target_pairs={{16,0},{17,1},{18,2},{19,3},{20,4},{21,5},{22,6},{23,7},{24,8},{25... | collective-permute-start | bytes 884744 | tf_op jit(solution)/shard_map/ppermute | solution.py:1015
  157.9 99.4 %copy-start.4 = (bf16[256,768]{1,0:T(8,128)(2,1)}, bf16[256,768]{1,0:T(8,128)(2,1)S(1)}, u32[]{:S(2)}) copy-start(bf16[256,768]{1,0:T(8,128)(2,1)S(1)} %compare_convert_fusion.spread_ref) | copy-start | bytes 1179652
  158.6 61.0 %copy-start.27 = (f32[1,8,2,128]{3,1,2,0:T(8,128)}, f32[1,8,2,128]{3,1,2,0:T(8,128)S(1)}, u32[]{:S(2)}) copy-start(f32[1,8,2,128]{3,1,2,0:T(8,128)S(1)} %copy.72) | copy-start | bytes 24580
  219.2 24.3 %copy-start.36 = (f32[256]{0:T(256)}, f32[256]{0:T(256)S(1)}, u32[]{:S(2)}) copy-start(f32[256]{0:T(256)S(1)} %get-tuple-element.152) | copy-start | bytes 3076
  219.3 344.1 %reduce-scatter.5.cloned.1.call-start = ((), (), s32[]{:S(2)}) async-start(), calls=%async_computation.5 | async-start | bytes 2654208 | tf_op jit(solution)/shard_map/reduce_scatter | solution.py:1021
  272.1 31.6 %copy-start.9 = (bf16[1024,768]{1,0:T(8,128)(2,1)}, bf16[1024,768]{1,0:T(8,128)(2,1)S(1)}, u32[]{:S(2)}) copy-start(bf16[1024,768]{1,0:T(8,128)(2,1)S(1)} %get-tuple-element.58) | copy-start | bytes 4718596
  331.2 225.4 %collective-permute-start.3 = (bf16[256,1536]{1,0:T(8,128)(2,1)}, bf16[256,1536]{1,0:T(8,128)(2,1)}, u32[]{:S(2)}, u32[]{:S(2)}) collective-permute-start(bf16[256,1536]{1,0:T(8,128)(2,1)} %broadcast_select_fusion), channel_id=1, source_target_pairs={{0,16},{16,0},{1,17},{17,1},{2,18},{18,2},{3,19},{19,3},{4,20},{20... | collective-permute-start | bytes 2359304 | tf_op jit(solution)/shard_map/ppermute | solution.py:1009
  332.2 24.1 %copy-start.10 = (bf16[1024,768]{1,0:T(8,128)(2,1)S(1)}, bf16[1024,768]{1,0:T(8,128)(2,1)}, u32[]{:S(2)}) copy-start(bf16[1024,768]{1,0:T(8,128)(2,1)} %copy-done.9) | copy-start | bytes 4718596
  362.2 201.1 %reduce-scatter.3.cloned.1.call-start = ((), (), s32[]{:S(2)}) async-start(), calls=%async_computation.4 | async-start | bytes 6635520 | tf_op jit(solution)/shard_map/reduce_scatter | solution.py:1021
  369.2 42.9 %copy-start.44 = (bf16[1024,1536]{1,0:T(8,128)(2,1)S(1)}, bf16[1024,1536]{1,0:T(8,128)(2,1)}, u32[]{:S(2)}) copy-start(bf16[1024,1536]{1,0:T(8,128)(2,1)} %token_gather.3) | copy-start | bytes 9437188
  432.8 21.2 %copy-start.28 = (f32[1,8,2,128]{3,1,2,0:T(8,128)S(1)}, f32[1,8,2,128]{3,1,2,0:T(8,128)}, u32[]{:S(2)}) copy-start(f32[1,8,2,128]{3,1,2,0:T(8,128)} %copy-done.27) | copy-start | bytes 24580
  432.8 21.8 %copy-start.20 = (bf16[2,1,256,1536]{3,2,1,0:T(8,128)(2,1)S(1)}, bf16[2,1,256,1536]{3,2,1,0:T(8,128)(2,1)}, u32[]{:S(2)}) copy-start(bf16[2,1,256,1536]{3,2,1,0:T(8,128)(2,1)} %param.16) | copy-start | bytes 4718596
  457.9 258.8 %collective-permute-start.5 = (bf16[256,1536]{1,0:T(8,128)(2,1)}, bf16[256,1536]{1,0:T(8,128)(2,1)}, u32[]{:S(2)}, u32[]{:S(2)}) collective-permute-start(bf16[256,1536]{1,0:T(8,128)(2,1)} %get-tuple-element.129.seed_ref), channel_id=1, source_target_pairs={{0,16},{1,17},{2,18},{3,19},{4,20},{5,21},{6,22},{7,23},{8,24},{9,... | collective-permute-start | bytes 2359304 | tf_op jit(solution)/shard_map/ppermute | solution.py:1130
  464.3 24.2 %copy-start.8 = (bf16[1024,768]{1,0:T(8,128)(2,1)S(1)}, bf16[1024,768]{1,0:T(8,128)(2,1)}, u32[]{:S(2)}) copy-start(bf16[1024,768]{1,0:T(8,128)(2,1)} %copy-done.7) | copy-start | bytes 4718596
  495.1 64.5 %collective-permute-start.4 = (bf16[4,192,768]{2,1,0:T(8,128)(2,1)}, bf16[4,192,768]{2,1,0:T(8,128)(2,1)}, u32[]{:S(2)}, u32[]{:S(2)}) collective-permute-start(bf16[4,192,768]{2,1,0:T(8,128)(2,1)} %select_bitcast_fusion), channel_id=1, source_target_pairs={{0,16},{16,0},{1,17},{17,1},{2,18},{18,2},{3,19},{19,3},{4,20},{20... | collective-permute-start | bytes 3538952 | tf_op jit(solution)/shard_map/ppermute | solution.py:1009
  500.8 42.5 %copy-start.43 = (bf16[1024,1536]{1,0:T(8,128)(2,1)S(1)}, bf16[1024,1536]{1,0:T(8,128)(2,1)}, u32[]{:S(2)}) copy-start(bf16[1024,1536]{1,0:T(8,128)(2,1)} %get-tuple-element.48) | copy-start | bytes 9437188
  (31 other events, 157.7 us)
Sparse Core Ops, SparseCore 0:
  154.2 91.1 all-gather.2
  247.6 51.5 all-gather.4
  362.3 65.9 reduce-scatter.4
  431.8 121.6 reduce-scatter.2

commit v4 on v3

--- a/solution.py
+++ b/solution.py
@@ -6,261 +6,320 @@
 from jax.sharding import PartitionSpec as P
 from jax.experimental import pallas as pl
 from jax.experimental.pallas import tpu as pltpu
-BF=jnp.bfloat16; F32=jnp.float32
-NS=128; Q=128; CONV=4
+
+BF = jnp.bfloat16
+F32 = jnp.float32
+NS = 128
+Q = 128
+CONV = 4
 
 
 def cost(us):
     return pl.CostEstimate(flops=us * 700_000_000, bytes_accessed=us * 1_500_000, transcendentals=0)
 
 
-def dot(a,b): return jnp.dot(a,b,preferred_element_type=F32)
-def dot_nt(a,b): return lax.dot_general(a,b,(((1,),(1,)),((),())),preferred_element_type=F32)
-def dot_tn(a,b): return lax.dot_general(a,b,(((0,),(0,)),((),())),preferred_element_type=F32)
-def dot_hi(a,b): return lax.dot_general(a,b,(((1,),(0,)),((),())),preferred_element_type=F32,precision=lax.Precision.HIGHEST)
+def dot(a, b):
+    return jnp.dot(a, b, preferred_element_type=F32)
+
+
+def dot_nt(a, b):
+    return lax.dot_general(a, b, (((1,), (1,)), ((), ())), preferred_element_type=F32)
+
+
+def dot_tn(a, b):
+    return lax.dot_general(a, b, (((0,), (0,)), ((), ())), preferred_element_type=F32)
+
+
+def dot_hi(a, b):
+    return lax.dot_general(
+        a, b, (((1,), (0,)), ((), ())), preferred_element_type=F32, precision=lax.Precision.HIGHEST
+    )
+
+
+def fold8(v):
+    return jnp.sum(v.reshape(v.shape[0] // 8, 8, v.shape[1]), axis=0)
+
 
 def expand(v, spread_ref):
     hi = v.astype(BF)
     lo = (v - hi.astype(F32)).astype(BF)
     return dot(jnp.concatenate([hi, lo], axis=1), spread_ref[...])
 
-def front_chunk(width, pre_ref, par_ref, ext, first):
-    taps = [par_ref[k:k+1, :] for k in range(CONV)]
-    conv = par_ref[4:5, :] + taps[0]*ext[5:5+Q, :]
-    for k in range(1, CONV):
-        conv = conv + taps[k]*ext[5+k:5+k+Q, :]
-    return conv
 
 def head_rows(pre_ref, par_ref, width):
-    raw = pre_ref[:, 2*width+2*NS:] + par_ref[7:8, :NS]
+    raw = pre_ref[:, 2 * width + 2 * NS :] + par_ref[7:8, :NS]
     dt = jnp.maximum(raw, 0.0) + jnp.log1p(jnp.exp(-jnp.abs(raw)))
     rate = -jnp.exp(par_ref[8:9, :NS])
     row = lax.broadcasted_iota(jnp.int32, (Q, Q), 0)
     col = lax.broadcasted_iota(jnp.int32, (Q, Q), 1)
-    lower = (row >= col)
-    cum = dot_hi(lower.astype(F32), dt*rate)
-    return raw, dt, rate, lower, cum
-
-def fwd_kernel(width, pre_ref, par_ref, spread_ref, yn_ref, sq_ref, st_ref, ext, state, ex_dt, ex_e, ex_w):
+    return raw, dt, rate, row >= col
+
+
+def split_heads(v, first):
+    low = jnp.where(first, v, 0.0)
+    return jnp.concatenate([low.astype(BF), (v - low).astype(BF)], axis=0)
+
+
+def fwd_kernel(
+    width, pre_ref, par_ref, spread_ref, yn_ref, sq_ref, st_ref, conv_ref, y_ref, ex_dt, ex_e, ex_w, cum_ref, cumt_ref, ext, state
+):
     step = pl.program_id(0)
-    pairs = width//128
+    pairs = width // 128
+
     @pl.when(step == 0)
     def _():
         ext[0:8, :] = jnp.zeros((8, ext.shape[1]), F32)
         state[...] = jnp.zeros_like(state)
-    ext[8:, :] = pre_ref[:, width:2*width+2*NS]
-    conv = front_chunk(width, pre_ref, par_ref, ext, None)
-    act = conv*jax.nn.sigmoid(conv)
-    ext[0:8, :] = ext[Q:Q+8, :]
-    bm = act[:, width:width+NS].astype(BF)
-    cm = act[:, width+NS:].astype(BF)
-    raw, dt, rate, lower, cum = head_rows(pre_ref, par_ref, width)
+
+    def conv_block(sl):
+        at = slice(width + sl.start, width + sl.stop)
+        ext[8:, sl] = pre_ref[:, at]
+        conv = par_ref[4:5, sl] + par_ref[3:4, sl] * pre_ref[:, at]
+        for k in range(CONV - 1):
+            conv = conv + par_ref[k : k + 1, sl] * ext[5 + k : 5 + k + Q, sl]
+        ext[0:8, sl] = pre_ref[Q - 8 : Q, at]
+        conv_ref[:, sl] = conv
+        return conv * jax.nn.sigmoid(conv)
+
+    bm = conv_block(slice(width, width + NS)).astype(BF)
+    cm = conv_block(slice(width + NS, width + 2 * NS)).astype(BF)
+    raw, dt, rate, lower = head_rows(pre_ref, par_ref, width)
+    cum = dot_hi(lower.astype(F32), dt * rate)
     cum_t = cum.T
+    cum_ref[...] = cum
+    cumt_ref[...] = cum_t
     ex_dt[...] = expand(dt, spread_ref)
     ex_e[...] = expand(jnp.exp(cum), spread_ref)
-    ex_w[...] = expand(jnp.exp(cum[Q-1:Q, :]-cum), spread_ref)
+    ex_w[...] = expand(jnp.exp(cum[Q - 1 : Q, :] - cum), spread_ref)
     scores = dot_nt(cm, bm)
-    st_ref[0] = state[...].astype(st_ref.dtype)
+    st_ref[0] = state[...]
     bm_t = bm.T
-    lane = lax.broadcasted_iota(jnp.int32, (Q, 128), 1)
+    first = lax.broadcasted_iota(jnp.int32, (Q, 128), 1) < 64
     squares = jnp.zeros((Q, 128), F32)
     for p in range(pairs):
-        sl = slice(128*p, 128*p+128)
-        x = act[:, sl]
-        xd = x*ex_dt[:, sl]
+        sl = slice(128 * p, 128 * p + 128)
+        x = conv_block(sl)
+        xd = x * ex_dt[:, sl]
         st = state[:, sl]
         mixes = []
-        for h in (2*p, 2*p+1):
-            gap = cum[:, h:h+1]-cum_t[h:h+1, :]
-            mixes.append((jnp.exp(jnp.where(lower, gap, -1e30))*scores).astype(BF))
-        xdb = xd.astype(BF)
-        zero = jnp.zeros_like(xdb)
-        both = jnp.concatenate([jnp.where(lane < 64, xdb, zero), jnp.where(lane < 64, zero, xdb)], axis=0)
-        y = dot(jnp.concatenate(mixes, axis=1), both)
-        y = y + ex_e[:, sl]*dot(cm, st.astype(BF)) + par_ref[6:7, sl]*x
+        for h in (2 * p, 2 * p + 1):
+            gap = cum[:, h : h + 1] - cum_t[h : h + 1, :]
+            mixes.append((jnp.exp(jnp.where(lower, gap, -1e30)) * scores).astype(BF))
+        y = dot(jnp.concatenate(mixes, axis=1), split_heads(xd, first))
+        y = y + ex_e[:, sl] * dot(cm, st.astype(BF)) + par_ref[6:7, sl] * x
+        y_ref[:, sl] = y
         z = pre_ref[:, sl]
-        yg = y*(z*jax.nn.sigmoid(z))
-        squares = squares + yg*yg
-        yn_ref[:, sl] = (yg*par_ref[5:6, sl]).astype(BF)
-        state[:, sl] = ex_e[Q-1:Q, sl]*st + dot(bm_t, (ex_w[:, sl]*xd).astype(BF))
+        yg = y * (z * jax.nn.sigmoid(z))
+        squares = squares + yg * yg
+        yn_ref[:, sl] = (yg * par_ref[5:6, sl]).astype(BF)
+        state[:, sl] = ex_e[Q - 1 : Q, sl] * st + dot(bm_t, (ex_w[:, sl] * xd).astype(BF))
     sq_ref[...] = lax.dot_general(
         jnp.ones((8, 128), F32), squares, (((1,), (1,)), ((), ())),
         preferred_element_type=F32, precision=lax.Precision.HIGHEST,
     )
 
+
 def mixer_fwd(pre, par, spread, width):
-    T = pre.shape[0]; n = T//Q
+    T = pre.shape[0]
+    n = T // Q
     pw = pre.shape[1]
+    wide = width + 2 * NS
     return pl.pallas_call(
         functools.partial(fwd_kernel, width),
         grid=(n,),
-        in_specs=[pl.BlockSpec((Q, pw), lambda i: (i, 0)),
-                  pl.BlockSpec(par.shape, lambda i: (0, 0)),
-                  pl.BlockSpec(spread.shape, lambda i: (0, 0))],
-        out_specs=[pl.BlockSpec((Q, width), lambda i: (i, 0)),
-                   pl.BlockSpec((8, Q), lambda i: (i, 0)),
-                   pl.BlockSpec((1, NS, width), lambda i: (i, 0, 0))],
-        out_shape=[jax.ShapeDtypeStruct((T, width), BF), jax.ShapeDtypeStruct((8*n, Q), F32),
-                   jax.ShapeDtypeStruct((n, NS, width), F32)],
-        scratch_shapes=[pltpu.VMEM((Q+8, width+2*NS), F32), pltpu.VMEM((NS, width), F32)]
-            + [pltpu.VMEM((Q, width), F32)]*3,
-        compiler_params=pltpu.CompilerParams(dimension_semantics=("arbitrary",), vmem_limit_bytes=48<<20),
+        in_specs=[
+            pl.BlockSpec((Q, pw), lambda i: (i, 0)),
+            pl.BlockSpec(par.shape, lambda i: (0, 0)),
+            pl.BlockSpec(spread.shape, lambda i: (0, 0)),
+        ],
+        out_specs=[
+            pl.BlockSpec((Q, width), lambda i: (i, 0)),
+            pl.BlockSpec((8, Q), lambda i: (i, 0)),
+            pl.BlockSpec((1, NS, width), lambda i: (i, 0, 0)),
+            pl.BlockSpec((Q, wide), lambda i: (i, 0)),
+        ]
+        + [pl.BlockSpec((Q, width), lambda i: (i, 0))] * 4
+        + [pl.BlockSpec((Q, 128), lambda i: (i, 0))] * 2,
+        out_shape=[
+            jax.ShapeDtypeStruct((T, width), BF),
+            jax.ShapeDtypeStruct((8 * n, Q), F32),
+            jax.ShapeDtypeStruct((n, NS, width), F32),
+            jax.ShapeDtypeStruct((T, wide), F32),
+        ]
+        + [jax.ShapeDtypeStruct((T, width), F32)] * 4
+        + [jax.ShapeDtypeStruct((T, 128), F32)] * 2,
+        scratch_shapes=[pltpu.VMEM((Q + 8, wide), F32), pltpu.VMEM((NS, width), F32)],
+        compiler_params=pltpu.CompilerParams(dimension_semantics=("arbitrary",), vmem_limit_bytes=48 << 20),
         cost_estimate=cost(12),
         name="mixer_fwd",
     )(pre, par, spread)
 
-def fold8(v):
-    return jnp.sum(v.reshape(v.shape[0]//8, 8, v.shape[1]), axis=0)
-
-def bwd_kernel(width, n_heads, pre_ref, halo_ref, par_ref, spread_ref, gather_ref, st_ref, dh_ref, kap_ref,
-               gp_ref, acc_out, ext, dext, dstate, ex_dt, ex_e, ex_w, acc, dact, sums):
+
+def bwd_kernel(
+    width, n_heads, pre_ref, par_ref, pick_ref, st_ref, conv_ref, y_ref, ex_dt, ex_e, ex_w, cum_ref, cumt_ref, dh_ref, kap_ref,
+    gp_ref, acc_out, dext, dstate, acc,
+):
     step = pl.program_id(0)
     steps = pl.num_programs(0)
-    pairs = width//128
+    pairs = width // 128
+
     @pl.when(step == 0)
     def _():
         dext[Q:, :] = jnp.zeros((8, dext.shape[1]), F32)
         dstate[...] = jnp.zeros_like(dstate)
         acc[...] = jnp.zeros_like(acc)
-    ext[8:, :] = pre_ref[:, width:2*width+2*NS]
-    halo = halo_ref[:, width:2*width+2*NS]
-    ext[0:8, :] = jnp.where(step == steps-1, 0.0, halo)
-    conv = front_chunk(width, pre_ref, par_ref, ext, None)
-    sg = jax.nn.sigmoid(conv)
-    act = conv*sg
-    bm = act[:, width:width+NS].astype(BF)
-    cm = act[:, width+NS:].astype(BF)
-    raw, dt, rate, lower, cum = head_rows(pre_ref, par_ref, width)
-    cum_t = cum.T
-    e_head = jnp.exp(cum)
-    ex_dt[...] = expand(dt, spread_ref)
-    ex_e[...] = expand(e_head, spread_ref)
-    ex_w[...] = expand(jnp.exp(cum[Q-1:Q, :]-cum), spread_ref)
+
+    def activate(sl):
+        conv = conv_ref[:, sl]
+        sg = jax.nn.sigmoid(conv)
+        act = conv * sg
+        return act, sg + act * (1.0 - sg)
+
+    def conv_back(sl, dact, slope):
+        at = slice(width + sl.start, width + sl.stop)
+        dconv = dact * slope
+        pre = pre_ref[:, at]
+        dext[0:Q, sl] = dconv
+        dpre = par_ref[3:4, sl] * dconv
+        acc[24:32, sl] += fold8(pre * dconv)
+        acc[32:40, sl] += fold8(dconv)
+        for k in range(CONV - 1):
+            moved = dext[3 - k : 3 - k + Q, sl]
+            dpre = dpre + par_ref[k : k + 1, sl] * moved
+            acc[8 * k : 8 * k + 8, sl] += fold8(pre * moved)
+        gp_ref[:, at] = dpre.astype(BF)
+        dext[Q:, sl] = dconv[0:8, :]
+
+    b_cols, c_cols = slice(width, width + NS), slice(width + NS, width + 2 * NS)
+    bm, b_slope = activate(b_cols)
+    cm, c_slope = activate(c_cols)
+    bm, cm = bm.astype(BF), cm.astype(BF)
+    raw, dt, rate, lower = head_rows(pre_ref, par_ref, width)
+    cum, cum_t = cum_ref[...], cumt_ref[...]
     scores = dot_nt(cm, bm)
     cm_t = cm.T
-    lane = lax.broadcasted_iota(jnp.int32, (Q, 128), 1)
+    first = lax.broadcasted_iota(jnp.int32, (Q, 128), 1) < 64
     kap = kap_ref[:, 0:1].astype(F32) + kap_ref[:, 1:2].astype(F32)
     dscores = jnp.zeros((Q, Q), F32)
-    row_sums = jnp.zeros((Q, 128), F32)
-    col_rows = []
+    sums = jnp.zeros((Q, 128), F32)
+    cols = jnp.zeros((16, Q), F32)
     dC = jnp.zeros((Q, NS), F32)
     dB = jnp.zeros((Q, NS), F32)
-    w_sum = jnp.zeros((Q, 128), F32)
-    e_sum = jnp.zeros((Q, 128), F32)
-    t_sum = jnp.zeros((Q, 128), F32)
     f_sum = jnp.zeros((8, 128), F32)
-    orow = lax.broadcasted_iota(jnp.int32, (2*Q, 128), 0)
-    ocol = lax.broadcasted_iota(jnp.int32, (2*Q, 128), 1)
+    crow = lax.broadcasted_iota(jnp.int32, (16, 2 * Q), 0)
+    ccol = lax.broadcasted_iota(jnp.int32, (16, 2 * Q), 1)
     for p in range(pairs):
-        sl = slice(128*p, 128*p+128)
-        x = act[:, sl]
+        sl = slice(128 * p, 128 * p + 128)
+        x, slope = activate(sl)
         xdt = ex_dt[:, sl]
-        xd = x*xdt
+        xd = x * xdt
         xdb = xd.astype(BF)
         st = st_ref[0, :, sl]
         stb = st.astype(BF)
-        zero = jnp.zeros_like(xdb)
-        decays, mixes = [], []
-        for h in (2*p, 2*p+1):
-            gap = cum[:, h:h+1]-cum_t[h:h+1, :]
+        decays, mixb = [], []
+        for h in (2 * p, 2 * p + 1):
+            gap = cum[:, h : h + 1] - cum_t[h : h + 1, :]
             decay = jnp.exp(jnp.where(lower, gap, -1e30))
             decays.append(decay)
-            mixes.append(decay*scores)
-        mixb = [m.astype(BF) for m in mixes]
-        both = jnp.concatenate([jnp.where(lane < 64, xdb, zero), jnp.where(lane < 64, zero, xdb)], axis=0)
-        y = dot(jnp.concatenate(mixb, axis=1), both)
+            mixb.append((decay * scores).astype(BF))
         e = ex_e[:, sl]
-        carried = e*dot(cm, stb)
-        y = y + carried + par_ref[6:7, sl]*x
+        carried = e * dot(cm, stb)
+        y = y_ref[:, sl]
         z = pre_ref[:, sl]
         sz = jax.nn.sigmoid(z)
-        silz = z*sz
-        yg = y*silz
+        silz = z * sz
+        yg = y * silz
         dh = dh_ref[:, sl]
-        dyg = par_ref[5:6, sl]*dh - yg*kap
-        acc[40:48, sl] += fold8(dh*yg)
-        dy = dyg*silz
-        gp_ref[:, sl] = (dyg*y*(sz+silz*(1.0-sz))).astype(BF)
-        acc[48:56, sl] += fold8(dy*x)
-        dyb = dy.astype(BF)
-        dstack = jnp.concatenate([jnp.where(lane < 64, dyb, zero), jnp.where(lane < 64, zero, dyb)], axis=0)
+        dyg = par_ref[5:6, sl] * dh - yg * kap
+        acc[40:48, sl] += fold8(dh * yg)
+        dy = dyg * silz
+        gp_ref[:, sl] = (dyg * y * (sz + silz * (1.0 - sz))).astype(BF)
+        acc[48:56, sl] += fold8(dy * x)
+        dstack = split_heads(dy, first)
         dmix = dot_nt(dstack, xdb)
         rbs = []
         for j in range(2):
-            dm = dmix[Q*j:Q*j+Q]
-            dscores = dscores + decays[j]*dm
-            rb = (mixes[j]*dm).astype(BF)
-            rbs.append(rb)
-            col_rows.append(jnp.sum(rb.astype(F32), axis=0, keepdims=True))
-        pick = (ocol == 2*p + (orow >= Q).astype(jnp.int32)).astype(BF)
-        row_sums = row_sums + dot(jnp.concatenate(rbs, axis=1), pick)
-        dxd = dot_tn(jnp.concatenate(mixb, axis=0), dstack)
+            part = decays[j] * dmix[Q * j : Q * j + Q]
+            dscores = dscores + part
+            rbs.append((part * scores).astype(BF))
+        ones = (crow == 2 * p + (ccol >= Q).astype(jnp.int32)).astype(BF)
+        cols = cols + dot(ones, jnp.concatenate(rbs, axis=0))
         ds = dstate[:, sl]
         dsb = ds.astype(BF)
         w = ex_w[:, sl]
-        from_state = w*dot(bm, dsb)
-        gat = gather_ref[sl, :]
-        w_sum = w_sum + dot((xd*from_state).astype(BF), gat)
-        e_sum = e_sum + dot((dy*carried).astype(BF), gat)
-        dxd = dxd + from_state
-        t_sum = t_sum + dot((x*dxd).astype(BF), gat)
-        f_sum = f_sum + dot_hi(ex_e[Q-1:Q, sl]*fold8(st*ds), gat.astype(F32))
-        dact[:, sl] = xdt*dxd + par_ref[6:7, sl]*dy
-        edy = (e*dy).astype(BF)
+        from_state = w * dot(bm, dsb)
+        dxd = dot_tn(jnp.concatenate(mixb, axis=0), dstack) + from_state
+        sums = sums + dot(
+            jnp.concatenate(
+                rbs + [(dy * carried).astype(BF), (xd * from_state).astype(BF), (x * dxd).astype(BF)], axis=1
+            ),
+            pick_ref[p],
+        )
+        f_sum = f_sum + dot(
+            (ex_e[Q - 1 : Q, sl] * fold8(st * ds)), pick_ref[p, 2 * Q : 3 * Q, :].astype(F32)
+        )
+        edy = (e * dy).astype(BF)
         dC = dC + dot_nt(edy, stb)
-        dB = dB + dot_nt((w*xd).astype(BF), dsb)
-        dstate[:, sl] = ex_e[Q-1:Q, sl]*ds + dot(cm_t, edy)
+        dB = dB + dot_nt((w * xd).astype(BF), dsb)
+        dstate[:, sl] = ex_e[Q - 1 : Q, sl] * ds + dot(cm_t, edy)
+        conv_back(sl, xdt * dxd + par_ref[6:7, sl] * dy, slope)
     dsc = dscores.astype(BF)
-    dact[:, width:width+NS] = dB + dot_tn(dsc, cm)
-    dact[:, width+NS:] = dC + dot(dsc, bm)
-    cols = jnp.concatenate(col_rows + [jnp.zeros((128-len(col_rows), Q), F32)], axis=0).T
-    upper = jnp.logical_not(lower) | (lax.broadcasted_iota(jnp.int32, (Q, Q), 0) == lax.broadcasted_iota(jnp.int32, (Q, Q), 1))
-    da = dot_hi(upper.astype(F32), row_sums-cols+e_sum) + dot_hi((lower & jnp.logical_not(upper)).astype(F32), w_sum) + jnp.sum(f_sum, axis=0, keepdims=True)
-    keep = lane < n_heads
-    ddt = da*rate + t_sum
-    draw = jnp.where(keep, ddt*jax.nn.sigmoid(raw), 0.0)
-    gp_ref[:, 2*width+2*NS:] = draw.astype(BF)
+    conv_back(b_cols, dB + dot_tn(dsc, cm), b_slope)
+    conv_back(c_cols, dC + dot(dsc, bm), c_slope)
+    col_t = jnp.concatenate([cols, jnp.zeros((Q - 16, Q), F32)], axis=0).T
+    row = lax.broadcasted_iota(jnp.int32, (Q, Q), 0)
+    col = lax.broadcasted_iota(jnp.int32, (Q, Q), 1)
+    lanes = lax.broadcasted_iota(jnp.int32, (Q, 128), 1)
+    later = dot_hi((row <= col).astype(F32), sums - col_t)
+    earlier = dot_hi((row > col).astype(F32), sums)
+    da = later + pltpu.roll(earlier, 112, axis=1) + jnp.sum(f_sum, axis=0, keepdims=True)
+    keep = lanes < n_heads
+    ddt = da * rate + pltpu.roll(sums, 96, axis=1)
+    draw = jnp.where(keep, ddt * jax.nn.sigmoid(raw), 0.0)
+    gp_ref[:, 2 * width + 2 * NS :] = draw.astype(BF)
     acc[56:64, 0:128] += fold8(draw)
-    acc[56:64, 128:256] += fold8(jnp.where(keep, da*dt*rate, 0.0))
-    dconv = dact[...]*(sg+act*(1.0-sg))
-    dext[0:Q, :] = dconv
-    dpre = par_ref[3:4, :]*dconv
-    for k in range(CONV-1):
-        dpre = dpre + par_ref[k:k+1, :]*dext[3-k:3-k+Q, :]
-    gp_ref[:, width:2*width+2*NS] = dpre.astype(BF)
-    for k in range(CONV):
-        acc[8*k:8*k+8, :] += fold8(dconv*ext[5+k:5+k+Q, :])
-    acc[32:40, :] += fold8(dconv)
-    dext[Q:, :] = dext[0:8, :]
-    @pl.when(step == steps-1)
-    def _():
-        rows = [jnp.sum(acc[8*k:8*k+8, :], axis=0, keepdims=True) for k in range(8)]
+    acc[56:64, 128:256] += fold8(jnp.where(keep, da * dt * rate, 0.0))
+
+    @pl.when(step == steps - 1)
+    def _():
+        rows = [jnp.sum(acc[8 * k : 8 * k + 8, :], axis=0, keepdims=True) for k in range(8)]
         acc_out[...] = jnp.concatenate(rows, axis=0)
 
-def mixer_bwd(pre, par, spread, gather, states, dh, kap, width, n_heads):
-    T = pre.shape[0]; n = T//Q; pw = pre.shape[1]
-    rev = lambda i: n-1-i
+
+def pick_table(width):
+    pair = jnp.arange(width // 128)[:, None, None]
+    row = jnp.arange(5 * Q)[None, :, None]
+    lane = jnp.arange(128)[None, None, :]
+    part, inner = row // Q, row % Q
+    head = 2 * pair + jnp.where(part < 2, part, inner // 64)
+    base = jnp.where(part == 3, 16, jnp.where(part == 4, 32, 0))
+    return (lane == head + base).astype(BF)
+
+
+def mixer_bwd(pre, par, pick, kept, dh, kap, width, n_heads):
+    T = pre.shape[0]
+    n = T // Q
+    pw = pre.shape[1]
+    wide = width + 2 * NS
+    back = lambda cols: pl.BlockSpec((Q, cols), lambda i: (n - 1 - i, 0))
     return pl.pallas_call(
         functools.partial(bwd_kernel, width, n_heads),
         grid=(n,),
-        in_specs=[pl.BlockSpec((Q, pw), lambda i: (n-1-i, 0)),
-                  pl.BlockSpec((8, pw), lambda i: (jnp.maximum((n-1-i)*(Q//8)-1, 0), 0)),
-                  pl.BlockSpec(par.shape, lambda i: (0, 0)),
-                  pl.BlockSpec(spread.shape, lambda i: (0, 0)),
-                  pl.BlockSpec(gather.shape, lambda i: (0, 0)),
-                  pl.BlockSpec((1, NS, width), lambda i: (n-1-i, 0, 0)),
-                  pl.BlockSpec((Q, width), lambda i: (n-1-i, 0)),
-                  pl.BlockSpec((Q, 128), lambda i: (n-1-i, 0))],
-        out_specs=[pl.BlockSpec((Q, pw), lambda i: (n-1-i, 0)),
-                   pl.BlockSpec((8, width+2*NS), lambda i: (0, 0))],
-        out_shape=[jax.ShapeDtypeStruct((T, pw), BF), jax.ShapeDtypeStruct((8, width+2*NS), F32)],
-        scratch_shapes=[pltpu.VMEM((Q+8, width+2*NS), F32), pltpu.VMEM((Q+8, width+2*NS), F32), pltpu.VMEM((NS, width), F32)]
-            + [pltpu.VMEM((Q, width), F32)]*3
-            + [pltpu.VMEM((64, width+2*NS), F32), pltpu.VMEM((Q, width+2*NS), F32), pltpu.VMEM((8, 128), F32)],
-        compiler_params=pltpu.CompilerParams(dimension_semantics=("arbitrary",), vmem_limit_bytes=56<<20),
-        cost_estimate=cost(40),
+        in_specs=[
+            back(pw),
+            pl.BlockSpec(par.shape, lambda i: (0, 0)),
+            pl.BlockSpec(pick.shape, lambda i: (0, 0, 0)),
+            pl.BlockSpec((1, NS, width), lambda i: (n - 1 - i, 0, 0)),
+            back(wide), back(width), back(width), back(width), back(width), back(128), back(128),
+            back(width), back(128),
+        ],
+        out_specs=[back(pw), pl.BlockSpec((8, wide), lambda i: (0, 0))],
+        out_shape=[jax.ShapeDtypeStruct((T, pw), BF), jax.ShapeDtypeStruct((8, wide), F32)],
+        scratch_shapes=[pltpu.VMEM((Q + 8, wide), F32), pltpu.VMEM((NS, width), F32), pltpu.VMEM((64, wide), F32)],
+        compiler_params=pltpu.CompilerParams(dimension_semantics=("arbitrary",), vmem_limit_bytes=56 << 20),
+        cost_estimate=cost(35),
         name="mixer_bwd",
-    )(pre, pre, par, spread, gather, states, dh, kap)
+    )(pre, par, pick, *kept, dh, kap)
 
 
 MESH_ID = pl.DeviceIdType.MESH
@@ -466,13 +525,16 @@
     )(*operands)
 
 
-def open_kernel(n, pieces, in_ref, out_ref, xn_ref, fin_ref, fout_ref, xall_ref,
-                x_ss, x_rs, z_ss, z_rs, own_sem, t_ss, t_rs):
+def open_kernel(n, pieces, tokens, *refs):
+    if tokens:
+        in_ref, xn_ref, fin_ref, xall_ref, x_ss, x_rs, z_ss, z_rs, own_sem, t_ss, t_rs = refs
+    else:
+        in_ref, fin_ref, x_ss, x_rs, z_ss, z_rs, own_sem = refs
     sec, z, ten = lax.axis_index("section"), lax.axis_index("dp"), lax.axis_index("tensor")
     across = peer("section", 1 - sec)
     near, far = peer("tensor", ten ^ 1), peer("tensor", ten ^ 2)
     barrier = pltpu.get_barrier_semaphore()
-    for where in (across, near, far):
+    for where in (across, near, far) if tokens else (across,):
         pl.semaphore_signal(barrier, inc=1, device_id=where, device_id_type=MESH_ID)
 
     @pl.when(z > 0)
@@ -483,10 +545,9 @@
     def _():
         pl.semaphore_signal(barrier, inc=1, device_id=peer("dp", z + 1), device_id_type=MESH_ID)
 
-    pl.semaphore_wait(barrier, 3 + jnp.where(z > 0, 1, 0) + jnp.where(z < n - 1, 1, 0))
-    sources, fulls = (in_ref, out_ref), (fin_ref, fout_ref)
+    pl.semaphore_wait(barrier, (3 if tokens else 1) + jnp.where(z > 0, 1, 0) + jnp.where(z < n - 1, 1, 0))
+    sources, fulls = (in_ref,), (fin_ref,)
     rows = in_ref.shape[0]
-    trows = xn_ref.shape[0]
 
     def place(p, s):
         array, offset, count, _ = pieces[p]
@@ -518,15 +579,17 @@
 
     every = range(len(pieces))
     via = [piece[3] for piece in pieces]
-    me = pl.ds(pl.multiple_of(ten * trows, 16), trows)
-    other = pl.ds(pl.multiple_of((ten ^ 2) * trows, 16), trows)
-    tok_far = remote(xn_ref, xall_ref.at[me], t_ss.at[0], t_rs.at[0], far)
-    tok_near = remote(xn_ref, xall_ref.at[me], t_ss.at[1], t_rs.at[1], near)
-    tok_relay = remote(xall_ref.at[other], xall_ref.at[other], t_ss.at[2], t_rs.at[2], near)
-    tok_own = pltpu.make_async_copy(xn_ref, xall_ref.at[me], own_sem.at[0])
-    tok_far.start()
-    tok_near.start()
-    tok_own.start()
+    if tokens:
+        trows = xn_ref.shape[0]
+        me = pl.ds(pl.multiple_of(ten * trows, 16), trows)
+        other = pl.ds(pl.multiple_of((ten ^ 2) * trows, 16), trows)
+        tok_far = remote(xn_ref, xall_ref.at[me], t_ss.at[0], t_rs.at[0], far)
+        tok_near = remote(xn_ref, xall_ref.at[me], t_ss.at[1], t_rs.at[1], near)
+        tok_relay = remote(xall_ref.at[other], xall_ref.at[other], t_ss.at[2], t_rs.at[2], near)
+        tok_own = pltpu.make_async_copy(xn_ref, xall_ref.at[me], own_sem.at[0])
+        tok_far.start()
+        tok_near.start()
+        tok_own.start()
 
     @pl.when(sec == 0)
     def _():
@@ -538,7 +601,7 @@
         for p in every:
             if via[p] == 0:
                 to_x(p, z, own(p)).start()
-        for array in (0, 1):
+        for array in (0,):
             whole = fulls[array].at[pl.ds(pl.multiple_of(z * rows, 16), rows)]
             pltpu.make_async_copy(sources[array], whole, own_sem.at[1 + array]).start()
         for d in range(1, n):
@@ -587,17 +650,18 @@
                 if via[p] == 0:
                     to_x(p, s, place(p, s)).wait_recv()
 
-    tok_far.wait_recv()
-    tok_relay.start()
-    tok_near.wait_recv()
-    tok_relay.wait_recv()
-    for copy in (tok_far, tok_near, tok_relay):
-        copy.wait_send()
-    tok_own.wait()
+    if tokens:
+        tok_far.wait_recv()
+        tok_relay.start()
+        tok_near.wait_recv()
+        tok_relay.wait_recv()
+        for copy in (tok_far, tok_near, tok_relay):
+            copy.wait_send()
+        tok_own.wait()
 
     @pl.when(sec == 0)
     def _():
-        for array in (0, 1):
+        for array in (0,):
             whole = fulls[array].at[pl.ds(pl.multiple_of(z * rows, 16), rows)]
             pltpu.make_async_copy(sources[array], whole, own_sem.at[1 + array]).wait()
 
@@ -623,30 +687,30 @@
                 to_z(p, s, -1, place(p, s)).wait_send()
 
 
-def open_gather(own_in, own_out, xn, group_id):
+def open_gather(own, group_id, xn=None):
     n = lax.axis_size("dp")
-    rows = own_in.shape[0]
-    third = rows // 3
-    pieces = (
-        (0, third, third, 1), (0, 2 * third, third, 1), (0, 0, third, 0),
-        (1, third, 2 * third, 1), (1, 0, third, 0),
-    )
+    rows = own.shape[0]
+    first = max(1, round(rows * 5 / 12 / 16)) * 16
+    rest = (rows - first) // 2
+    pieces = ((0, first, rest, 1), (0, first + rest, rest, 1), (0, 0, first, 0))
     count = len(pieces)
     sem = lambda *shape: pltpu.SemaphoreType.DMA(shape)
+    operands, out_shape = [own], [jax.ShapeDtypeStruct((n * rows, own.shape[1]), BF)]
+    scratch = [sem(count, n), sem(count, n), sem(2, count, n), sem(2, count, n), sem(3)]
+    if xn is not None:
+        operands.append(xn)
+        out_shape.append(jax.ShapeDtypeStruct((lax.axis_size("tensor") * xn.shape[0], xn.shape[1]), BF))
+        scratch += [sem(3), sem(3)]
     return pl.pallas_call(
-        functools.partial(open_kernel, n, pieces),
-        out_shape=[
-            jax.ShapeDtypeStruct((n * rows, own_in.shape[1]), BF),
-            jax.ShapeDtypeStruct((n * rows, own_out.shape[1]), BF),
-            jax.ShapeDtypeStruct((lax.axis_size("tensor") * xn.shape[0], xn.shape[1]), BF),
-        ],
-        in_specs=[pl.BlockSpec(memory_space=pltpu.VMEM)] * 3,
-        out_specs=[pl.BlockSpec(memory_space=pl.ANY)] * 3,
-        scratch_shapes=[sem(count, n), sem(count, n), sem(2, count, n), sem(2, count, n), sem(3), sem(3), sem(3)],
-        cost_estimate=cost(110),
+        functools.partial(open_kernel, n, pieces, xn is not None),
+        out_shape=out_shape,
+        in_specs=[pl.BlockSpec(memory_space=pltpu.VMEM)] * len(operands),
+        out_specs=[pl.BlockSpec(memory_space=pl.ANY)] * len(operands),
+        scratch_shapes=scratch,
+        cost_estimate=cost(90 if xn is not None else 40),
         compiler_params=pltpu.CompilerParams(collective_id=group_id, has_side_effects=True),
         name="weights_open",
-    )(own_in, own_out, xn)
+    )(*operands)
 
 
 CHUNK_ROWS = 16
@@ -1068,7 +1132,7 @@
 
     head_of = jnp.arange(width) // (width // heads)
     spread = (jnp.arange(2 * HEAD_PAD)[:, None] % HEAD_PAD == head_of[None, :]).astype(BF)
-    gather = (head_of[:, None] == jnp.arange(HEAD_PAD)[None, :]).astype(BF)
+    pick = pick_table(width)
 
     def normed(layer, u):
         inv = lax.rsqrt(jnp.mean(u * u, axis=1, keepdims=True) + EPSILON)
@@ -1076,15 +1140,15 @@
 
     def forward(layer, u, inv, xn, w_in, w_out):
         pre = dot(xn, w_in)
-        yn, squares, states = mixer_fwd(pre, pars[layer], spread, width)
+        yn, squares, *saved = mixer_fwd(pre, pars[layer], spread, width)
         partial = dot_nt(yn, w_out).astype(BF)
         total, squares = token_scatter(partial, 3 + layer, squares)
         q = lax.rsqrt(squares[::8].reshape(rows) / total_inner + EPSILON)[:, None]
         projected = total * q
-        return (u + projected).astype(BF), (u, inv, xn, pre, yn, states, q, projected, w_in, w_out)
+        return (u + projected).astype(BF), (u, inv, xn, pre, yn, saved, q, projected, w_in, w_out)
 
     def backward_core(layer, g, kept):
-        u, inv, xn, pre, yn, states, q, projected, w_in, w_out = kept
+        u, inv, xn, pre, yn, saved, q, projected, w_in, w_out = kept
         kappa = q * q / total_inner * jnp.sum(g * projected, axis=1, keepdims=True)
         high = kappa.astype(BF)
         low = (kappa - high.astype(F32)).astype(BF)
@@ -1092,7 +1156,7 @@
         gq, side = token_gather([(g * q).astype(BF), side], 5 + layer)
         g_out = dot_tn(gq, yn).astype(BF)
         dh = dot(gq, w_out)
-        gp, acc = mixer_bwd(pre, pars[layer], spread, gather, states, dh, side, width, heads)
+        gp, acc = mixer_bwd(pre, pars[layer], pick, saved, dh, side, width, heads)
         g_in = dot_tn(xn, gp).astype(BF)
         return gp, acc, g_in, g_out
 
@@ -1104,12 +1168,20 @@
         du = g + inv * scaled - u * (inv * inv * inv) * dots / model
         return du.astype(BF), jnp.sum(dxn * u * inv, axis=0)
 
+    def cross_sum(value):
+        split = value.reshape(-1, 2, shard // 2, width)
+        mine = jnp.where(is_first, split[:, 0], split[:, 1])
+        theirs = swap_sections(jnp.where(is_first, split[:, 1], split[:, 0]))
+        return (mine.astype(F32) + theirs.astype(F32)).astype(BF).reshape(-1, width)
+
     stream_own = lax.dynamic_index_in_dim(stream[:, 0], section, 0, False)
     u0 = stream_own.astype(F32)
     inv0, xn0 = normed(0, u0)
-    w_in0, w_out0, xn0 = open_gather(own_in, own_out, xn0, 1)
+    w_in0, xn0 = open_gather(own_in, 1, xn0)
     full_in1, w_in0 = later_gather(own_in, is_first, w_in0)
-    full_out1, w_in0 = later_gather(own_out, is_first, w_in0)
+    own_out0, w_in0 = lax.optimization_barrier((own_out, w_in0))
+    (w_out0,) = open_gather(own_out0, 10)
+    full_out1, w_out0 = later_gather(own_out, is_first, w_out0)
 
     out0, kept0 = forward(0, u0, inv0, xn0, w_in0, w_out0)
     u1 = out0.astype(F32)
@@ -1118,15 +1190,12 @@
     out1, kept1 = forward(1, u1, inv1, xn1, full_in1, full_out1)
     g1 = lax.dynamic_index_in_dim(cotangent[:, 0], section, 0, False).astype(F32)
     gp1, acc1, g_in1, g_out1 = backward_core(1, g1, kept1)
-    half_out1 = grad_scatter(g_out1)
+    half_out1 = lax.psum_scatter(cross_sum(g_out1), "dp", scatter_dimension=0, tiled=True)
     half_in1 = grad_scatter(g_in1)
     gp1, g_in1 = lax.optimization_barrier((gp1, g_in1))
     du1, gain1 = backward_input(1, g1, kept1, gp1)
     gp0, acc0, g_in0, g_out0 = backward_core(0, du1.astype(F32), kept0)
-    split_out = g_out0.reshape(-1, 2, shard // 2, width)
-    mine = jnp.where(is_first, split_out[:, 0], split_out[:, 1])
-    theirs = swap_sections(jnp.where(is_first, split_out[:, 1], split_out[:, 0]))
-    out_mid = (mine.astype(F32) + theirs.astype(F32)).astype(BF).reshape(-1, width)
+    out_mid = cross_sum(g_out0)
     du1_first = lax.ppermute(du1, "section", [(0, 1)])
 
     def by_batch(first_value, second_value):

time: 733 us -> 740 us (level)
  waiting for transfers between devices: 34.9 us -> 45.7 us
  Pallas kernels: 517 us -> 509 us
    pallas_call x2, Pallas kernels: 85.4 us -> 63.3 us  [mixer_bwd(): pl.pallas_call(functools.partial(bwd_kernel, width, n_heads), grid=(n,),...]
    ppermute x3 -> x4, waiting for transfers between devices: 0.01 us -> 20 us  [swap_sections(): lax.ppermute(value, 'section', [(i, (i + 1) % count) for i in range(count)])]
    all_gather x2, waiting for transfers between devices: 28.9 us -> 20.8 us  [later_gather(): return (lax.all_gather(piece, ('dp', 'section'), axis=0, tiled=True), after)]
    pallas_call x1 -> x2, Pallas kernels: 129 us -> 133 us  [open_gather(): pl.pallas_call(functools.partial(open_kernel, n, pieces, xn is not None),...]
  transfers between devices with their start and end apart: 10 -> 11, of which waited for: 3 -> 3; matrix products, arithmetic and copies ran while one was open for 17% -> 17% of each run, Pallas kernels for 68% -> 63%
where the time goes in v4:
time: 740 us; the launch traced here: 731 us
  Pallas kernels  509 us (69%)
  matrix products  80.4 us (11%)
  waiting for transfers between devices  45.7 us (6%)
  local copies, waits for them, and re-layouts  41.3 us (6%)
  other arithmetic  30.2 us (4%)
  between operations  14.7 us (2%)
  starting transfers between devices  8.84 us (1%)
    pallas_call x1, Pallas kernels, finish(): pl.pallas_call(functools.partial(finish_kernel, n, bc_at, gain_rows), out...  139 us
    pallas_call x2, Pallas kernels, open_gather(): pl.pallas_call(functools.partial(open_kernel, n, pieces, xn is not None),...  133 us
    pallas_call x3, Pallas kernels, token_scatter(): pl.pallas_call(functools.partial(token_scatter_kernel, side is not None),...  73 us
    pallas_call x3, Pallas kernels, token_gather(): pl.pallas_call(functools.partial(token_gather_kernel, count), out_shape=[...  71 us
    pallas_call x2, Pallas kernels, mixer_bwd(): pl.pallas_call(functools.partial(bwd_kernel, width, n_heads), grid=(n,),...  63.3 us
    dot_general x4, matrix products, dot(): return jnp.dot(a, b, preferred_element_type=F32)  32.4 us
    dot_general x4, matrix products, dot_tn(): lax.dot_general(a, b, (((0,), (0,)), ((), ())), preferred_element_type=F32)  30.6 us
    pallas_call x2, Pallas kernels, mixer_fwd(): pl.pallas_call(functools.partial(fwd_kernel, width), grid=(n,), in_specs=...  30 us
  transfers between devices with their start and end apart: 11, of which 3 were waited for; matrix products, arithmetic and copies ran while one was open for 17% of the time, Pallas kernels for 63%

profile of v4, /device:TPU:9, one launch (start us, length us, event | category | flops | bytes accessed | tf_op | source)
XLA Modules:
  0.0 730.5 jit_solution(9638092016103172901)
XLA Ops:
  22.4 83.5 %weights_open.2 = (bf16[1536,1920]{1,0:T(8,128)(2,1)}, bf16[1024,1536]{1,0:T(8,128)(2,1)}) custom-call(bf16[384,1920]{1,0:T(8,128)(2,1)} %copy-done.19, bf16[256,1536]{1,0:T(8,128)(2,1)} %fusion.8.refs_1_), custom_call_target="tpu_custom_call" | custom-call | flops 62999998464 | bytes 135000000 | tf_op jit(solution)/shard_map/weights_open/pallas_call | solution.py:704
  113.8 4.8 collective-permute-done.2
  119.4 49.3 %weights_open.3 = bf16[1536,768]{1,0:T(8,128)(2,1)} custom-call(bf16[384,768]{1,0:T(8,128)(2,1)} %bitcast.150), custom_call_target="tpu_custom_call" | custom-call | flops 28000000000 | bytes 60000000 | tf_op jit(solution)/shard_map/weights_open/pallas_call | solution.py:704
  168.7 11.9 %fusion.47.pre_ref = f32[1024,1920]{1,0:T(8,128)} fusion(bf16[1024,1536]{1,0:T(8,128)(2,1)} %get-tuple-element.63, bf16[1536,1920]{1,0:T(8,128)(2,1)} %get-tuple-element.66.w_ref), kind=kOutput, calls=%fused_computation.132 | convolution fusion | flops 6039797760 | bytes 16908288 | tf_op jit(solution)/shard_map/dot_general | solution.py:22
  180.6 15.1 %mixer_fwd.2 = (bf16[1024,768]{1,0:T(8,128)(2,1)S(1)}, f32[64,128]{1,0:T(8,128)S(1)}, f32[8,128,768]{2,1,0:T(8,128)}, f32[1024,1024]{1,0:T(8,128)}, f32[1024,768...) custom-call(f32[1024,1920]{1,0:T(8,128)} %fusion.47.pre_ref, ...), custom_call_target="tpu_custom_call" | custom-call | flops 8400000000 | bytes 18000000 | tf_op jit(solution)/shard_map/mixer_fwd/pallas_call | solution.py:127
  198.6 26.5 %token_scatter.3 = (f32[256,1536]{1,0:T(8,128)S(1)}, f32[16,128]{1,0:T(8,128)S(1)}) custom-call(bf16[1024,1536]{1,0:T(8,128)(2,1)S(1)} %convolution_convert_fusion.4.refs_0_, f32[64,128]{1,0:T(8,128)S(1)} %get-tuple-element.70.refs_1_), custom_call_target="tpu_custom_call" | custom-call | flops 15399999488 | bytes 33000000 | tf_op jit(solution)/shard_map/token_scatter/pallas_call | solution.py:516
  228.4 22.9 %token_gather.3 = bf16[1024,1536]{1,0:T(8,128)(2,1)} custom-call(bf16[256,1536]{1,0:T(8,128)(2,1)} %fusion.16.refs_0_), custom_call_target="tpu_custom_call" | custom-call | flops 15399999488 | bytes 33000000 | tf_op jit(solution)/shard_map/token_gather/pallas_call | solution.py:402
  251.3 11.9 %fusion.48.pre_ref = f32[1024,1920]{1,0:T(8,128)} fusion(bf16[1024,1536]{1,0:T(8,128)(2,1)} %token_gather.3, bf16[1536,1920]{1,0:T(8,128)(2,1)} %all-gather.3.cloned.1.call-done), kind=kOutput, calls=%fused_computation.133 | convolution fusion | flops 6039797760 | bytes 16908288 | tf_op jit(solution)/shard_map/dot_general | solution.py:22
  263.2 14.9 %mixer_fwd.3 = (bf16[1024,768]{1,0:T(8,128)(2,1)S(1)}, f32[64,128]{1,0:T(8,128)S(1)}, f32[8,128,768]{2,1,0:T(8,128)}, f32[1024,1024]{1,0:T(8,128)}, f32[1024,768...) custom-call(f32[1024,1920]{1,0:T(8,128)} %fusion.48.pre_ref, ...), custom_call_target="tpu_custom_call" | custom-call | flops 8400000000 | bytes 18000000 | tf_op jit(solution)/shard_map/mixer_fwd/pallas_call | solution.py:127
  279.7 20.8 %all-gather.5.cloned.1.call-done = bf16[1536,768]{1,0:T(8,128)(2,1)} async-done(((bf16[192,768]{1,0:T(8,128)(2,1)}), bf16[1536,768]{1,0:T(8,128)(2,1)}) %all-gather.5.cloned.1.call-update) | async-done | bytes 2359312 | tf_op jit(solution)/shard_map/all_gather | solution.py:1081
  305.1 23.8 %token_scatter.4 = (f32[256,1536]{1,0:T(8,128)S(1)}, f32[16,128]{1,0:T(8,128)S(1)}) custom-call(bf16[1024,1536]{1,0:T(8,128)(2,1)S(1)} %convolution_convert_fusion.3.refs_0_, f32[64,128]{1,0:T(8,128)S(1)} %get-tuple-element.76.refs_1_), custom_call_target="tpu_custom_call" | custom-call | flops 15399999488 | bytes 33000000 | tf_op jit(solution)/shard_map/token_scatter/pallas_call | solution.py:516
  332.1 24.0 %token_gather.4 = (bf16[1024,1536]{1,0:T(8,128)(2,1)}, bf16[1024,128]{1,0:T(8,128)(2,1)}) custom-call(bf16[256,1536]{1,0:T(8,128)(2,1)} %get-tuple-element.167.refs_0_, bf16[256,128]{1,0:T(8,128)(2,1)} %pad.41.refs_1_), custom_call_target="tpu_custom_call" | custom-call | flops 15399999488 | bytes 33000000 | tf_op jit(solution)/shard_map/token_gather/pallas_call | solution.py:402
  356.1 4.6 convolution_convert_fusion.5
  368.3 20.0 %collective-permute-done.5 = bf16[4,192,768]{2,1,0:T(8,128)(2,1)S(1)} collective-permute-done((bf16[4,192,768]{2,1,0:T(8,128)(2,1)S(1)}, bf16[4,192,768]{2,1,0:T(8,128)(2,1)S(1)}, u32[]{:S(2)}, u32[]{:S(2)}) %collective-permute-start.5) | collective-permute-done | bytes 1179680 | tf_op jit(solution)/shard_map/ppermute | solution.py:1073
  390.3 31.6 %mixer_bwd.2 = (bf16[1024,1920]{1,0:T(8,128)(2,1)}, f32[8,1024]{1,0:T(8,128)}) custom-call(f32[1024,1920]{1,0:T(8,128)} %fusion.48.pre_ref, f32[16,1024]{1,0:T(8,128)} %copy-done.3, bf16[6,640,128]{2,1,0:T(8,128)(2,1)} %fusion.3.pick_ref, f32[8,128,768]{2,1,0:T(8,128)} %get-tuple-element.87.st_ref, f32[1024,1024]{1,0:T(8,128)} %get-tuple-element.88.conv_ref, ...), custom_call_target="tpu_custom_call" | custom-call | flops 24500000768 | bytes 52500000 | tf_op jit(solution)/shard_map/mixer_bwd/pallas_call | solution.py:305
  421.9 10.6 %convolution_convert_fusion.1 = bf16[1536,1920]{1,0:T(8,128)(2,1)} fusion(bf16[1024,1536]{1,0:T(8,128)(2,1)S(1)} %copy-done.40, bf16[1024,1920]{1,0:T(8,128)(2,1)} %get-tuple-element.98), kind=kOutput, calls=%fused_computation.1 | convolution fusion | flops 6042746880 | bytes 12976128 | tf_op jit(solution)/shard_map/dot_general | solution.py:30
  432.5 9.9 %convolution_convert_fusion.2.refs_0_ = bf16[1024,1536]{1,0:T(8,128)(2,1)S(1)} fusion(bf16[1024,1920]{1,0:T(8,128)(2,1)} %get-tuple-element.98, bf16[1536,1920]{1,0:T(8,128)(2,1)} %all-gather.3.cloned.1.call-done), kind=kOutput, calls=%fused_computation.2 | convolution fusion | flops 6041370624 | bytes 12976128 | tf_op jit(solution)/shard_map/dot_general | solution.py:26
  442.5 22.7 %token_scatter.5 = f32[256,1536]{1,0:T(8,128)S(1)} custom-call(bf16[1024,1536]{1,0:T(8,128)(2,1)S(1)} %convolution_convert_fusion.2.refs_0_), custom_call_target="tpu_custom_call" | custom-call | flops 15399999488 | bytes 33000000 | tf_op jit(solution)/shard_map/token_scatter/pallas_call | solution.py:516
  474.5 24.1 %token_gather.5 = (bf16[1024,1536]{1,0:T(8,128)(2,1)}, bf16[1024,128]{1,0:T(8,128)(2,1)}) custom-call(bf16[256,1536]{1,0:T(8,128)(2,1)} %fusion.4.refs_0_, bf16[256,128]{1,0:T(8,128)(2,1)} %pad.42.refs_1_), custom_call_target="tpu_custom_call" | custom-call | flops 15399999488 | bytes 33000000 | tf_op jit(solution)/shard_map/token_gather/pallas_call | solution.py:402
  498.5 4.8 convolution_convert_fusion.6
  510.8 31.8 %mixer_bwd.3 = (bf16[1024,1920]{1,0:T(8,128)(2,1)}, f32[8,1024]{1,0:T(8,128)}) custom-call(f32[1024,1920]{1,0:T(8,128)} %fusion.47.pre_ref, f32[16,1024]{1,0:T(8,128)} %copy-done.2, bf16[6,640,128]{2,1,0:T(8,128)(2,1)} %fusion.3.pick_ref, f32[8,128,768]{2,1,0:T(8,128)} %get-tuple-element.79.st_ref, f32[1024,1024]{1,0:T(8,128)} %get-tuple-element.80.conv_ref, ...), custom_call_target="tpu_custom_call" | custom-call | flops 24500000768 | bytes 52500000 | tf_op jit(solution)/shard_map/mixer_bwd/pallas_call | solution.py:305
  542.6 10.6 %convolution_convert_fusion.g_ref = bf16[1536,1920]{1,0:T(8,128)(2,1)} fusion(bf16[1024,1536]{1,0:T(8,128)(2,1)S(1)} %copy-done.39, bf16[1024,1920]{1,0:T(8,128)(2,1)} %get-tuple-element.101.gp_ref), kind=kOutput, calls=%fused_computation | convolution fusion | flops 6042746880 | bytes 12976128 | tf_op jit(solution)/shard_map/dot_general | solution.py:30
  555.1 5.5 concatenate.27.small_ref
  566.1 139.3 %grad_finish.1 = (f32[384,1920]{1,0:T(8,128)}, f32[384,768]{1,0:T(8,128)}, f32[16,1024]{1,0:T(8,128)}, f32[16,1024]{1,0:T(8,128)}, f32[384,256]{1,0:T(8,128)}, /...) custom-call(bf16[1536,1920]{1,0:T(8,128)(2,1)} %convolution_convert_fusion.g_ref, bf16[768,768]{1,0:T(8,128)(2,1)} %bitcast.151, ...), custom_call_target="tpu_custom_call" | custom-call | flops 83999997952 | bytes 180000000 | tf_op jit(solution)/shard_map/grad_finish/pallas_call | solution.py:1036
  (199 shorter events, 91.0 us)
Async XLA Ops:
  7.2 244.1 %all-gather.3.cloned.1.call-start = ((), (), s32[]{:S(2)}) async-start(), calls=%async_computation.2 | async-start | bytes 6635520 | tf_op jit(solution)/shard_map/all_gather | solution.py:1081
  13.1 7.4 %collective-permute-start = (f32[16,1024]{1,0:T(8,128)S(1)}, f32[16,1024]{1,0:T(8,128)S(1)}, u32[]{:S(2)}, u32[]{:S(2)}) collective-permute-start(f32[16,1024]{1,0:T(8,128)S(1)} %concatenate.24), channel_id=1, source_target_pairs={{0,16},{16,0},{1,17},{17,1},{2,18},{18,2},{3,19},{19,3},{4,20},{20... | collective-permute-start | bytes 196616 | tf_op jit(solution)/shard_map/ppermute | solution.py:1073
  17.7 88.2 %collective-permute-start.1 = (bf16[192,1920]{1,0:T(8,128)(2,1)}, bf16[192,1920]{1,0:T(8,128)(2,1)S(1)}, u32[]{:S(2)}, u32[]{:S(2)}) collective-permute-start(bf16[192,1920]{1,0:T(8,128)(2,1)} %slice.110), channel_id=1, source_target_pairs={{16,0},{17,1},{18,2},{19,3},{20,4},{21,5},{22,6},{23,7},{24,8},{25... | collective-permute-start | bytes 2211848 | tf_op jit(solution)/shard_map/ppermute | solution.py:1079
  20.4 205.4 %copy-start.18 = (bf16[256,1536]{1,0:T(8,128)(2,1)}, bf16[256,1536]{1,0:T(8,128)(2,1)S(1)}, u32[]{:S(2)}) copy-start(bf16[256,1536]{1,0:T(8,128)(2,1)S(1)} %get-tuple-element.163.u_ref) | copy-start | bytes 2359300
  20.5 160.1 %copy-start.2 = (f32[16,1024]{1,0:T(8,128)}, f32[16,1024]{1,0:T(8,128)S(1)}, u32[]{:S(2)}) copy-start(f32[16,1024]{1,0:T(8,128)S(1)} %get-tuple-element.169.par_ref) | copy-start | bytes 196612
  22.4 83.5 %copy-start.20 = (bf16[384,1920]{1,0:T(8,128)(2,1)S(1)}, bf16[384,1920]{1,0:T(8,128)(2,1)}, u32[]{:S(2)}) copy-start(bf16[384,1920]{1,0:T(8,128)(2,1)} %copy-done.19) | copy-start | bytes 4423684
  106.9 193.6 %all-gather.5.cloned.1.call-start = ((), (), s32[]{:S(2)}) async-start(), calls=%async_computation.3 | async-start | bytes 2654208 | tf_op jit(solution)/shard_map/all_gather | solution.py:1081
  108.3 10.3 %collective-permute-start.2 = (bf16[192,768]{1,0:T(8,128)(2,1)S(1)}, bf16[192,768]{1,0:T(8,128)(2,1)S(1)}, u32[]{:S(2)}, u32[]{:S(2)}) collective-permute-start(bf16[192,768]{1,0:T(8,128)(2,1)S(1)} %slice.112), channel_id=1, source_target_pairs={{16,0},{17,1},{18,2},{19,3},{20,4},{21,5},{22,6},{23,7},{24,8},{25... | collective-permute-start | bytes 884744 | tf_op jit(solution)/shard_map/ppermute | solution.py:1079
  180.6 15.1 %copy-start.37 = (bf16[1536,768]{1,0:T(8,128)(2,1)S(1)}, bf16[1536,768]{1,0:T(8,128)(2,1)}, u32[]{:S(2)}) copy-start(bf16[1536,768]{1,0:T(8,128)(2,1)} %weights_open.3) | copy-start | bytes 7077892
  227.0 339.1 %reduce-scatter.5.cloned.1.call-start = ((), (), s32[]{:S(2)}) async-start(), calls=%async_computation.5 | async-start | bytes 1474560 | tf_op jit(solution)/shard_map/reduce_scatter | solution.py:1193
  279.7 25.4 %copy-start.7 = (bf16[1024,768]{1,0:T(8,128)(2,1)}, bf16[1024,768]{1,0:T(8,128)(2,1)S(1)}, u32[]{:S(2)}) copy-start(bf16[1024,768]{1,0:T(8,128)(2,1)S(1)} %get-tuple-element.74) | copy-start | bytes 4718596
  328.9 32.5 %copy-start.29 = (f32[256]{0:T(256)}, f32[256]{0:T(256)S(1)}, u32[]{:S(2)}) copy-start(f32[256]{0:T(256)S(1)} %get-tuple-element.184) | copy-start | bytes 3076
  332.1 24.1 %copy-start.8 = (bf16[1024,768]{1,0:T(8,128)(2,1)S(1)}, bf16[1024,768]{1,0:T(8,128)(2,1)}, u32[]{:S(2)}) copy-start(bf16[1024,768]{1,0:T(8,128)(2,1)} %copy-done.7) | copy-start | bytes 4718596
  360.9 27.4 %collective-permute-start.5 = (bf16[4,192,768]{2,1,0:T(8,128)(2,1)S(1)}, bf16[4,192,768]{2,1,0:T(8,128)(2,1)S(1)}, u32[]{:S(2)}, u32[]{:S(2)}) collective-permute-start(bf16[4,192,768]{2,1,0:T(8,128)(2,1)S(1)} %select_bitcast_fusion), channel_id=1, source_target_pairs={{0,16},{16,0},{1,17},{17,1},{2,18},{18,2},{3,19},{19,3},{4,20},{20... | collective-permute-start | bytes 3538952 | tf_op jit(solution)/shard_map/ppermute | solution.py:1073
  363.1 197.6 %collective-permute-start.3 = (bf16[256,1536]{1,0:T(8,128)(2,1)}, bf16[256,1536]{1,0:T(8,128)(2,1)}, u32[]{:S(2)}, u32[]{:S(2)}) collective-permute-start(bf16[256,1536]{1,0:T(8,128)(2,1)} %broadcast_select_fusion), channel_id=1, source_target_pairs={{0,16},{16,0},{1,17},{17,1},{2,18},{18,2},{3,19},{19,3},{4,20},{20... | collective-permute-start | bytes 2359304 | tf_op jit(solution)/shard_map/ppermute | solution.py:1073
  389.8 176.3 %reduce-scatter.3.cloned.1.call-start = ((), (), s32[]{:S(2)}) async-start(), calls=%async_computation.4 | async-start | bytes 6635520 | tf_op jit(solution)/shard_map/reduce_scatter | solution.py:1085
  390.3 31.6 %copy-start.40 = (bf16[1024,1536]{1,0:T(8,128)(2,1)S(1)}, bf16[1024,1536]{1,0:T(8,128)(2,1)}, u32[]{:S(2)}) copy-start(bf16[1024,1536]{1,0:T(8,128)(2,1)} %token_gather.3) | copy-start | bytes 9437188
  442.5 23.3 %copy-start.22 = (bf16[2,1,256,1536]{3,2,1,0:T(8,128)(2,1)S(1)}, bf16[2,1,256,1536]{3,2,1,0:T(8,128)(2,1)}, u32[]{:S(2)}) copy-start(bf16[2,1,256,1536]{3,2,1,0:T(8,128)(2,1)} %param.16) | copy-start | bytes 4718596
  469.1 252.6 %collective-permute-start.6 = (bf16[256,1536]{1,0:T(8,128)(2,1)}, bf16[256,1536]{1,0:T(8,128)(2,1)}, u32[]{:S(2)}, u32[]{:S(2)}) collective-permute-start(bf16[256,1536]{1,0:T(8,128)(2,1)} %get-tuple-element.159.seed_ref), channel_id=1, source_target_pairs={{0,16},{1,17},{2,18},{3,19},{4,20},{5,21},{6,22},{7,23},{8,24},{9,... | collective-permute-start | bytes 2359304 | tf_op jit(solution)/shard_map/ppermute | solution.py:1199
  474.5 24.1 %copy-start.6 = (bf16[1024,768]{1,0:T(8,128)(2,1)S(1)}, bf16[1024,768]{1,0:T(8,128)(2,1)}, u32[]{:S(2)}) copy-start(bf16[1024,768]{1,0:T(8,128)(2,1)} %copy-done.5) | copy-start | bytes 4718596
  505.2 58.5 %collective-permute-start.4 = (bf16[4,192,768]{2,1,0:T(8,128)(2,1)}, bf16[4,192,768]{2,1,0:T(8,128)(2,1)S(1)}, u32[]{:S(2)}, u32[]{:S(2)}) collective-permute-start(bf16[4,192,768]{2,1,0:T(8,128)(2,1)} %select_bitcast_fusion.1), channel_id=1, source_target_pairs={{0,16},{16,0},{1,17},{17,1},{2,18},{18,2},{3,19},{19,3},{4,20},{20... | collective-permute-start | bytes 3538952 | tf_op jit(solution)/shard_map/ppermute | solution.py:1073
  510.8 31.8 %copy-start.39 = (bf16[1024,1536]{1,0:T(8,128)(2,1)S(1)}, bf16[1024,1536]{1,0:T(8,128)(2,1)}, u32[]{:S(2)}) copy-start(bf16[1024,1536]{1,0:T(8,128)(2,1)} %get-tuple-element.63) | copy-start | bytes 9437188
  542.6 12.6 %copy-start.28 = (f32[2,1024]{1,0:T(2,128)S(1)}, f32[2,1024]{1,0:T(2,128)}, u32[]{:S(2)}) copy-start(f32[2,1024]{1,0:T(2,128)} %reshape.447) | copy-start | bytes 24580
  542.6 18.1 %copy-start.15 = (bf16[256,1536]{1,0:T(8,128)(2,1)S(1)}, bf16[256,1536]{1,0:T(8,128)(2,1)}, u32[]{:S(2)}) copy-start(bf16[256,1536]{1,0:T(8,128)(2,1)} %copy-done.13) | copy-start | bytes 2359300
  (28 other events, 86.0 us)
Sparse Core Ops, SparseCore 0:
  107.0 113.7 all-gather.2
  227.1 73.3 all-gather.4
  389.9 29.2 reduce-scatter.4
  432.6 124.0 reduce-scatter.2
